TPU v7x, 768 devices: a whole 4x8x12 slice. The times are simulated.
768 devices in a mesh: dp: 384 (over x, y, z), mp: 2 (over core).
Axes of the slice: x: 4, y: 8, z: 12, core: 2. Of those that a mesh axis runs over, the one named last changes fastest.
Arguments:
- attn: bfloat16 [147456, 1536], P('dp', 'mp'), may hold values from -6 to 6
- w_out: bfloat16 [1536, 1536], P('mp'), may hold values from -0.15625 to 0.15625
- resid: bfloat16 [147456, 1536], P('dp', 'mp'), may hold values from -6 to 6
- target: bfloat16 [147456, 1536], P('dp', 'mp'), may hold values from -6 to 6
- gate: float32 [1152, 1536], P('dp', 'mp'), may hold values from -5 to 5
- bins: int32 [1152], P('dp'), may hold values from 0 to 127
Outputs:
- grad_w_out: float32 [1536, 1536], P('dp', 'mp')
- grad_gate: float32 [1152, 1536], P('dp', 'mp')
- bin_loss: float32 [128], replicated
All inputs are finite; a program needn't handle non-finite values.
Results may differ from a plain program's by a relative error of at most 0.0008.
Values may be sent and summed in bfloat16 or wider, within the bound.
No kernel may reach another device: no remote copies, remote signals or barrier semaphores. Data moves between devices by JAX's collectives and lax.ppermute only.
A program may use at most 32 MiB of HBM per device.

v0:
```python
import math

import jax
import jax.numpy as jnp
from jax import lax
from jax.sharding import Mesh
from jax.sharding import PartitionSpec as P

NBINS = 128
DP_MP = ("dp_0", "dp_1", "dp_2", "mp")
DP = ("dp_0", "dp_1", "dp_2")


LOSS_SCALE = 4096.0


def from_everyone(x, axis):
    size = lax.axis_size(axis)
    return lax.all_to_all(jnp.broadcast_to(x[None], (size, *x.shape)), axis, 0, 0, tiled=True)


def laid_out(blocks, dim):
    shape = list(blocks.shape[1:])
    shape[dim] *= blocks.shape[0]
    return jnp.moveaxis(blocks, 0, dim).reshape(shape)


def collect(x, axis, dim):
    blocks = from_everyone(x, axis)
    return laid_out(blocks, dim)


def over_axes(x, axes):
    for axis in axes:
        x = lax.psum(x, axis)
    return x


def summed_rows(x, axes, dim):
    for axis in axes:
        x = lax.psum_scatter(x, axis, scatter_dimension=dim, tiled=True)
    return x


def bin_weights():
    centre = (jnp.arange(NBINS).astype(jnp.float32) + 0.5) / NBINS
    logit = jnp.log(centre) - jnp.log(1.0 - centre)
    return jnp.exp(-0.5 * logit * logit) / (math.sqrt(2.0 * math.pi) * centre * (1.0 - centre))


def shards(attn, w_out, resid, target, gate, bins):
    samples = bins.shape[0]
    tok_rows = attn.shape[0]
    per_sample = tok_rows // samples
    full_width = w_out.shape[1]
    own_cols = resid.shape[1]
    bin_ids = jnp.arange(NBINS, dtype=jnp.int32)
    one_hot = (bins[:, None] == bin_ids[None, :]).astype(jnp.float32)
    local_counts = jnp.sum(one_hot, axis=0)
    weights = bin_weights()
    w_cols = lax.all_to_all(w_out, "mp", split_axis=1, concat_axis=0, tiled=True)
    whole_attn = collect(attn, "mp", 1)
    projected = jnp.dot(whole_attn, w_cols, preferred_element_type=jnp.float32)
    proj_cube = projected.reshape(samples, per_sample, own_cols)
    hidden = (
        resid.reshape(samples, per_sample, own_cols).astype(jnp.float32)
        + gate[:, None, :] * proj_cube
    )
    error_cube = hidden - target.reshape(samples, per_sample, own_cols).astype(jnp.float32)
    sample_error = jnp.sum(error_cube * error_cube, axis=(1, 2)) / (per_sample * full_width)
    bin_part = jnp.sum(one_hot * sample_error[:, None], axis=0)
    sums, counts = (
        over_axes(bin_part, DP_MP),
        over_axes(local_counts / lax.axis_size("mp"), DP_MP),
    )
    floored = jnp.maximum(counts, 1.0)
    scale_bin = LOSS_SCALE * weights / floored
    coefficient = jnp.sum(one_hot * scale_bin[None, :], axis=1) * (2.0 / (per_sample * full_width))
    d_hidden = coefficient[:, None, None] * error_cube
    grad_gate = jnp.sum(d_hidden * proj_cube, axis=1)
    d_proj = (d_hidden * gate[:, None, :]).astype(jnp.bfloat16).reshape(tok_rows, own_cols)
    full_grad = lax.dot_general(
        whole_attn, d_proj, (((0,), (0,)), ((), ())), preferred_element_type=jnp.float32
    )
    grad_out = summed_rows(full_grad, DP, 0)
    bin_loss = weights * sums / floored
    return (grad_out, grad_gate, bin_loss)


def solution(mesh):
    finer = Mesh(mesh.devices.reshape(4, 8, 12, mesh.shape["mp"]), ("dp_0", "dp_1", "dp_2", "mp"))
    placed = (P(DP, "mp"), P("mp", None), P(DP, "mp"), P(DP, "mp"), P(DP, "mp"), P(DP))
    return jax.shard_map(
        shards,
        mesh=finer,
        in_specs=placed,
        out_specs=(P(DP, "mp"), P(DP, "mp"), P()),
        check_vma=False,
    )
```

profile of v0, /device:TPU:2, one launch (start us, length us, event | category | flops | bytes accessed | tf_op | source)
XLA Modules:
  0.0 318.5 jit_solution(10924526723229674776)
XLA Ops:
  7.2 2.2 broadcast_in_dim.2
  9.3 3.7 %all-to-all-start = ((bf16[2,384,768]{2,1,0:T(8,128)(2,1)}), bf16[2,384,768]{2,1,0:T(8,128)(2,1)S(1)}, u32[]{:S(2)}, u32[]{:S(2)}) async-start(bf16[2,384,768]{2,1,0:T(8,128)(2,1)} %broadcast_in_dim.2), calls=%async_computation | async-start | bytes 2359296 | tf_op jit(solution)/shard_map/all_to_all | solution.py:19
  13.1 1.6 copy.29
  14.6 0.6 all-to-all-done
  15.3 4.9 %all-to-all-start.1 = ((bf16[768,2,768]{2,0,1:T(8,128)(2,1)}), bf16[768,2,768]{2,0,1:T(8,128)(2,1)}, u32[]{:S(2)}, u32[]{:S(2)}) async-start(bf16[768,2,768]{2,0,1:T(8,128)(2,1)} %bitcast.27), calls=%async_computation.1 | async-start | bytes 4718592 | tf_op jit(solution)/shard_map/all_to_all | solution.py:61
  20.2 0.0 reduce-scatter.6.cloned.1.call-start
  20.2 1.2 copy.19
  21.5 0.8 dot_general.10
  22.3 0.1 convert_reduce_fusion
  22.4 17.2 %psum.56 = f32[128]{0:T(128)S(1)} all-reduce(f32[128]{0:T(128)S(1)} %broadcast_multiply_fusion.2), channel_id=1, replica_groups=mesh['dp_0'=4,'dp_1'=8,'dp_2'=12,'mp'=2] {'dp_0'}, use_global_device_ids=true, to_apply=%region_1.0 | all-reduce | flops 128 | bytes 1024 | tf_op jit(solution)/shard_map/psum | solution.py:35
  39.6 14.1 %psum.57 = f32[128]{0:T(128)S(1)} all-reduce(f32[128]{0:T(128)S(1)} %psum.56), channel_id=1, replica_groups=mesh['dp_0'=4,'dp_1'=8,'dp_2'=12,'mp'=2] {'dp_1'}, use_global_device_ids=true, to_apply=%region_2.0 | all-reduce | flops 128 | bytes 1024 | tf_op jit(solution)/shard_map/psum | solution.py:35
  53.8 28.1 %psum.58 = f32[128]{0:T(128)S(1)} all-reduce(f32[128]{0:T(128)S(1)} %psum.57), channel_id=1, replica_groups=mesh['dp_0'=4,'dp_1'=8,'dp_2'=12,'mp'=2] {'dp_2'}, use_global_device_ids=true, to_apply=%region_3.0 | all-reduce | flops 128 | bytes 1024 | tf_op jit(solution)/shard_map/psum | solution.py:35
  81.9 2.5 psum.59
  84.3 0.2 select_reduce_fusion.1
  84.6 4.0 %multiply_reduce_fusion = (f32[3]{0:T(128)S(1)}, f32[3,768]{1,0:T(4,128)}, bf16[3,128,768]{2,1,0:T(8,128)(2,1)S(1)}) fusion(bf16[3,128,768]{2,1,0:T(8,128)(2,1)} %bitcast.32, f32[3,768]{1,0:T(4,128)S(1)} %copy-done.1, bf16[3,128,768]{2,1,0:T(8,128)(2,1)} %bitcast.33, f32[3]{0:T(128)S(1)} %broadcast_multiply_fusion.1, ...), kind=kOutput, calls=%fused_computation.4 | convolution fusion | flops 909506304 | bytes 5326872 | tf_op jit(solution)/shard_map/dot_general | solution.py:63
  88.5 0.7 copy.18
  89.2 3.6 %convolution_bitcast_fusion = f32[1536,768]{0,1:T(8,128)} fusion(bf16[384,768]{1,0:T(8,128)(2,1)S(1)} %bitcast.31, bf16[384,1536]{0,1:T(8,128)(2,1)S(1)} %bitcast.29), kind=kOutput, calls=%fused_computation | convolution fusion | flops 905969664 | bytes 6488064 | tf_op jit(solution)/shard_map/dot_general | solution.py:82
  92.8 0.0 reduce-scatter.8.cloned.1.call-start
  92.9 49.6 %reduce-scatter.6.cloned.1.call-done = f32[384,768]{0,1:T(8,128)} async-done(((f32[1536,768]{0,1:T(8,128)}), f32[384,768]{0,1:T(8,128)}) %reduce-scatter.6.cloned.1.call-update) | async-done | bytes 1179664 | tf_op jit(solution)/shard_map/reduce_scatter | solution.py:41
  142.5 2.6 copy.23
  145.1 0.0 all-reduce.3.cloned.1.call-start
  145.2 1.3 dynamic-slice
  147.1 0.1 select_reduce_fusion
  147.2 9.5 %psum.60 = f32[128]{0:T(128)S(1)} all-reduce(f32[128]{0:T(128)S(1)} %select_reduce_fusion), channel_id=1, replica_groups=mesh['dp_0'=4,'dp_1'=8,'dp_2'=12,'mp'=2] {'dp_0'}, use_global_device_ids=true, to_apply=%region_12.0 | all-reduce | flops 128 | bytes 1024 | tf_op jit(solution)/shard_map/psum | solution.py:35
  156.7 17.0 %psum.61 = f32[128]{0:T(128)S(1)} all-reduce(f32[128]{0:T(128)S(1)} %psum.60), channel_id=1, replica_groups=mesh['dp_0'=4,'dp_1'=8,'dp_2'=12,'mp'=2] {'dp_1'}, use_global_device_ids=true, to_apply=%region_13.0 | all-reduce | flops 128 | bytes 1024 | tf_op jit(solution)/shard_map/psum | solution.py:35
  173.7 25.3 %psum.62 = f32[128]{0:T(128)S(1)} all-reduce(f32[128]{0:T(128)S(1)} %psum.61), channel_id=1, replica_groups=mesh['dp_0'=4,'dp_1'=8,'dp_2'=12,'mp'=2] {'dp_2'}, use_global_device_ids=true, to_apply=%region_14.0 | all-reduce | flops 128 | bytes 1024 | tf_op jit(solution)/shard_map/psum | solution.py:35
  198.9 2.5 psum.63
  201.4 1.8 copy.24
  203.2 0.5 multiply_divide_fusion
  203.8 106.3 %all-reduce.3.cloned.1.call-done = f32[48,768]{0,1:T(8,128)} async-done(((f32[48,768]{0,1:T(8,128)}), f32[48,768]{0,1:T(8,128)}) %all-reduce.3.cloned.1.call-update) | async-done | bytes 147472
  310.0 1.2 constant_dynamic-slice_fusion
  311.2 0.8 copy.21
  (15 shorter events, 0.1 us)
Async XLA Ops:
  9.3 3.7 %copy-start = (bf16[768,1536]{1,0:T(8,128)(2,1)S(1)}, bf16[768,1536]{1,0:T(8,128)(2,1)}, u32[]{:S(2)}) copy-start(bf16[768,1536]{1,0:T(8,128)(2,1)} %param.7) | copy-start | bytes 7077892
  9.3 5.9 %all-to-all-start = ((bf16[2,384,768]{2,1,0:T(8,128)(2,1)}), bf16[2,384,768]{2,1,0:T(8,128)(2,1)S(1)}, u32[]{:S(2)}, u32[]{:S(2)}) async-start(bf16[2,384,768]{2,1,0:T(8,128)(2,1)} %broadcast_in_dim.2), calls=%async_computation | async-start | bytes 2359296 | tf_op jit(solution)/shard_map/all_to_all | solution.py:19
  15.3 69.3 %all-to-all-start.1 = ((bf16[768,2,768]{2,0,1:T(8,128)(2,1)}), bf16[768,2,768]{2,0,1:T(8,128)(2,1)}, u32[]{:S(2)}, u32[]{:S(2)}) async-start(bf16[768,2,768]{2,0,1:T(8,128)(2,1)} %bitcast.27), calls=%async_computation.1 | async-start | bytes 4718592 | tf_op jit(solution)/shard_map/all_to_all | solution.py:61
  20.2 122.3 %reduce-scatter.6.cloned.1.call-start = ((), (), s32[]{:S(2)}) async-start(), calls=%async_computation.4 | async-start | bytes 5898240 | tf_op jit(solution)/shard_map/reduce_scatter | solution.py:41
  21.4 0.8 copy-start.2
  21.5 63.1 %copy-start.1 = (f32[3,768]{1,0:T(4,128)S(1)}, f32[3,768]{1,0:T(4,128)}, u32[]{:S(2)}) copy-start(f32[3,768]{1,0:T(4,128)} %param.10) | copy-start | bytes 27652
  92.8 108.6 %reduce-scatter.8.cloned.1.call-start = ((), (), s32[]{:S(2)}) async-start(), calls=%async_computation.5 | async-start | bytes 1327104
  145.1 164.9 %all-reduce.3.cloned.1.call-start = ((), (), s32[]{:S(2)}) async-start(), calls=%async_computation.6 | async-start | bytes 786432
Sparse Core Ops, SparseCore 0:
  93.0 49.4 reduce-scatter.5
  145.6 45.5 reduce-scatter.7
  203.4 106.6 all-reduce.2
where the time goes:
time: 319 us; the launch traced here: 318 us
  waiting for transfers between devices  157 us (49%)
  blocking collectives  116 us (36%)
  between operations  14.5 us (5%)
  local copies, waits for them, and re-layouts  14.1 us (4%)
  starting transfers between devices  8.76 us (3%)
  matrix products  7.52 us (2%)
    psum x8, blocking collectives, over_axes(): x = lax.psum(x, axis)  116 us
    unnamed x5, waiting for transfers between devices  106 us
    reduce_scatter x1, waiting for transfers between devices, summed_rows(): x = lax.psum_scatter(x, axis, scatter_dimension=dim, tiled=True)  49.6 us
    unnamed x11, local copies, waits for them, and re-layouts  7.67 us
  transfers between devices with their start and end apart: 5, of which 3 were waited for; matrix products, arithmetic and copies ran while one was open for 2% of the time, Pallas kernels for 0%

commit v1 on v0

v1 whole, which is shorter than its diff:
```python
import math

import jax
import jax.numpy as jnp
from jax import lax
from jax.sharding import Mesh
from jax.sharding import PartitionSpec as P

NBINS = 128
DP = ("dp_0", "dp_1", "dp_2")
LOSS_SCALE = 4096.0
ATTN_BOUND = 6.0
TOP = 14.0
EXTRA = 8


def bin_weights():
    centre = (jnp.arange(NBINS).astype(jnp.float32) + 0.5) / NBINS
    logit = jnp.log(centre) - jnp.log(1.0 - centre)
    return jnp.exp(-0.5 * logit * logit) / (math.sqrt(2.0 * math.pi) * centre * (1.0 - centre))


def partner(x):
    return lax.ppermute(x, "mp", [(0, 1), (1, 0)])


def summed_everywhere(x, axes):
    size = math.prod(lax.axis_size(a) for a in ([axes] if isinstance(axes, str) else axes))
    spread = jnp.broadcast_to(x[None], (size, *x.shape))
    return jnp.sum(lax.all_to_all(spread, axes, 0, 0, tiled=True), axis=0)


def exponent_of(bound):
    return jnp.floor(jnp.log2(jnp.maximum(bound, 1e-30))) + 2.0


def side_rows(losses, bound_exp, cols):
    loss_exp = exponent_of(jnp.max(losses))
    scaled = losses * jnp.exp2(TOP - loss_exp)
    high = scaled.astype(jnp.float16)
    low = ((scaled - high.astype(jnp.float32)) * 1024.0).astype(jnp.float16)
    exps = jnp.concatenate(
        [jnp.broadcast_to(bound_exp, (NBINS,)), jnp.broadcast_to(loss_exp, (NBINS,))]
    ).astype(jnp.float16)
    row = jnp.concatenate([high, low, exps])
    return jnp.pad(row[None, :], ((0, EXTRA - 1), (0, cols - 4 * NBINS)))


def packed(total, losses, bound, size):
    rows, cols = total.shape
    bound_exp = exponent_of(bound)
    body = (total * jnp.exp2(TOP - bound_exp)).astype(jnp.float16).reshape(size, rows // size, cols)
    side = side_rows(losses, bound_exp, cols)
    fill = -(rows // size) % EXTRA
    body = jnp.pad(body, ((0, 0), (0, fill), (0, 0)))
    return jnp.concatenate([body, jnp.broadcast_to(side[None], (size, *side.shape))], axis=1)


def unpacked(got, rows):
    side = got[:, -EXTRA, :].astype(jnp.float32)
    bound_exp = side[:, 2 * NBINS]
    loss_exp = side[:, 3 * NBINS]
    scale = jnp.exp2(bound_exp - TOP)
    losses = jnp.sum(
        (side[:, :NBINS] + side[:, NBINS : 2 * NBINS] * (1.0 / 1024.0)) * jnp.exp2(loss_exp - TOP)[:, None],
        axis=0,
    )
    total = jnp.sum(got[:, :rows, :].astype(jnp.float32) * scale[:, None, None], axis=0)
    return total, losses, jnp.sum(jnp.exp2(bound_exp))


def shards(attn, w_out, resid, target, gate, bins):
    samples = bins.shape[0]
    tok_rows, half = attn.shape
    per_sample = tok_rows // samples
    full_width = w_out.shape[1]
    own_cols = resid.shape[1]
    bin_ids = jnp.arange(NBINS, dtype=jnp.int32)
    one_hot = (bins[:, None] == bin_ids[None, :]).astype(jnp.float32)
    weights = bin_weights()
    me = lax.axis_index("mp")

    w_mine = lax.dynamic_slice_in_dim(w_out, me * own_cols, own_cols, axis=1)
    w_theirs = lax.dynamic_slice_in_dim(w_out, (1 - me) * own_cols, own_cols, axis=1)
    attn_other = partner(attn)
    w_other = partner(w_theirs)

    counts = summed_everywhere(jnp.sum(one_hot, axis=0)[None], DP[:2])
    counts = summed_everywhere(counts, DP[2])[0]
    floored = jnp.maximum(counts, 1.0)

    first = me == 0
    whole_attn = jnp.concatenate(
        [jnp.where(first, attn, attn_other), jnp.where(first, attn_other, attn)], axis=1
    )
    w_cols = jnp.concatenate(
        [jnp.where(first, w_mine, w_other), jnp.where(first, w_other, w_mine)], axis=0
    )
    projected = jnp.dot(whole_attn, w_cols, preferred_element_type=jnp.float32)
    proj_cube = projected.reshape(samples, per_sample, own_cols)
    hidden = (
        resid.reshape(samples, per_sample, own_cols).astype(jnp.float32)
        + gate[:, None, :] * proj_cube
    )
    error_cube = hidden - target.reshape(samples, per_sample, own_cols).astype(jnp.float32)
    sample_error = jnp.sum(error_cube * error_cube, axis=(1, 2)) / (per_sample * full_width)
    error_proj = jnp.sum(error_cube * proj_cube, axis=1)
    losses = jnp.sum(one_hot * sample_error[:, None], axis=0)
    losses = losses + partner(losses)

    scale_bin = LOSS_SCALE * weights / floored
    coefficient = jnp.sum(one_hot * scale_bin[None, :], axis=1) * (2.0 / (per_sample * full_width))
    grad_gate = coefficient[:, None] * error_proj
    d_exact = coefficient[:, None, None] * error_cube * gate[:, None, :]
    bound = ATTN_BOUND * jnp.max(jnp.sum(jnp.abs(d_exact), axis=(0, 1))) * 1.01
    d_proj = d_exact.astype(jnp.bfloat16).reshape(tok_rows, own_cols)
    total = lax.dot_general(
        whole_attn, d_proj, (((0,), (0,)), ((), ())), preferred_element_type=jnp.float32
    )
    for axis in DP:
        size = lax.axis_size(axis)
        rows = total.shape[0] // size
        got = lax.all_to_all(packed(total, losses, bound, size), axis, 0, 0, tiled=True)
        total, losses, bound = unpacked(got, rows)
    bin_loss = weights * losses / floored
    return (total, grad_gate, bin_loss)


def solution(mesh):
    finer = Mesh(mesh.devices.reshape(4, 8, 12, mesh.shape["mp"]), ("dp_0", "dp_1", "dp_2", "mp"))
    placed = (P(DP, "mp"), P("mp", None), P(DP, "mp"), P(DP, "mp"), P(DP, "mp"), P(DP))
    return jax.shard_map(
        shards,
        mesh=finer,
        in_specs=placed,
        out_specs=(P(DP, "mp"), P(DP, "mp"), P()),
        check_vma=False,
    )
```

time: 319 us -> 150 us (0.47)
  waiting for transfers between devices: 157 us -> 23.8 us
  blocking collectives: 116 us -> 77.4 us
  starting transfers between devices: 8.76 us -> 22.2 us
  other arithmetic: 0.93 us -> 12.4 us
  local copies, waits for them, and re-layouts: 14.1 us -> 3.39 us
  between operations: 14.5 us -> 5.53 us
    psum x8 -> x0, blocking collectives: 116 us -> none  [over_axes(): x = lax.psum(x, axis)]
    unnamed x5 -> x0, waiting for transfers between devices: 106 us -> none
    all_to_all x0 -> x3, blocking collectives: none -> 77.4 us  [the longest x2 56.5 us: shards(): lax.all_to_all(packed(total, losses, bound, size), axis, 0, 0, tiled=True)]
    reduce_scatter x1 -> x0, waiting for transfers between devices: 49.6 us -> none  [summed_rows(): x = lax.psum_scatter(x, axis, scatter_dimension=dim, tiled=True)]
    all_to_all x2, waiting for transfers between devices: 0.62 us -> 23.8 us  [the longest x1 15.8 us: shards(): lax.all_to_all(packed(total, losses, bound, size), axis, 0, 0, tiled=True)]
    all_to_all x2, starting transfers between devices: 8.64 us -> 16.5 us  [the longest x1 12.9 us: summed_everywhere(): return jnp.sum(lax.all_to_all(spread, axes, 0, 0, tiled=True), axis=0)]
    unnamed x11 -> x27, local copies, waits for them, and re-layouts: 7.67 us -> 1.15 us
    ppermute x0 -> x3, starting transfers between devices: none -> 5.75 us  [partner(): return lax.ppermute(x, 'mp', [(0, 1), (1, 0)])]
  transfers between devices with their start and end apart: 5 -> 5, of which waited for: 3 -> 2; matrix products, arithmetic and copies ran while one was open for 2% -> 4% of each run, Pallas kernels for 0% -> 0%
where the time goes in v1:
time: 150 us
  blocking collectives  77.4 us (52%)
  waiting for transfers between devices  23.8 us (16%)
  starting transfers between devices  22.2 us (15%)
  other arithmetic  12.4 us (8%)
  between operations  5.53 us (4%)
  matrix products  5.05 us (3%)
  local copies, waits for them, and re-layouts  3.39 us (2%)
    all_to_all x2, blocking collectives, shards(): lax.all_to_all(packed(total, losses, bound, size), axis, 0, 0, tiled=True)  56.5 us
    all_to_all x1, blocking collectives, summed_everywhere(): return jnp.sum(lax.all_to_all(spread, axes, 0, 0, tiled=True), axis=0)  20.9 us
    all_to_all x1, waiting for transfers between devices, shards(): lax.all_to_all(packed(total, losses, bound, size), axis, 0, 0, tiled=True)  15.8 us
    all_to_all x1, starting transfers between devices, summed_everywhere(): return jnp.sum(lax.all_to_all(spread, axes, 0, 0, tiled=True), axis=0)  12.9 us
    all_to_all x1, waiting for transfers between devices, summed_everywhere(): return jnp.sum(lax.all_to_all(spread, axes, 0, 0, tiled=True), axis=0)  8.07 us
    ppermute x3, starting transfers between devices, partner(): return lax.ppermute(x, 'mp', [(0, 1), (1, 0)])  5.75 us
    all_to_all x1, starting transfers between devices, shards(): lax.all_to_all(packed(total, losses, bound, size), axis, 0, 0, tiled=True)  3.55 us
  transfers between devices with their start and end apart: 5, of which 2 were waited for; matrix products, arithmetic and copies ran while one was open for 4% of the time, Pallas kernels for 0%

profile of v1, /device:TPU:2, one launch (start us, length us, event | category | flops | bytes accessed | tf_op | source)
XLA Modules:
  0.0 149.9 jit_solution(10875390039893381684)
XLA Ops:
  0.7 1.4 constant_dynamic-slice_fusion
  2.1 1.9 %collective-permute-start.1 = (bf16[768,768]{1,0:T(8,128)(2,1)S(1)}, bf16[768,768]{1,0:T(8,128)(2,1)S(1)}, u32[]{:S(2)}, u32[]{:S(2)}) collective-permute-start(bf16[768,768]{1,0:T(8,128)(2,1)S(1)} %constant_dynamic-slice_fusion), channel_id=1, source_target_pairs={{0,1},{1,0},{2,3},{3,2},{4,5},{5,4},{6,7},{7,6},{8,9},{9,8},{10,11... | collective-permute-start | bytes 3538952 | tf_op jit(solution)/shard_map/ppermute | solution.py:24
  4.1 20.9 %all_to_all.25 = f32[32,1,128]{2,1,0:T(1,128)S(1)} all-to-all(f32[32,1,128]{2,1,0:T(1,128)S(1)} %broadcast_in_dim.22), channel_id=1, replica_groups=mesh['dp_0'=4,'dp_1'=8,'dp_2'=12,'mp'=2] {'dp_0','dp_1'}, dimensions={0} | all-to-all | bytes 32768 | tf_op jit(solution)/shard_map/all_to_all | solution.py:30
  25.0 0.6 broadcast_in_dim.23
  25.6 12.9 %all-to-all-start.1 = ((f32[12,1,128]{2,1,0:T(1,128)}), f32[12,1,128]{2,1,0:T(1,128)S(1)}, u32[]{:S(2)}, u32[]{:S(2)}) async-start(f32[12,1,128]{2,1,0:T(1,128)} %broadcast_in_dim.23), calls=%async_computation.1 | async-start | bytes 12288 | tf_op jit(solution)/shard_map/all_to_all | solution.py:30
  38.6 1.9 %collective-permute-start = (bf16[384,768]{1,0:T(8,128)(2,1)S(1)}, bf16[384,768]{1,0:T(8,128)(2,1)}, u32[]{:S(2)}, u32[]{:S(2)}) collective-permute-start(bf16[384,768]{1,0:T(8,128)(2,1)S(1)} %copy-done.6), channel_id=1, source_target_pairs={{0,1},{1,0},{2,3},{3,2},{4,5},{5,4},{6,7},{7,6},{8,9},{9,8},{10,11... | collective-permute-start | bytes 1769480 | tf_op jit(solution)/shard_map/ppermute | solution.py:24
  40.5 8.1 %all-to-all-done.1 = f32[12,1,128]{2,1,0:T(1,128)S(1)} async-done(((f32[12,1,128]{2,1,0:T(1,128)}), f32[12,1,128]{2,1,0:T(1,128)S(1)}, u32[]{:S(2)}, u32[]{:S(2)}) %all-to-all-start.1) | async-done | bytes 6176 | tf_op jit(solution)/shard_map/all_to_all | solution.py:30
  48.9 0.2 copy-done.8
  49.2 1.5 broadcast_select_fusion.3
  50.7 0.5 copy-done.1
  51.2 0.5 broadcast_select_fusion.1
  52.0 2.6 %multiply_reduce_fusion.3 = (f32[384]{0:T(512)S(1)}, f32[768]{0:T(1024)S(1)}, bf16[384,768]{1,0:T(8,128)(2,1)}, f32[384,768]{1,0:T(8,128)}) fusion(bf16[384,768]{1,0:T(8,128)(2,1)S(1)} %copy-done.2, f32[3,768]{1,0:T(4,128)S(1)} %copy-done.7, bf16[384,768]{1,0:T(8,128)(2,1)S(1)} %copy-done.4, f32[384]{0:T(512)S(1)} %broadcast_bitcast_fusion, ...), kind=kOutput, calls=%fused_computation.15 | convolution fusion | flops 916585344 | bytes 6503424 | tf_op jit(solution)/shard_map/dot_general | solution.py:99
  54.6 0.6 reduce_max.36
  56.0 0.6 select_reduce_fusion
  56.6 1.9 %collective-permute-start.2 = (f32[128]{0:T(128)}, f32[128]{0:T(128)}, u32[]{:S(2)}, u32[]{:S(2)}) collective-permute-start(f32[128]{0:T(128)} %select_reduce_fusion), channel_id=1, source_target_pairs={{0,1},{1,0},{2,3},{3,2},{4,5},{5,4},{6,7},{7,6},{8,9},{9,8},{10,11... | collective-permute-start | bytes 1544 | tf_op jit(solution)/shard_map/ppermute | solution.py:24
  58.5 2.5 %multiply_convert_fusion = f16[1536,768]{1,0:T(8,128)(2,1)S(1)} fusion(bf16[384,768]{1,0:T(8,128)(2,1)} %get-tuple-element.17, f32[]{:T(128)S(6)} %exp2.131, bf16[384,768]{1,0:T(8,128)(2,1)S(1)} %get-tuple-element.19, bf16[384,768]{1,0:T(8,128)(2,1)S(1)} %get-tuple-element.18), kind=kOutput, calls=%fused_computation.1 | convolution fusion | flops 910688256 | bytes 4128772 | tf_op jit(solution)/shard_map/dot_general | solution.py:117
  61.1 1.3 fusion.40
  63.2 0.6 pad_maximum_fusion
  63.7 33.0 %all_to_all.26 = f16[4,392,768]{2,1,0:T(8,128)(2,1)S(1)} all-to-all(f16[4,392,768]{2,1,0:T(8,128)(2,1)S(1)} %pad_maximum_fusion), channel_id=1, replica_groups=mesh['dp_0'=4,'dp_1'=8,'dp_2'=12,'mp'=2] {'dp_0'}, dimensions={0} | all-to-all | bytes 4816896 | tf_op jit(solution)/shard_map/all_to_all | solution.py:123
  96.8 0.6 exponential_reduce_fusion.3
  98.2 0.6 reduce_max.38
  99.6 0.6 multiply_reduce_fusion
  100.5 23.5 %all_to_all.27 = f16[8,56,768]{2,1,0:T(8,128)(2,1)S(1)} all-to-all(f16[8,56,768]{2,1,0:T(8,128)(2,1)S(1)} %pad_maximum_fusion.4), channel_id=1, replica_groups=mesh['dp_0'=4,'dp_1'=8,'dp_2'=12,'mp'=2] {'dp_1'}, dimensions={0} | all-to-all | bytes 1376256 | tf_op jit(solution)/shard_map/all_to_all | solution.py:123
  124.0 0.6 fusion.20
  125.4 0.6 reduce_max.39
  127.2 0.8 fusion.8
  128.0 3.5 %all-to-all-start.4 = ((f16[12,16,768]{2,1,0:T(8,128)(2,1)}), f16[12,16,768]{2,1,0:T(8,128)(2,1)S(1)}, u32[]{:S(2)}, u32[]{:S(2)}) async-start(f16[12,16,768]{2,1,0:T(8,128)(2,1)} %fusion.8), calls=%async_computation.4 | async-start | bytes 589824 | tf_op jit(solution)/shard_map/all_to_all | solution.py:123
  131.6 0.3 multiply_reduce_fusion.1
  131.9 0.7 broadcast_multiply_fusion
  132.6 15.8 %all-to-all-done.4 = f16[12,16,768]{2,1,0:T(8,128)(2,1)S(1)} async-done(((f16[12,16,768]{2,1,0:T(8,128)(2,1)}), f16[12,16,768]{2,1,0:T(8,128)(2,1)S(1)}, u32[]{:S(2)}, u32[]{:S(2)}) %all-to-all-start.4) | async-done | bytes 294944 | tf_op jit(solution)/shard_map/all_to_all | solution.py:123
  148.6 0.5 multiply_divide_fusion
  149.2 0.7 multiply_reduce_fusion.4
  (68 shorter events, 2.1 us)
Async XLA Ops:
  0.6 3.4 %copy-start.10 = (s32[3]{0:T(128)S(1)}, s32[3]{0:T(128)}, u32[]{:S(2)}) copy-start(s32[3]{0:T(128)} %param.11) | copy-start | bytes 40
  0.6 37.9 %copy-start.6 = (bf16[384,768]{1,0:T(8,128)(2,1)S(1)}, bf16[384,768]{1,0:T(8,128)(2,1)}, u32[]{:S(2)}) copy-start(bf16[384,768]{1,0:T(8,128)(2,1)} %param.6) | copy-start | bytes 1769476
  2.1 48.6 %collective-permute-start.1 = (bf16[768,768]{1,0:T(8,128)(2,1)S(1)}, bf16[768,768]{1,0:T(8,128)(2,1)S(1)}, u32[]{:S(2)}, u32[]{:S(2)}) collective-permute-start(bf16[768,768]{1,0:T(8,128)(2,1)S(1)} %constant_dynamic-slice_fusion), channel_id=1, source_target_pairs={{0,1},{1,0},{2,3},{3,2},{4,5},{5,4},{6,7},{7,6},{8,9},{9,8},{10,11... | collective-permute-start | bytes 3538952 | tf_op jit(solution)/shard_map/ppermute | solution.py:24
  25.6 23.0 %all-to-all-start.1 = ((f32[12,1,128]{2,1,0:T(1,128)}), f32[12,1,128]{2,1,0:T(1,128)S(1)}, u32[]{:S(2)}, u32[]{:S(2)}) async-start(f32[12,1,128]{2,1,0:T(1,128)} %broadcast_in_dim.23), calls=%async_computation.1 | async-start | bytes 12288 | tf_op jit(solution)/shard_map/all_to_all | solution.py:30
  38.6 10.6 %collective-permute-start = (bf16[384,768]{1,0:T(8,128)(2,1)S(1)}, bf16[384,768]{1,0:T(8,128)(2,1)}, u32[]{:S(2)}, u32[]{:S(2)}) collective-permute-start(bf16[384,768]{1,0:T(8,128)(2,1)S(1)} %copy-done.6), channel_id=1, source_target_pairs={{0,1},{1,0},{2,3},{3,2},{4,5},{5,4},{6,7},{7,6},{8,9},{9,8},{10,11... | collective-permute-start | bytes 1769480 | tf_op jit(solution)/shard_map/ppermute | solution.py:24
  48.6 0.5 copy-start.8
  49.1 2.0 %copy-start.1 = (bf16[768,1536]{1,0:T(8,128)(2,1)S(1)}, bf16[768,1536]{1,0:T(8,128)(2,1)}, u32[]{:S(2)}) copy-start(bf16[768,1536]{1,0:T(8,128)(2,1)} %param.7) | copy-start | bytes 7077892
  50.6 1.2 copy-start.2
  50.6 1.4 copy-start.4
  50.7 1.4 copy-start.7
  52.0 4.0 %copy-start.11 = (s32[3]{0:T(128)S(1)}, s32[3]{0:T(128)}, u32[]{:S(2)}) copy-start(s32[3]{0:T(128)} %param.11) | copy-start | bytes 40
  56.6 4.4 %collective-permute-start.2 = (f32[128]{0:T(128)}, f32[128]{0:T(128)}, u32[]{:S(2)}, u32[]{:S(2)}) collective-permute-start(f32[128]{0:T(128)} %select_reduce_fusion), channel_id=1, source_target_pairs={{0,1},{1,0},{2,3},{3,2},{4,5},{5,4},{6,7},{7,6},{8,9},{9,8},{10,11... | collective-permute-start | bytes 1544 | tf_op jit(solution)/shard_map/ppermute | solution.py:24
  126.8 4.7 %copy-start = (f32[384,768]{1,0:T(8,128)S(1)}, f32[384,768]{1,0:T(8,128)}, u32[]{:S(2)}) copy-start(f32[384,768]{1,0:T(8,128)} %get-tuple-element.26) | copy-start | bytes 3538948
  126.8 4.7 %copy-start.3 = (bf16[384,768]{1,0:T(8,128)(2,1)S(1)}, bf16[384,768]{1,0:T(8,128)(2,1)}, u32[]{:S(2)}) copy-start(bf16[384,768]{1,0:T(8,128)(2,1)} %param.9) | copy-start | bytes 1769476
  126.9 4.7 %copy-start.5 = (bf16[384,768]{1,0:T(8,128)(2,1)S(1)}, bf16[384,768]{1,0:T(8,128)(2,1)}, u32[]{:S(2)}) copy-start(bf16[384,768]{1,0:T(8,128)(2,1)} %param.8) | copy-start | bytes 1769476
  128.0 20.3 %all-to-all-start.4 = ((f16[12,16,768]{2,1,0:T(8,128)(2,1)}), f16[12,16,768]{2,1,0:T(8,128)(2,1)S(1)}, u32[]{:S(2)}, u32[]{:S(2)}) async-start(f16[12,16,768]{2,1,0:T(8,128)(2,1)} %fusion.8), calls=%async_computation.4 | async-start | bytes 589824 | tf_op jit(solution)/shard_map/all_to_all | solution.py:123
  131.6 17.0 %copy-start.9 = (f32[128]{0:T(128)S(1)}, f32[128]{0:T(128)}, u32[]{:S(2)}) copy-start(f32[128]{0:T(128)} %copy-done.8) | copy-start | bytes 1540

commit v2 on v0

v2 whole, which is shorter than its diff:
```python
import math

import jax
import jax.numpy as jnp
from jax import lax
from jax.sharding import Mesh
from jax.sharding import PartitionSpec as P

NBINS = 128
X, YH, YL, ZH, ZL = "dp_x", "dp_yh", "dp_yl", "dp_zh", "dp_zl"
DP = (X, YH, YL, ZH, ZL)
NEAR = (X, YL, ZL)
FAR = (YH, ZH)
LOSS_SCALE = 4096.0
ATTN_BOUND = 6.0
TOP = 14.0
SIDE = 8
LOW = 1024.0


def bin_weights():
    centre = (jnp.arange(NBINS).astype(jnp.float32) + 0.5) / NBINS
    logit = jnp.log(centre) - jnp.log(1.0 - centre)
    return jnp.exp(-0.5 * logit * logit) / (math.sqrt(2.0 * math.pi) * centre * (1.0 - centre))


def group(axes):
    return math.prod(lax.axis_size(a) for a in axes)


def partner(x):
    return lax.ppermute(x, "mp", [(0, 1), (1, 0)])


def exchange(x, axes):
    return lax.all_to_all(x, axes, 0, 0, tiled=True)


def summed_everywhere(x, axes):
    spread = jnp.broadcast_to(x[None], (group(axes), *x.shape))
    return jnp.sum(exchange(spread, axes), axis=0)


def exponent_of(bound):
    return jnp.floor(jnp.log2(jnp.maximum(bound, 1e-30))) + 2.0


def halves(scaled):
    high = lax.reduce_precision(scaled, 5, 10)
    return high, (scaled - high) * LOW


def by_chunk(attn):
    tokens, feats = attn.shape
    yh, yl, zh, zl = (lax.axis_size(a) for a in (YH, YL, ZH, ZL))
    xs = lax.axis_size(X) // lax.axis_size("mp")
    last = feats // (xs * yh * yl * zh * zl)
    rows = attn.T.reshape(xs, yh, yl, zh, zl, last, tokens).transpose(0, 2, 4, 1, 3, 5, 6)
    rows = rows.reshape(xs * yl * zl, yh * zh * last, tokens)
    return jnp.pad(rows, ((0, 0), (0, SIDE), (0, 0))).reshape(-1, tokens)


def shards(attn, w_out, resid, target, gate, bins):
    samples = bins.shape[0]
    tok_rows, half = attn.shape
    per_sample = tok_rows // samples
    full_width = w_out.shape[1]
    own_cols = resid.shape[1]
    bin_ids = jnp.arange(NBINS, dtype=jnp.int32)
    one_hot = (bins[:, None] == bin_ids[None, :]).astype(jnp.float32)
    weights = bin_weights()
    me = lax.axis_index("mp")
    norm = per_sample * full_width

    counts = summed_everywhere(jnp.sum(one_hot, axis=0)[None], (X, YH, YL))
    counts = summed_everywhere(counts, (ZH, ZL))[0]
    floored = jnp.maximum(counts, 1.0)

    w_mine = lax.dynamic_slice_in_dim(w_out, me * own_cols, own_cols, axis=1)
    w_theirs = lax.dynamic_slice_in_dim(w_out, (1 - me) * own_cols, own_cols, axis=1)
    other = partner(jnp.concatenate([w_theirs, attn], axis=0))
    w_other, attn_other = other[:half], other[half:]
    projected = jnp.dot(attn, w_mine, preferred_element_type=jnp.float32) + jnp.dot(
        attn_other, w_other, preferred_element_type=jnp.float32
    )
    proj_cube = projected.reshape(samples, per_sample, own_cols)
    hidden = (
        resid.reshape(samples, per_sample, own_cols).astype(jnp.float32)
        + gate[:, None, :] * proj_cube
    )
    error_cube = hidden - target.reshape(samples, per_sample, own_cols).astype(jnp.float32)
    sample_error = jnp.sum(error_cube * error_cube, axis=(1, 2)) / norm
    error_proj = jnp.sum(error_cube * proj_cube, axis=1)
    losses = jnp.sum(one_hot * sample_error[:, None], axis=0)
    losses = losses + partner(losses)
    largest = jnp.sum(one_hot * (LOSS_SCALE * weights)[None, :], axis=1) * (2.0 / norm)
    reach = jnp.sum(largest[:, None] * jnp.sum(jnp.abs(error_cube * gate[:, None, :]), axis=1), axis=0)
    grad_exp = exponent_of(1.01 * ATTN_BOUND * jnp.max(reach))
    loss_exp = exponent_of(losses)
    high, low = halves(losses * jnp.exp2(TOP - loss_exp))

    first = me == 0
    own_rows, other_rows = by_chunk(attn), by_chunk(attn_other)
    features = jnp.concatenate(
        [jnp.where(first, own_rows, other_rows), jnp.where(first, other_rows, own_rows)], axis=0
    )
    widen = lambda row: jnp.pad(row, (0, own_cols - NBINS))
    side = [widen(high), widen(low), jnp.broadcast_to(grad_exp, (own_cols,)), widen(loss_exp)]
    near, far = group(NEAR), group(FAR)
    chunk = features.shape[0] // near
    keep = chunk - SIDE
    place = lax.broadcasted_iota(jnp.int32, (features.shape[0], 1), 0) % chunk

    scale_bin = LOSS_SCALE * weights / floored
    coefficient = jnp.sum(one_hot * scale_bin[None, :], axis=1) * (2.0 / norm)
    d_proj = (coefficient[:, None, None] * error_cube * gate[:, None, :]).astype(jnp.bfloat16)
    partial = jnp.dot(features, d_proj.reshape(tok_rows, own_cols), preferred_element_type=jnp.float32)
    partial = partial * jnp.exp2(TOP - grad_exp)
    for n, row in enumerate(side):
        partial = jnp.where(place == keep + n, row[None, :], partial)
    got = exchange(partial.astype(jnp.float16).reshape(near, chunk, own_cols), NEAR)

    sides = got[:, keep : keep + 4, :].astype(jnp.float32)
    grad_exp = jnp.max(sides[:, 2], axis=0) + math.log2(near)
    scale = jnp.exp2(sides[:, 2] - grad_exp)
    total = jnp.sum(got[:, :keep].astype(jnp.float32) * scale[:, None, :], axis=0)
    sides = sides[:, :, :NBINS]
    loss_exp = jnp.max(sides[:, 3], axis=0) + math.log2(near)
    high, low = halves(
        jnp.sum((sides[:, 0] + sides[:, 1] * (1.0 / LOW)) * jnp.exp2(sides[:, 3] - loss_exp), axis=0)
    )
    side = jnp.stack([high, low, grad_exp[:NBINS], loss_exp])
    side = jnp.pad(side, ((0, SIDE - 4), (0, 0))).astype(jnp.float16)
    body = total.astype(jnp.float16).reshape(far, -1, NBINS)
    keep = body.shape[1]
    body = jnp.concatenate([body, jnp.broadcast_to(side[None], (far, *side.shape))], axis=1)
    got = exchange(body, FAR).astype(jnp.float32)

    sides = got[:, keep : keep + 4]
    total = jnp.sum(got[:, :keep] * jnp.exp2(sides[:, 2:3] - TOP), axis=0)
    losses = jnp.sum((sides[:, 0] + sides[:, 1] * (1.0 / LOW)) * jnp.exp2(sides[:, 3] - TOP), axis=0)
    grad_gate = coefficient[:, None] * error_proj
    return (total.reshape(-1, own_cols), grad_gate, weights * losses / floored)


def solution(mesh):
    finer = Mesh(mesh.devices.reshape(4, 4, 2, 6, 2, mesh.shape["mp"]), (*DP, "mp"))
    placed = (P(DP, "mp"), P("mp", None), P(DP, "mp"), P(DP, "mp"), P(DP, "mp"), P(DP))
    return jax.shard_map(
        shards,
        mesh=finer,
        in_specs=placed,
        out_specs=(P(DP, "mp"), P(DP, "mp"), P()),
        check_vma=False,
    )
```

time: 319 us -> 143 us (0.45)
  the two profiles are of different devices: /device:TPU:2 before, /device:TPU:8 now
where the time goes in v2:
time: 143 us
  blocking collectives  35.5 us (25%)
  starting transfers between devices  33.3 us (23%)
  waiting for transfers between devices  31.3 us (22%)
  local copies, waits for them, and re-layouts  17.2 us (12%)
  other arithmetic  14.6 us (10%)
  matrix products  8.94 us (6%)
  between operations  1.79 us (1%)
    all_to_all x1, blocking collectives, exchange(): return lax.all_to_all(x, axes, 0, 0, tiled=True)  35.5 us
    all_to_all x3, waiting for transfers between devices, exchange(): return lax.all_to_all(x, axes, 0, 0, tiled=True)  31.3 us
    all_to_all x3, starting transfers between devices, exchange(): return lax.all_to_all(x, axes, 0, 0, tiled=True)  29.5 us
    transpose x5, local copies, waits for them, and re-layouts, by_chunk(): attn.T.reshape(xs, yh, yl, zh, zl, last, tokens)  6.62 us
    dot_general x1, matrix products, shards(): jnp.dot(features, d_proj.reshape(tok_rows, own_cols), preferred_element_t...  4.23 us
    ppermute x2, starting transfers between devices, partner(): return lax.ppermute(x, 'mp', [(0, 1), (1, 0)])  3.82 us
    reshape x2, local copies, waits for them, and re-layouts, by_chunk(): rows = rows.reshape(xs * yl * zl, yh * zh * last, tokens)  3.19 us
    dot_general x1, matrix products, shards(): jnp.dot(attn_other, w_other, preferred_element_type=jnp.float32)  3.09 us
  transfers between devices with their start and end apart: 5, of which 3 were waited for; matrix products, arithmetic and copies ran while one was open for 16% of the time, Pallas kernels for 0%

profile of v2, /device:TPU:8, one launch (start us, length us, event | category | flops | bytes accessed | tf_op | source)
XLA Modules:
  0.0 142.6 jit_solution(13720750900206308693)
XLA Ops:
  0.7 1.6 %copy-done = bf16[768,1536]{1,0:T(8,128)(2,1)S(1)} copy-done((bf16[768,1536]{1,0:T(8,128)(2,1)S(1)}, bf16[768,1536]{1,0:T(8,128)(2,1)}, u32[]{:S(2)}) %copy-start) | copy-done | bytes 2359320
  2.4 1.3 pad_maximum_fusion
  3.7 1.9 %collective-permute-start = (bf16[1152,768]{1,0:T(8,128)(2,1)}, bf16[1152,768]{1,0:T(8,128)(2,1)}, u32[]{:S(2)}, u32[]{:S(2)}) collective-permute-start(bf16[1152,768]{1,0:T(8,128)(2,1)} %pad_maximum_fusion), channel_id=1, source_target_pairs={{0,1},{1,0},{2,3},{3,2},{4,5},{5,4},{6,7},{7,6},{8,9},{9,8},{10,11... | collective-permute-start | bytes 5308424 | tf_op jit(solution)/shard_map/ppermute | solution.py:32
  5.7 0.6 broadcast_in_dim.88
  6.3 12.8 %all-to-all-start = ((f32[32,1,128]{2,1,0:T(1,128)}), f32[32,1,128]{2,1,0:T(1,128)S(1)}, u32[]{:S(2)}, u32[]{:S(2)}) async-start(f32[32,1,128]{2,1,0:T(1,128)} %broadcast_in_dim.88), calls=%async_computation | async-start | bytes 32768 | tf_op jit(solution)/shard_map/all_to_all | solution.py:36
  19.8 1.6 %convolution_bitcast_fusion = f32[384,768]{1,0:T(8,128)} fusion(bf16[384,768]{1,0:T(8,128)(2,1)S(1)} %copy-done.3, bf16[768,1536]{1,0:T(8,128)(2,1)S(1)} %copy-done, s32[]{:T(128)S(6)} %select_n.65), kind=kOutput, calls=%fused_computation.5 | convolution fusion | flops 452984832 | bytes 2949124 | tf_op jit(solution)/shard_map/dot_general | solution.py:83
  22.0 5.9 %all-to-all-done = f32[32,1,128]{2,1,0:T(1,128)S(1)} async-done(((f32[32,1,128]{2,1,0:T(1,128)}), f32[32,1,128]{2,1,0:T(1,128)S(1)}, u32[]{:S(2)}, u32[]{:S(2)}) %all-to-all-start) | async-done | bytes 16416 | tf_op jit(solution)/shard_map/all_to_all | solution.py:36
  28.6 12.4 %all-to-all-start.1 = ((f32[12,1,128]{2,1,0:T(1,128)}), f32[12,1,128]{2,1,0:T(1,128)}, u32[]{:S(2)}, u32[]{:S(2)}) async-start(f32[12,1,128]{2,1,0:T(1,128)} %broadcast_in_dim.89), calls=%async_computation.1 | async-start | bytes 12288 | tf_op jit(solution)/shard_map/all_to_all | solution.py:36
  42.2 1.0 reshape.174
  43.2 7.8 %all-to-all-done.1 = f32[12,1,128]{2,1,0:T(1,128)} async-done(((f32[12,1,128]{2,1,0:T(1,128)}), f32[12,1,128]{2,1,0:T(1,128)}, u32[]{:S(2)}, u32[]{:S(2)}) %all-to-all-start.1) | async-done | bytes 6176 | tf_op jit(solution)/shard_map/all_to_all | solution.py:36
  51.0 0.7 reduce_sum.144
  52.2 3.1 %multiply_reduce_fusion.2 = (f32[384]{0:T(512)S(1)}, f32[384,768]{1,0:T(8,128)S(1)}) fusion(bf16[384,768]{1,0:T(8,128)(2,1)} %param.9, f32[3,768]{1,0:T(4,128)S(1)} %copy-done.6, bf16[384,768]{1,0:T(8,128)(2,1)} %param.8, f32[384,768]{1,0:T(8,128)} %convolution_bitcast_fusion, bf16[1152,768]{1,0:T(8,128)(2,1)} %collective-permute-done), kind=kOutput, calls=%fused_computation.18 | convolution fusion | flops 455343744 | bytes 5319168 | tf_op jit(solution)/shard_map/dot_general | solution.py:83
  55.5 0.7 select_reduce_fusion
  56.7 1.0 multiply_reduce_fusion.1
  57.8 0.6 reduce_max.27
  59.1 0.7 broadcast_bitcast_fusion
  59.8 1.9 %collective-permute-start.1 = (f32[128]{0:T(128)}, f32[128]{0:T(128)}, u32[]{:S(2)}, u32[]{:S(2)}) collective-permute-start(f32[128]{0:T(128)} %get-tuple-element.7), channel_id=1, source_target_pairs={{0,1},{1,0},{2,3},{3,2},{4,5},{5,4},{6,7},{7,6},{8,9},{9,8},{10,11... | collective-permute-start | bytes 1544 | tf_op jit(solution)/shard_map/ppermute | solution.py:32
  61.7 1.9 %slice_bitcast_fusion = bf16[768,384]{0,1:T(8,128)(2,1)} fusion(bf16[1152,768]{1,0:T(8,128)(2,1)} %collective-permute-done), kind=kLoop, calls=%fused_computation.22 | loop fusion | bytes 1179648 | tf_op jit(solution)/shard_map/transpose | solution.py:58
  63.6 2.1 %copy.50 = bf16[768,384]{1,0:T(8,128)(2,1)} copy(bf16[768,384]{0,1:T(8,128)(2,1)} %slice_bitcast_fusion) | data formatting | bytes 1179648 | tf_op jit(solution)/shard_map/transpose | solution.py:58
  65.7 2.3 %reshape.175 = bf16[2,4,2,6,2,4,384]{6,5,4,3,2,1,0:T(4,128)(2,1)} reshape(bf16[768,384]{1,0:T(8,128)(2,1)} %copy.50) | data formatting | bytes 1179648 | tf_op jit(solution)/shard_map/reshape | solution.py:58
  68.0 2.1 %copy.51 = bf16[2,2,2,4,6,4,384]{6,5,4,3,2,1,0:T(4,128)(2,1)} copy(bf16[2,2,2,4,6,4,384]{6,5,2,4,1,3,0:T(4,128)(2,1)} %bitcast.60) | data formatting | bytes 1179648 | tf_op jit(solution)/shard_map/transpose | solution.py:58
  70.1 2.2 %reshape.176 = bf16[8,96,384]{2,1,0:T(8,128)(2,1)} reshape(bf16[2,2,2,4,6,4,384]{6,5,4,3,2,1,0:T(4,128)(2,1)} %copy.51) | data formatting | bytes 1179648 | tf_op jit(solution)/shard_map/reshape | solution.py:59
  72.3 2.5 %broadcast_select_fusion.1 = (bf16[8,104,384]{2,1,0:T(8,128)(2,1)}, bf16[8,104,384]{2,1,0:T(8,128)(2,1)}) fusion(pred[]{:T(512)S(6)} %eq.73, bf16[8,96,384]{2,1,0:T(8,128)(2,1)} %reshape.176, bf16[8,96,384]{2,1,0:T(8,128)(2,1)} %reshape.174), kind=kLoop, calls=%fused_computation.21 | loop fusion | flops 638976 | bytes 2457601 | tf_op jit(solution)/shard_map/jit(_where)/select_n | solution.py:105
  74.9 1.6 %fusion.8 = bf16[384,768]{1,0:T(8,128)(2,1)S(1)} fusion(f32[384]{0:T(512)S(1)} %broadcast_bitcast_fusion, f32[3,768]{1,0:T(4,128)S(1)} %copy-done.6, bf16[384,768]{1,0:T(8,128)(2,1)} %param.9, f32[384,768]{1,0:T(8,128)S(1)} %get-tuple-element.26, bf16[384,768]{1,0:T(8,128)(2,1)} %param.8), kind=kLoop, calls=%fused_computation.13 | loop fusion | flops 2359296 | bytes 2959872 | tf_op jit(solution)/shard_map/convert_element_type | solution.py:116
  76.6 0.6 subtract_multiply_fusion
  77.3 4.2 %select_convert_fusion = f16[1664,768]{1,0:T(8,128)(2,1)S(1)} fusion(f32[]{:T(128)S(6)} %exp2.57, f32[768]{0:T(1024)S(1)} %pad.24, f32[768]{0:T(1024)S(1)} %pad.23, f32[]{:T(128)S(6)} %add.134, f32[768]{0:T(1024)S(1)} %pad.22, pred[1664]{0:T(1024)(128)(4,1)S(1)} %copy-done.10, pred[1664]{0:T(1024)(128)(4,1)S(1)} %copy-done.11, ...), kind=kOutput, calls=%fused_computation | convolution fusion | flops 991690752 | bytes 4439560 | tf_op jit(solution)/shard_map/dot_general | solution.py:117
  81.6 35.5 %all_to_all.20 = f16[16,104,768]{2,1,0:T(8,128)(2,1)S(1)} all-to-all(f16[16,104,768]{2,1,0:T(8,128)(2,1)S(1)} %bitcast.57), channel_id=1, replica_groups=mesh['dp_x'=4,'dp_yh'=4,'dp_yl'=2,'dp_zh'=6,'dp_zl'=2,'mp'=2] {'dp_x','d..., dimensions={0} | all-to-all | bytes 5111808 | tf_op jit(solution)/shard_map/all_to_all | solution.py:36
  118.1 0.7 pad_maximum_fusion.1
  118.8 4.2 %all-to-all-start.3 = ((f16[24,32,128]{2,1,0:T(8,128)(2,1)}), f16[24,32,128]{2,1,0:T(8,128)(2,1)S(1)}, u32[]{:S(2)}, u32[]{:S(2)}) async-start(f16[24,32,128]{2,1,0:T(8,128)(2,1)} %pad_maximum_fusion.1), calls=%async_computation.3 | async-start | bytes 393216 | tf_op jit(solution)/shard_map/all_to_all | solution.py:36
  123.1 0.7 broadcast_multiply_fusion
  123.8 17.5 %all-to-all-done.3 = f16[24,32,128]{2,1,0:T(8,128)(2,1)S(1)} async-done(((f16[24,32,128]{2,1,0:T(8,128)(2,1)}), f16[24,32,128]{2,1,0:T(8,128)(2,1)S(1)}, u32[]{:S(2)}, u32[]{:S(2)}) %all-to-all-start.3) | async-done | bytes 196640 | tf_op jit(solution)/shard_map/all_to_all | solution.py:36
  142.0 0.6 reshape.178
  (75 shorter events, 6.2 us)
Async XLA Ops:
  0.6 1.7 %copy-start = (bf16[768,1536]{1,0:T(8,128)(2,1)S(1)}, bf16[768,1536]{1,0:T(8,128)(2,1)}, u32[]{:S(2)}) copy-start(bf16[768,1536]{1,0:T(8,128)(2,1)} %param.7) | copy-start | bytes 7077892
  0.6 1.8 %copy-start.3 = (bf16[384,768]{1,0:T(8,128)(2,1)S(1)}, bf16[384,768]{1,0:T(8,128)(2,1)}, u32[]{:S(2)}) copy-start(bf16[384,768]{1,0:T(8,128)(2,1)} %param.6) | copy-start | bytes 1769476
  2.4 3.2 %copy-start.16 = (s32[3]{0:T(128)S(1)}, s32[3]{0:T(128)}, u32[]{:S(2)}) copy-start(s32[3]{0:T(128)} %param.11) | copy-start | bytes 40
  3.7 48.5 %collective-permute-start = (bf16[1152,768]{1,0:T(8,128)(2,1)}, bf16[1152,768]{1,0:T(8,128)(2,1)}, u32[]{:S(2)}, u32[]{:S(2)}) collective-permute-start(bf16[1152,768]{1,0:T(8,128)(2,1)} %pad_maximum_fusion), channel_id=1, source_target_pairs={{0,1},{1,0},{2,3},{3,2},{4,5},{5,4},{6,7},{7,6},{8,9},{9,8},{10,11... | collective-permute-start | bytes 5308424 | tf_op jit(solution)/shard_map/ppermute | solution.py:32
  6.3 21.6 %all-to-all-start = ((f32[32,1,128]{2,1,0:T(1,128)}), f32[32,1,128]{2,1,0:T(1,128)S(1)}, u32[]{:S(2)}, u32[]{:S(2)}) async-start(f32[32,1,128]{2,1,0:T(1,128)} %broadcast_in_dim.88), calls=%async_computation | async-start | bytes 32768 | tf_op jit(solution)/shard_map/all_to_all | solution.py:36
  28.6 22.4 %all-to-all-start.1 = ((f32[12,1,128]{2,1,0:T(1,128)}), f32[12,1,128]{2,1,0:T(1,128)}, u32[]{:S(2)}, u32[]{:S(2)}) async-start(f32[12,1,128]{2,1,0:T(1,128)} %broadcast_in_dim.89), calls=%async_computation.1 | async-start | bytes 12288 | tf_op jit(solution)/shard_map/all_to_all | solution.py:36
  42.0 10.2 %copy-start.6 = (f32[3,768]{1,0:T(4,128)S(1)}, f32[3,768]{1,0:T(4,128)}, u32[]{:S(2)}) copy-start(f32[3,768]{1,0:T(4,128)} %param.10) | copy-start | bytes 27652
  51.7 0.5 copy-start.14
  52.2 3.2 %copy-start.17 = (f32[128]{0:T(128)S(1)}, f32[128]{0:T(128)}, u32[]{:S(2)}) copy-start(f32[128]{0:T(128)} %broadcast_multiply_fusion.3) | copy-start | bytes 1540
  52.2 4.5 %copy-start.1 = (bf16[384,768]{1,0:T(8,128)(2,1)S(1)}, bf16[384,768]{1,0:T(8,128)(2,1)}, u32[]{:S(2)}) copy-start(bf16[384,768]{1,0:T(8,128)(2,1)} %param.9) | copy-start | bytes 1769476
  52.2 4.5 %copy-start.2 = (bf16[384,768]{1,0:T(8,128)(2,1)S(1)}, bf16[384,768]{1,0:T(8,128)(2,1)}, u32[]{:S(2)}) copy-start(bf16[384,768]{1,0:T(8,128)(2,1)} %param.8) | copy-start | bytes 1769476
  59.8 16.8 %collective-permute-start.1 = (f32[128]{0:T(128)}, f32[128]{0:T(128)}, u32[]{:S(2)}, u32[]{:S(2)}) collective-permute-start(f32[128]{0:T(128)} %get-tuple-element.7), channel_id=1, source_target_pairs={{0,1},{1,0},{2,3},{3,2},{4,5},{5,4},{6,7},{7,6},{8,9},{9,8},{10,11... | collective-permute-start | bytes 1544 | tf_op jit(solution)/shard_map/ppermute | solution.py:32
  74.8 1.7 %copy-start.9 = (f32[128]{0:T(128)S(1)}, f32[128]{0:T(128)}, u32[]{:S(2)}) copy-start(f32[128]{0:T(128)} %get-tuple-element.7) | copy-start | bytes 1540
  74.8 2.4 %copy-start.4 = (bf16[8,104,384]{2,1,0:T(8,128)(2,1)S(1)}, bf16[8,104,384]{2,1,0:T(8,128)(2,1)}, u32[]{:S(2)}) copy-start(bf16[8,104,384]{2,1,0:T(8,128)(2,1)} %get-tuple-element.10) | copy-start | bytes 1916932
  74.9 2.4 %copy-start.5 = (bf16[8,104,384]{2,1,0:T(8,128)(2,1)S(1)}, bf16[8,104,384]{2,1,0:T(8,128)(2,1)}, u32[]{:S(2)}) copy-start(bf16[8,104,384]{2,1,0:T(8,128)(2,1)} %get-tuple-element.11) | copy-start | bytes 1916932
  74.9 2.4 %copy-start.10 = (pred[1664]{0:T(1024)(128)(4,1)S(1)}, pred[1664]{0:T(1024)(128)(4,1)}, u32[]{:S(2)}) copy-start(pred[1664]{0:T(1024)(128)(4,1)} %get-tuple-element.29) | copy-start | bytes 4996
  74.9 2.4 %copy-start.11 = (pred[1664]{0:T(1024)(128)(4,1)S(1)}, pred[1664]{0:T(1024)(128)(4,1)}, u32[]{:S(2)}) copy-start(pred[1664]{0:T(1024)(128)(4,1)} %get-tuple-element.30) | copy-start | bytes 4996
  74.9 2.4 %copy-start.12 = (pred[1664]{0:T(1024)(128)(4,1)S(1)}, pred[1664]{0:T(1024)(128)(4,1)}, u32[]{:S(2)}) copy-start(pred[1664]{0:T(1024)(128)(4,1)} %get-tuple-element.31) | copy-start | bytes 4996
  74.9 2.4 %copy-start.13 = (pred[1664]{0:T(1024)(128)(4,1)S(1)}, pred[1664]{0:T(1024)(128)(4,1)}, u32[]{:S(2)}) copy-start(pred[1664]{0:T(1024)(128)(4,1)} %get-tuple-element.32) | copy-start | bytes 4996
  117.8 5.3 %copy-start.7 = (f32[3,768]{1,0:T(4,128)S(1)}, f32[3,768]{1,0:T(4,128)}, u32[]{:S(2)}) copy-start(f32[3,768]{1,0:T(4,128)} %get-tuple-element.3) | copy-start | bytes 27652
  117.8 5.3 %copy-start.8 = (f32[3]{0:T(128)S(1)}, f32[3]{0:T(128)}, u32[]{:S(2)}) copy-start(f32[3]{0:T(128)} %get-tuple-element.27) | copy-start | bytes 40
  117.8 23.6 %copy-start.15 = (f32[128]{0:T(128)S(1)}, f32[128]{0:T(128)}, u32[]{:S(2)}) copy-start(f32[128]{0:T(128)} %copy-done.14) | copy-start | bytes 1540
  118.8 22.5 %all-to-all-start.3 = ((f16[24,32,128]{2,1,0:T(8,128)(2,1)}), f16[24,32,128]{2,1,0:T(8,128)(2,1)S(1)}, u32[]{:S(2)}, u32[]{:S(2)}) async-start(f16[24,32,128]{2,1,0:T(8,128)(2,1)} %pad_maximum_fusion.1), calls=%async_computation.3 | async-start | bytes 393216 | tf_op jit(solution)/shard_map/all_to_all | solution.py:36

commit v3 on v2

v3 whole, which is shorter than its diff:
```python
import math

import jax
import jax.numpy as jnp
from jax import lax
from jax.experimental import pallas as pl
from jax.experimental.pallas import tpu as pltpu
from jax.sharding import Mesh
from jax.sharding import PartitionSpec as P

NBINS = 128
X, YH, YL, ZH, ZL = "dp_x", "dp_yh", "dp_yl", "dp_zh", "dp_zl"
DP = (X, YH, YL, ZH, ZL)
NEAR = (X, YL, ZL)
FAR = (YH, ZH)
LOSS_SCALE = 4096.0
ATTN_BOUND = 6.0
TOP = 14.0
SIDE = 8
LOW = 1024.0


def bin_weights():
    return weights_at(jnp.arange(NBINS).astype(jnp.float32))


def weights_at(index):
    centre = (index + 0.5) / NBINS
    logit = jnp.log(centre) - jnp.log(1.0 - centre)
    return jnp.exp(-0.5 * logit * logit) / (math.sqrt(2.0 * math.pi) * centre * (1.0 - centre))


def group(axes):
    return math.prod(lax.axis_size(a) for a in axes)


def partner(x):
    return lax.ppermute(x, "mp", [(0, 1), (1, 0)])


def exchange(x, axes):
    return lax.all_to_all(x, axes, 0, 0, tiled=True)


def summed_everywhere(x, axes):
    spread = jnp.broadcast_to(x[None], (group(axes), *x.shape))
    return jnp.sum(exchange(spread, axes), axis=0)


def exponent_of(bound):
    return jnp.floor(jnp.log2(jnp.maximum(bound, 1e-30))) + 2.0


def halves(scaled):
    high = lax.reduce_precision(scaled, 5, 10)
    return high, (scaled - high) * LOW


def forward_kernel(
    me, bins, attn, other, part, resid, target, gate, error, features, error_proj, losses, grad_exp
):
    tokens, half = attn.shape
    samples = gate.shape[0]
    per_sample = tokens // samples
    run = half // 2
    row = lax.broadcasted_iota(jnp.int32, (run, run), 0)
    piece = (row * 683) >> 16
    inner = row - 96 * piece
    quad = inner >> 2
    y_high = (quad * 43) >> 8
    z_high = quad - 6 * y_high
    source = y_high * 96 + (piece >> 1) * 48 + z_high * 8 + (piece & 1) * 4 + (inner & 3)
    picks = (source == lax.broadcasted_iota(jnp.int32, (run, run), 1)).astype(jnp.bfloat16)
    own, far = me[0] * half, (1 - me[0]) * half
    for first, block in ((own, attn), (far, other.at[half:, :])):
        for n in range(2):
            moved = lax.dot_general(
                picks,
                block[:, n * run : (n + 1) * run],
                (((1,), (1,)), ((), ())),
                preferred_element_type=jnp.float32,
            )
            features[pl.ds(pl.multiple_of(first + n * run, run), run), :] = moved.astype(jnp.bfloat16)

    lane = lax.broadcasted_iota(jnp.int32, (1, NBINS), 1)
    steepest = weights_at(lane.astype(jnp.float32)) * (LOSS_SCALE / (per_sample * half))
    found = jnp.zeros((1, NBINS), jnp.float32)
    reach = jnp.zeros((1, half), jnp.float32)
    for s in range(samples):
        rows = slice(s * per_sample, (s + 1) * per_sample)
        projected = part[rows, :] + jnp.dot(
            other[half + s * per_sample : half + (s + 1) * per_sample, :],
            other[:half, :],
            preferred_element_type=jnp.float32,
        )
        scale = gate[s : s + 1, :]
        diff = resid[rows, :].astype(jnp.float32) + scale * projected - target[rows, :].astype(jnp.float32)
        error[rows, :] = diff
        error_proj[s : s + 1, :] = jnp.sum(diff * projected, axis=0, keepdims=True)
        mine = lane == bins[s]
        largest = jnp.sum(jnp.where(mine, steepest, 0.0), axis=1, keepdims=True)
        reach = reach + largest * jnp.sum(jnp.abs(diff * scale), axis=0, keepdims=True)
        squares = jnp.sum(jnp.sum(diff * diff, axis=0, keepdims=True), axis=1, keepdims=True)
        found = found + jnp.where(mine, squares * (1.0 / (per_sample * 2 * half)), 0.0)
    losses[...] = found
    bound = jnp.max(reach, axis=1, keepdims=True) * (1.01 * ATTN_BOUND)
    grad_exp[...] = jnp.broadcast_to(exponent_of(bound), (1, NBINS))


def forward(me, bins, attn, other, part, resid, target, gate):
    tokens, half = attn.shape
    vmem, smem = pl.BlockSpec(memory_space=pltpu.VMEM), pl.BlockSpec(memory_space=pltpu.SMEM)
    return pl.pallas_call(
        forward_kernel,
        out_shape=(
            jax.ShapeDtypeStruct((tokens, half), jnp.float32),
            jax.ShapeDtypeStruct((2 * half, tokens), jnp.bfloat16),
            jax.ShapeDtypeStruct(gate.shape, jnp.float32),
            jax.ShapeDtypeStruct((1, NBINS), jnp.float32),
            jax.ShapeDtypeStruct((1, NBINS), jnp.float32),
        ),
        in_specs=[smem] * 2 + [vmem] * 6,
        out_specs=(vmem,) * 5,
        cost_estimate=pl.CostEstimate(flops=2 * 10**9, bytes_accessed=8 * 10**6, transcendentals=0),
        compiler_params=pltpu.CompilerParams(vmem_limit_bytes=20 * 2**20),
        name="forward",
    )(me, bins, attn, other, part, resid, target, gate)


def body(attn, w_out, resid, target, gate, bins):
    samples = bins.shape[0]
    tok_rows, _ = attn.shape
    per_sample = tok_rows // samples
    full_width = w_out.shape[1]
    own_cols = resid.shape[1]
    bin_ids = jnp.arange(NBINS, dtype=jnp.int32)
    one_hot = (bins[:, None] == bin_ids[None, :]).astype(jnp.float32)
    weights = bin_weights()
    me = lax.axis_index("mp")
    norm = per_sample * full_width

    counts = summed_everywhere(jnp.sum(one_hot, axis=0)[None], (X, YH, YL))
    counts = summed_everywhere(counts, (ZH, ZL))[0]
    floored = jnp.maximum(counts, 1.0)

    w_mine = lax.dynamic_slice_in_dim(w_out, me * own_cols, own_cols, axis=1)
    w_theirs = lax.dynamic_slice_in_dim(w_out, (1 - me) * own_cols, own_cols, axis=1)
    other = partner(jnp.concatenate([w_theirs, attn], axis=0))
    part = jnp.dot(attn, w_mine, preferred_element_type=jnp.float32)
    error, features, error_proj, losses, grad_exp = forward(
        me.reshape(1), bins, attn, other, part, resid, target, gate
    )
    error_cube = error.reshape(samples, per_sample, own_cols)
    losses, grad_exp = losses[0], grad_exp[0]
    losses = losses + partner(losses)
    loss_exp = exponent_of(losses)
    high, low = halves(losses * jnp.exp2(TOP - loss_exp))
    widen = lambda rows: jnp.pad(rows, ((0, SIDE - 4), (0, own_cols - NBINS)))
    side = widen(jnp.stack([high, low, grad_exp, loss_exp])).astype(jnp.float16)
    near, far = group(NEAR), group(FAR)

    scale_bin = LOSS_SCALE * weights / floored
    coefficient = jnp.sum(one_hot * scale_bin[None, :], axis=1) * (2.0 / norm)
    d_proj = (coefficient[:, None, None] * error_cube * gate[:, None, :]).astype(jnp.bfloat16)
    partial = jnp.dot(features, d_proj.reshape(tok_rows, own_cols), preferred_element_type=jnp.float32)
    grad_row = jnp.tile(jnp.exp2(TOP - grad_exp), own_cols // NBINS)
    partial = (partial * grad_row[None, :]).astype(jnp.float16).reshape(near, -1, own_cols)
    keep = partial.shape[1]
    partial = jnp.concatenate([partial, jnp.broadcast_to(side[None], (near, *side.shape))], axis=1)
    got = exchange(partial, NEAR)

    sides = got[:, keep : keep + 4, :NBINS].astype(jnp.float32)
    grad_exp = jnp.max(sides[:, 2], axis=0) + math.log2(near)
    scale = jnp.tile(jnp.exp2(sides[:, 2] - grad_exp), (1, own_cols // NBINS))
    total = jnp.sum(got[:, :keep].astype(jnp.float32) * scale[:, None, :], axis=0)
    loss_exp = jnp.max(sides[:, 3], axis=0) + math.log2(near)
    high, low = halves(
        jnp.sum((sides[:, 0] + sides[:, 1] * (1.0 / LOW)) * jnp.exp2(sides[:, 3] - loss_exp), axis=0)
    )
    side = jnp.stack([high, low, grad_exp, loss_exp])
    side = jnp.pad(side, ((0, SIDE - 4), (0, 0))).astype(jnp.float16)
    rows = total.astype(jnp.float16).reshape(far, -1, NBINS)
    keep = rows.shape[1]
    rows = jnp.concatenate([rows, jnp.broadcast_to(side[None], (far, *side.shape))], axis=1)
    got = exchange(rows, FAR).astype(jnp.float32)

    sides = got[:, keep : keep + 4]
    total = jnp.sum(got[:, :keep] * jnp.exp2(sides[:, 2:3] - TOP), axis=0)
    losses = jnp.sum((sides[:, 0] + sides[:, 1] * (1.0 / LOW)) * jnp.exp2(sides[:, 3] - TOP), axis=0)
    grad_gate = coefficient[:, None] * error_proj
    return (total.reshape(-1, own_cols), grad_gate, weights * losses / floored)


def solution(mesh):
    finer = Mesh(mesh.devices.reshape(4, 4, 2, 6, 2, mesh.shape["mp"]), (*DP, "mp"))
    placed = (P(DP, "mp"), P("mp", None), P(DP, "mp"), P(DP, "mp"), P(DP, "mp"), P(DP))
    return jax.shard_map(
        body,
        mesh=finer,
        in_specs=placed,
        out_specs=(P(DP, "mp"), P(DP, "mp"), P()),
        check_vma=False,
    )
```

time: 143 us -> 124 us (0.87)
  local copies, waits for them, and re-layouts: 17.2 us -> 7.27 us
  other arithmetic: 14.6 us -> 5.18 us
  matrix products: 8.94 us -> 3.03 us
  waiting for transfers between devices: 31.3 us -> 34.8 us
  Pallas kernels: 0 us -> 3.27 us
    transpose x5 -> x0, local copies, waits for them, and re-layouts: 6.62 us -> none  [by_chunk(): attn.T.reshape(xs, yh, yl, zh, zl, last, tokens)]
    dot_general x3 -> x2, matrix products: 8.94 us -> 3.03 us  [the longest x1 1.63 us: body(): part = jnp.dot(attn, w_mine, preferred_element_type=jnp.float32)]
    reshape x5 -> x1, local copies, waits for them, and re-layouts: 6.19 us -> 0.61 us  [body(): return (total.reshape(-1, own_cols), grad_gate, weights * losses / floored)]
    all_to_all x3, waiting for transfers between devices: 31.3 us -> 34.8 us  [exchange(): return lax.all_to_all(x, axes, 0, 0, tiled=True)]
    pallas_call x0 -> x1, Pallas kernels: none -> 3.27 us  [forward(): pl.pallas_call(forward_kernel, out_shape=(jax.ShapeDtypeStruct((tokens, h...]
    unnamed x37 -> x15, local copies, waits for them, and re-layouts: 2.27 us -> 5.1 us
    select_n x1 -> x0, other arithmetic: 2.51 us -> none  [shards(): jnp.where(first, own_rows, other_rows)]
    reduce_sum x9 -> x5, other arithmetic: 2.58 us -> 0.82 us  [the longest x1 0.48 us: body(): jnp.sum(got[:, :keep].astype(jnp.float32) * scale[:, None, :], axis=0)]
  transfers between devices with their start and end apart: 5 -> 5, of which waited for: 3 -> 3; matrix products, arithmetic and copies ran while one was open for 16% -> 4% of each run, Pallas kernels for 0% -> 0%
where the time goes in v3:
time: 124 us; the launch traced here: 123 us
  blocking collectives  35.5 us (29%)
  waiting for transfers between devices  34.8 us (28%)
  starting transfers between devices  33.3 us (27%)
  local copies, waits for them, and re-layouts  7.27 us (6%)
  other arithmetic  5.18 us (4%)
  Pallas kernels  3.27 us (3%)
  matrix products  3.03 us (2%)
    all_to_all x1, blocking collectives, exchange(): return lax.all_to_all(x, axes, 0, 0, tiled=True)  35.5 us
    all_to_all x3, waiting for transfers between devices, exchange(): return lax.all_to_all(x, axes, 0, 0, tiled=True)  34.8 us
    all_to_all x3, starting transfers between devices, exchange(): return lax.all_to_all(x, axes, 0, 0, tiled=True)  29.3 us
    unnamed x15, local copies, waits for them, and re-layouts  5.1 us
    ppermute x2, starting transfers between devices, partner(): return lax.ppermute(x, 'mp', [(0, 1), (1, 0)])  3.96 us
    pallas_call x1, Pallas kernels, forward(): pl.pallas_call(forward_kernel, out_shape=(jax.ShapeDtypeStruct((tokens, h...  3.27 us
  transfers between devices with their start and end apart: 5, of which 3 were waited for; matrix products, arithmetic and copies ran while one was open for 4% of the time, Pallas kernels for 0%

profile of v3, /device:TPU:8, one launch (start us, length us, event | category | flops | bytes accessed | tf_op | source)
XLA Modules:
  0.0 123.2 jit_solution(6580320333536725702)
XLA Ops:
  0.7 1.6 %copy-done = bf16[768,1536]{1,0:T(8,128)(2,1)S(1)} copy-done((bf16[768,1536]{1,0:T(8,128)(2,1)S(1)}, bf16[768,1536]{1,0:T(8,128)(2,1)}, u32[]{:S(2)}) %copy-start) | copy-done | bytes 2359320
  2.3 0.1 constant_dynamic-slice_fusion
  2.4 1.3 %pad_maximum_fusion.1 = bf16[1152,768]{1,0:T(8,128)(2,1)} fusion(bf16[384,768]{1,0:T(8,128)(2,1)S(1)} %copy-done.1, bf16[768,768]{1,0:T(8,128)(2,1)S(1)} %constant_dynamic-slice_fusion), kind=kLoop, calls=%fused_computation.3 | loop fusion | flops 3538944 | bytes 3538944 | tf_op jit(solution)/shard_map/concatenate | solution.py:148
  3.7 2.0 %collective-permute-start = (bf16[1152,768]{1,0:T(8,128)(2,1)}, bf16[1152,768]{1,0:T(8,128)(2,1)}, u32[]{:S(2)}, u32[]{:S(2)}) collective-permute-start(bf16[1152,768]{1,0:T(8,128)(2,1)} %pad_maximum_fusion.1), channel_id=1, source_target_pairs={{0,1},{1,0},{2,3},{3,2},{4,5},{5,4},{6,7},{7,6},{8,9},{9,8},{10,11... | collective-permute-start | bytes 5308424 | tf_op jit(solution)/shard_map/ppermute | solution.py:38
  5.8 0.1 convert_reduce_fusion
  5.9 0.6 broadcast_in_dim.8
  6.5 12.8 %all-to-all-start = ((f32[32,1,128]{2,1,0:T(1,128)}), f32[32,1,128]{2,1,0:T(1,128)S(1)}, u32[]{:S(2)}, u32[]{:S(2)}) async-start(f32[32,1,128]{2,1,0:T(1,128)} %broadcast_in_dim.8), calls=%async_computation | async-start | bytes 32768 | tf_op jit(solution)/shard_map/all_to_all | solution.py:42
  19.3 8.8 %all-to-all-done = f32[32,1,128]{2,1,0:T(1,128)S(1)} async-done(((f32[32,1,128]{2,1,0:T(1,128)}), f32[32,1,128]{2,1,0:T(1,128)S(1)}, u32[]{:S(2)}, u32[]{:S(2)}) %all-to-all-start) | async-done | bytes 16416 | tf_op jit(solution)/shard_map/all_to_all | solution.py:42
  28.1 0.6 broadcast_in_dim.9
  28.7 12.4 %all-to-all-start.1 = ((f32[12,1,128]{2,1,0:T(1,128)}), f32[12,1,128]{2,1,0:T(1,128)S(1)}, u32[]{:S(2)}, u32[]{:S(2)}) async-start(f32[12,1,128]{2,1,0:T(1,128)} %broadcast_in_dim.9), calls=%async_computation.1 | async-start | bytes 12288 | tf_op jit(solution)/shard_map/all_to_all | solution.py:42
  41.1 1.6 %convolution_bitcast_fusion.part = f32[384,768]{1,0:T(8,128)} fusion(bf16[384,768]{1,0:T(8,128)(2,1)S(1)} %copy-done.1, bf16[768,1536]{1,0:T(8,128)(2,1)S(1)} %copy-done, s32[]{:T(128)S(6)} %select_n.7), kind=kOutput, calls=%fused_computation.4 | convolution fusion | flops 452984832 | bytes 2949124 | tf_op jit(solution)/shard_map/dot_general | solution.py:149
  42.7 8.4 %all-to-all-done.1 = f32[12,1,128]{2,1,0:T(1,128)S(1)} async-done(((f32[12,1,128]{2,1,0:T(1,128)}), f32[12,1,128]{2,1,0:T(1,128)S(1)}, u32[]{:S(2)}, u32[]{:S(2)}) %all-to-all-start.1) | async-done | bytes 6176 | tf_op jit(solution)/shard_map/all_to_all | solution.py:42
  51.2 0.2 select_reduce_fusion
  51.4 0.1 broadcast_bitcast_fusion.1
  51.4 1.1 copy-done.3
  52.5 1.1 copy-done.4
  53.6 1.3 %copy-done.6 = f32[384,768]{1,0:T(8,128)S(1)} copy-done((f32[384,768]{1,0:T(8,128)S(1)}, f32[384,768]{1,0:T(8,128)}, u32[]{:S(2)}) %copy-start.6) | copy-done | bytes 1179672
  54.9 3.3 %forward.1 = (f32[384,768]{1,0:T(8,128)S(1)}, bf16[1536,384]{1,0:T(8,128)(2,1)S(1)}, f32[3,768]{1,0:T(4,128)S(1)}, f32[1,128]{1,0:T(1,128)S(1)}, f32[1,128]{1,0:T(1,128)S(1)}) custom-call(s32[1]{0:T(128)} %bitcast.me, s32[3]{0:T(128)S(1)} %copy-done.5, bf16[384,768]{1,0:T(8,128)(2,1)S(1)} %copy-done.1, bf16[1152,768]{1,0:T(8,128)(2,1)} %collective-permute-done.other, ...), custom_call_target="tpu_custom_call" | custom-call | flops 2000000000 | bytes 8000000 | tf_op jit(solution)/shard_map/forward/pallas_call | solution.py:113
  58.1 1.9 %collective-permute-start.1 = (f32[128]{0:T(128)S(1)}, f32[128]{0:T(128)S(1)}, u32[]{:S(2)}, u32[]{:S(2)}) collective-permute-start(f32[128]{0:T(128)S(1)} %bitcast.65), channel_id=1, source_target_pairs={{0,1},{1,0},{2,3},{3,2},{4,5},{5,4},{6,7},{7,6},{8,9},{9,8},{10,11... | collective-permute-start | bytes 1544 | tf_op jit(solution)/shard_map/ppermute | solution.py:38
  60.1 0.2 fusion
  60.3 1.4 %multiply_convert_fusion = f16[1536,768]{1,0:T(8,128)(2,1)S(1)} fusion(bf16[1536,384]{1,0:T(8,128)(2,1)S(1)} %get-tuple-element.8, bf16[384,768]{1,0:T(8,128)(2,1)S(1)} %fusion, f32[768]{0:T(1024)S(1)} %broadcast_bitcast_fusion), kind=kOutput, calls=%fused_computation.1 | convolution fusion | flops 908328960 | bytes 4131840 | tf_op jit(solution)/shard_map/dot_general | solution.py:165
  61.8 0.6 pad_maximum_fusion
  62.4 35.5 %all_to_all.20 = f16[16,104,768]{2,1,0:T(8,128)(2,1)S(1)} all-to-all(f16[16,104,768]{2,1,0:T(8,128)(2,1)S(1)} %pad_maximum_fusion), channel_id=1, replica_groups=mesh['dp_x'=4,'dp_yh'=4,'dp_yl'=2,'dp_zh'=6,'dp_zl'=2,'mp'=2] {'dp_x','d..., dimensions={0} | all-to-all | bytes 5111808 | tf_op jit(solution)/shard_map/all_to_all | solution.py:42
  98.0 0.5 multiply_reduce_fusion
  98.5 0.2 convert_element_type.48
  98.7 0.7 pad_maximum_fusion.2
  99.4 4.1 %all-to-all-start.3 = ((f16[24,32,128]{2,1,0:T(8,128)(2,1)}), f16[24,32,128]{2,1,0:T(8,128)(2,1)S(1)}, u32[]{:S(2)}, u32[]{:S(2)}) async-start(f16[24,32,128]{2,1,0:T(8,128)(2,1)} %pad_maximum_fusion.2), calls=%async_computation.3 | async-start | bytes 393216 | tf_op jit(solution)/shard_map/all_to_all | solution.py:42
  103.6 0.7 broadcast_multiply_fusion
  104.2 17.7 %all-to-all-done.3 = f16[24,32,128]{2,1,0:T(8,128)(2,1)S(1)} async-done(((f16[24,32,128]{2,1,0:T(8,128)(2,1)}), f16[24,32,128]{2,1,0:T(8,128)(2,1)S(1)}, u32[]{:S(2)}, u32[]{:S(2)}) %all-to-all-start.3) | async-done | bytes 196640 | tf_op jit(solution)/shard_map/all_to_all | solution.py:42
  121.9 0.1 copy_convert_fusion
  122.0 0.5 multiply_divide_fusion
  122.6 0.6 reshape.140
  (35 shorter events, 0.4 us)
Async XLA Ops:
  0.6 1.7 %copy-start = (bf16[768,1536]{1,0:T(8,128)(2,1)S(1)}, bf16[768,1536]{1,0:T(8,128)(2,1)}, u32[]{:S(2)}) copy-start(bf16[768,1536]{1,0:T(8,128)(2,1)} %param.7) | copy-start | bytes 7077892
  0.6 1.8 %copy-start.1 = (bf16[384,768]{1,0:T(8,128)(2,1)S(1)}, bf16[384,768]{1,0:T(8,128)(2,1)}, u32[]{:S(2)}) copy-start(bf16[384,768]{1,0:T(8,128)(2,1)} %attn.1) | copy-start | bytes 1769476
  2.4 3.4 %copy-start.5 = (s32[3]{0:T(128)S(1)}, s32[3]{0:T(128)}, u32[]{:S(2)}) copy-start(s32[3]{0:T(128)} %bins.1) | copy-start | bytes 40
  3.7 47.7 %copy-start.2 = (f32[3,768]{1,0:T(4,128)S(1)}, f32[3,768]{1,0:T(4,128)}, u32[]{:S(2)}) copy-start(f32[3,768]{1,0:T(4,128)} %gate.1) | copy-start | bytes 27652
  3.7 47.7 %collective-permute-start = (bf16[1152,768]{1,0:T(8,128)(2,1)}, bf16[1152,768]{1,0:T(8,128)(2,1)}, u32[]{:S(2)}, u32[]{:S(2)}) collective-permute-start(bf16[1152,768]{1,0:T(8,128)(2,1)} %pad_maximum_fusion.1), channel_id=1, source_target_pairs={{0,1},{1,0},{2,3},{3,2},{4,5},{5,4},{6,7},{7,6},{8,9},{9,8},{10,11... | collective-permute-start | bytes 5308424 | tf_op jit(solution)/shard_map/ppermute | solution.py:38
  6.5 21.6 %all-to-all-start = ((f32[32,1,128]{2,1,0:T(1,128)}), f32[32,1,128]{2,1,0:T(1,128)S(1)}, u32[]{:S(2)}, u32[]{:S(2)}) async-start(f32[32,1,128]{2,1,0:T(1,128)} %broadcast_in_dim.8), calls=%async_computation | async-start | bytes 32768 | tf_op jit(solution)/shard_map/all_to_all | solution.py:42
  28.7 22.4 %all-to-all-start.1 = ((f32[12,1,128]{2,1,0:T(1,128)}), f32[12,1,128]{2,1,0:T(1,128)S(1)}, u32[]{:S(2)}, u32[]{:S(2)}) async-start(f32[12,1,128]{2,1,0:T(1,128)} %broadcast_in_dim.9), calls=%async_computation.1 | async-start | bytes 12288 | tf_op jit(solution)/shard_map/all_to_all | solution.py:42
  51.4 1.1 copy-start.3
  52.5 1.1 copy-start.4
  53.6 1.3 %copy-start.6 = (f32[384,768]{1,0:T(8,128)S(1)}, f32[384,768]{1,0:T(8,128)}, u32[]{:S(2)}) copy-start(f32[384,768]{1,0:T(8,128)} %convolution_bitcast_fusion.part) | copy-start | bytes 3538948
  58.1 3.5 %collective-permute-start.1 = (f32[128]{0:T(128)S(1)}, f32[128]{0:T(128)S(1)}, u32[]{:S(2)}, u32[]{:S(2)}) collective-permute-start(f32[128]{0:T(128)S(1)} %bitcast.65), channel_id=1, source_target_pairs={{0,1},{1,0},{2,3},{3,2},{4,5},{5,4},{6,7},{7,6},{8,9},{9,8},{10,11... | collective-permute-start | bytes 1544 | tf_op jit(solution)/shard_map/ppermute | solution.py:38
  99.4 22.4 %all-to-all-start.3 = ((f16[24,32,128]{2,1,0:T(8,128)(2,1)}), f16[24,32,128]{2,1,0:T(8,128)(2,1)S(1)}, u32[]{:S(2)}, u32[]{:S(2)}) async-start(f16[24,32,128]{2,1,0:T(8,128)(2,1)} %pad_maximum_fusion.2), calls=%async_computation.3 | async-start | bytes 393216 | tf_op jit(solution)/shard_map/all_to_all | solution.py:42

commit v4 on v3

v4 whole, which is shorter than its diff:
```python
import math

import jax
import jax.numpy as jnp
from jax import lax
from jax.experimental import pallas as pl
from jax.experimental.pallas import tpu as pltpu
from jax.sharding import Mesh
from jax.sharding import PartitionSpec as P

NBINS = 128
X, YH, YL, ZH, ZL = "dp_x", "dp_yh", "dp_yl", "dp_zh", "dp_zl"
DP = (X, YH, YL, ZH, ZL)
NEAR = (X, YL, ZL)
FAR = (YH, ZH)
LOSS_SCALE = 4096.0
ATTN_BOUND = 6.0
TOP = 14.0
SIDE = 8
LOW = 1024.0


def weights_at(index):
    centre = (index + 0.5) / NBINS
    logit = jnp.log(centre) - jnp.log(1.0 - centre)
    return jnp.exp(-0.5 * logit * logit) / (math.sqrt(2.0 * math.pi) * centre * (1.0 - centre))


def group(axes):
    return math.prod(lax.axis_size(a) for a in axes)


def partner(x):
    return lax.ppermute(x, "mp", [(0, 1), (1, 0)])


def exchange(x, axes):
    return lax.all_to_all(x, axes, 0, 0, tiled=True)


def exponent_of(bound):
    return jnp.floor(jnp.log2(jnp.maximum(bound, 1e-30))) + 2.0


def halves(scaled):
    high = lax.reduce_precision(scaled, 5, 10)
    return high, (scaled - high) * LOW


VMEM = pl.BlockSpec(memory_space=pltpu.VMEM)
SMEM = pl.BlockSpec(memory_space=pltpu.SMEM)
HBM = pl.BlockSpec(memory_space=pltpu.HBM)


def grant(mib):
    return pltpu.CompilerParams(vmem_limit_bytes=mib * 2**20)


def bin_lanes():
    return lax.broadcasted_iota(jnp.int32, (1, NBINS), 1)


def count_kernel(bins, spread):
    lane = bin_lanes()
    found = jnp.zeros((1, NBINS), jnp.float32)
    for s in range(bins.shape[0]):
        found = found + (lane == bins[s]).astype(jnp.float32)
    spread[...] = jnp.broadcast_to(found[None], spread.shape)


def fold_kernel(got, spread):
    spread[...] = jnp.broadcast_to(jnp.sum(got[...], axis=0, keepdims=True), spread.shape)


def count_sweep(bins):
    plane, column = (X, YH, YL), (ZH, ZL)
    spread = pl.pallas_call(
        count_kernel,
        out_shape=jax.ShapeDtypeStruct((group(plane), 1, NBINS), jnp.float32),
        in_specs=[SMEM],
        out_specs=VMEM,
        name="count",
    )(bins)
    got = exchange(spread, plane)
    spread = pl.pallas_call(
        fold_kernel,
        out_shape=jax.ShapeDtypeStruct((group(column), 1, NBINS), jnp.float32),
        in_specs=[VMEM],
        out_specs=VMEM,
        compiler_params=grant(2),
        name="fold",
    )(got)
    return exchange(spread, column)


def feature_rows(block, picks):
    run = picks.shape[0]
    for n in range(block.shape[1] // run):
        yield lax.dot_general(
            picks,
            block[:, n * run : (n + 1) * run],
            (((1,), (1,)), ((), ())),
            preferred_element_type=jnp.float32,
        ).astype(jnp.bfloat16)


def row_picks(run):
    row = lax.broadcasted_iota(jnp.int32, (run, run), 0)
    piece = (row * 683) >> 16
    inner = row - 96 * piece
    quad = inner >> 2
    y_high = (quad * 43) >> 8
    z_high = quad - 6 * y_high
    source = y_high * 96 + (piece >> 1) * 48 + z_high * 8 + (piece & 1) * 4 + (inner & 3)
    return (source == lax.broadcasted_iota(jnp.int32, (run, run), 1)).astype(jnp.bfloat16)


def forward_kernel(
    me,
    bins,
    attn_hbm,
    other_hbm,
    part_hbm,
    resid_hbm,
    target_hbm,
    gate,
    error,
    features_hbm,
    error_proj,
    losses,
    grad_exp,
    grad_scale,
    attn,
    other,
    part,
    resid,
    target,
    features,
    sems,
):
    tokens, half = part.shape
    samples = gate.shape[0]
    per_sample = tokens // samples
    run = half // 2
    loads = [
        pltpu.make_async_copy(src, dst, sems.at[n])
        for n, (src, dst) in enumerate(
            (
                (attn_hbm, attn),
                (other_hbm, other),
                (part_hbm, part),
                (resid_hbm, resid),
                (target_hbm, target),
            )
        )
    ]
    for load in loads:
        load.start()
    picks = row_picks(run)
    mine = pl.multiple_of(me[0] * half, half)
    theirs = pl.multiple_of((1 - me[0]) * half, half)
    stores = []
    for first, block, load in ((mine, attn, loads[0]), (theirs, other.at[half:, :], loads[1])):
        load.wait()
        for n, moved in enumerate(feature_rows(block, picks)):
            features[pl.ds(pl.multiple_of(first + n * run, run), run), :] = moved
        rows = pl.ds(first, half)
        stores.append(pltpu.make_async_copy(features.at[rows, :], features_hbm.at[rows, :], sems.at[len(loads) + len(stores)]))
        stores[-1].start()
    for load in loads[2:]:
        load.wait()

    lane = bin_lanes()
    steepest = weights_at(lane.astype(jnp.float32)) * (LOSS_SCALE / (per_sample * half))
    found = jnp.zeros((1, NBINS), jnp.float32)
    reach = jnp.zeros((1, half), jnp.float32)
    for s in range(samples):
        rows = slice(s * per_sample, (s + 1) * per_sample)
        projected = part[rows, :] + jnp.dot(
            other[half + s * per_sample : half + (s + 1) * per_sample, :],
            other[:half, :],
            preferred_element_type=jnp.float32,
        )
        scale = gate[s : s + 1, :]
        diff = resid[rows, :].astype(jnp.float32) + scale * projected - target[rows, :].astype(jnp.float32)
        error[rows, :] = diff
        error_proj[s : s + 1, :] = jnp.sum(diff * projected, axis=0, keepdims=True)
        hit = lane == bins[s]
        largest = jnp.sum(jnp.where(hit, steepest, 0.0), axis=1, keepdims=True)
        reach = reach + largest * jnp.sum(jnp.abs(diff * scale), axis=0, keepdims=True)
        squares = jnp.sum(jnp.sum(diff * diff, axis=0, keepdims=True), axis=1, keepdims=True)
        found = found + jnp.where(hit, squares * (1.0 / (per_sample * 2 * half)), 0.0)
    losses[...] = found
    bound = exponent_of(jnp.max(reach, axis=1, keepdims=True) * (1.01 * ATTN_BOUND))
    grad_exp[...] = jnp.broadcast_to(bound, grad_exp.shape)
    grad_scale[...] = jnp.broadcast_to(jnp.exp2(TOP - bound), grad_scale.shape)
    for store in stores:
        store.wait()


def forward(me, bins, attn, other, part, resid, target, gate):
    tokens, half = part.shape
    operands = (attn, other, part, resid, target)
    return pl.pallas_call(
        forward_kernel,
        out_shape=(
            jax.ShapeDtypeStruct((tokens, half), jnp.float32),
            jax.ShapeDtypeStruct((2 * half, tokens), jnp.bfloat16),
            jax.ShapeDtypeStruct(gate.shape, jnp.float32),
            jax.ShapeDtypeStruct((1, NBINS), jnp.float32),
            jax.ShapeDtypeStruct((1, NBINS), jnp.float32),
            jax.ShapeDtypeStruct((1, half), jnp.float32),
        ),
        in_specs=[SMEM] * 2 + [HBM] * 5 + [VMEM],
        out_specs=(VMEM, HBM, VMEM, VMEM, VMEM, VMEM),
        scratch_shapes=[
            *(pltpu.VMEM(x.shape, x.dtype) for x in operands),
            pltpu.VMEM((2 * half, tokens), jnp.bfloat16),
            pltpu.SemaphoreType.DMA((len(operands) + 2,)),
        ],
        cost_estimate=pl.CostEstimate(flops=10**9, bytes_accessed=6 * 10**6, transcendentals=0),
        name="forward",
    )(me, bins, *operands, gate)


def scale_kernel(
    bins, got, losses, other_losses, grad_exp, error, gate, d_proj, steepness, per_count, side
):
    tokens, half = error.shape
    samples = gate.shape[0]
    per_sample = tokens // samples
    lane = bin_lanes()
    floored = jnp.maximum(jnp.sum(got[...], axis=0), 1.0)
    slope = weights_at(lane.astype(jnp.float32)) / floored
    per_count[...] = slope
    for s in range(samples):
        rows = slice(s * per_sample, (s + 1) * per_sample)
        coefficient = jnp.sum(jnp.where(lane == bins[s], slope * LOSS_SCALE, 0.0), axis=1, keepdims=True)
        coefficient = coefficient * (1.0 / (per_sample * half))
        d_proj[rows, :] = (coefficient * error[rows, :] * gate[s : s + 1, :]).astype(jnp.bfloat16)
        steepness[s : s + 1, :] = jnp.broadcast_to(coefficient, (1, NBINS))
    total = losses[...] + other_losses[...]
    loss_exp = exponent_of(total)
    high, low = halves(total * jnp.exp2(TOP - loss_exp))
    side[...] = jnp.zeros(side.shape, jnp.float32)
    for n, row in enumerate((high, low, grad_exp[...], loss_exp)):
        side[n : n + 1, :NBINS] = row


def scaled(bins, got, losses, other_losses, grad_exp, error, gate):
    return pl.pallas_call(
        scale_kernel,
        out_shape=(
            jax.ShapeDtypeStruct(error.shape, jnp.bfloat16),
            jax.ShapeDtypeStruct((gate.shape[0], NBINS), jnp.float32),
            jax.ShapeDtypeStruct((1, NBINS), jnp.float32),
            jax.ShapeDtypeStruct((SIDE, gate.shape[1]), jnp.float32),
        ),
        in_specs=[SMEM] + [VMEM] * 6,
        out_specs=(VMEM,) * 4,
        cost_estimate=pl.CostEstimate(flops=10**7, bytes_accessed=2 * 10**6, transcendentals=0),
        compiler_params=grant(20),
        name="scaled",
    )(bins, got, losses, other_losses, grad_exp, error, gate)


def body(attn, w_out, resid, target, gate, bins):
    own_cols = resid.shape[1]
    me = lax.axis_index("mp")
    got = count_sweep(bins)
    w_mine = lax.dynamic_slice_in_dim(w_out, me * own_cols, own_cols, axis=1)
    w_theirs = lax.dynamic_slice_in_dim(w_out, (1 - me) * own_cols, own_cols, axis=1)
    other = partner(jnp.concatenate([w_theirs, attn], axis=0))
    part = jnp.dot(attn, w_mine, preferred_element_type=jnp.float32)
    error, features, error_proj, losses, grad_exp, grad_scale = forward(
        me.reshape(1), bins, attn, other, part, resid, target, gate
    )
    other_losses = partner(losses)
    near, far = group(NEAR), group(FAR)
    d_proj, steepness, per_count, side = scaled(bins, got, losses, other_losses, grad_exp, error, gate)
    side = side.astype(jnp.float16)
    partial = jnp.dot(features, d_proj, preferred_element_type=jnp.float32)
    partial = (partial * grad_scale).astype(jnp.float16).reshape(near, -1, own_cols)
    keep = partial.shape[1]
    partial = jnp.concatenate([partial, jnp.broadcast_to(side[None], (near, *side.shape))], axis=1)
    got = exchange(partial, NEAR)

    sides = got[:, keep : keep + 4, :NBINS].astype(jnp.float32)
    grad_exp = jnp.max(sides[:, 2], axis=0) + math.log2(near)
    scale = jnp.tile(jnp.exp2(sides[:, 2] - grad_exp), (1, own_cols // NBINS))
    total = jnp.sum(got[:, :keep].astype(jnp.float32) * scale[:, None, :], axis=0)
    loss_exp = jnp.max(sides[:, 3], axis=0) + math.log2(near)
    high, low = halves(
        jnp.sum((sides[:, 0] + sides[:, 1] * (1.0 / LOW)) * jnp.exp2(sides[:, 3] - loss_exp), axis=0)
    )
    side = jnp.stack([high, low, grad_exp, loss_exp])
    side = jnp.pad(side, ((0, SIDE - 4), (0, 0))).astype(jnp.float16)
    rows = total.astype(jnp.float16).reshape(far, -1, NBINS)
    keep = rows.shape[1]
    rows = jnp.concatenate([rows, jnp.broadcast_to(side[None], (far, *side.shape))], axis=1)
    got = exchange(rows, FAR).astype(jnp.float32)

    sides = got[:, keep : keep + 4]
    total = jnp.sum(got[:, :keep] * jnp.exp2(sides[:, 2:3] - TOP), axis=0)
    losses = jnp.sum((sides[:, 0] + sides[:, 1] * (1.0 / LOW)) * jnp.exp2(sides[:, 3] - TOP), axis=0)
    return (total.reshape(-1, own_cols), steepness[:, :1] * error_proj, per_count[0] * losses)


def solution(mesh):
    finer = Mesh(mesh.devices.reshape(4, 4, 2, 6, 2, mesh.shape["mp"]), (*DP, "mp"))
    placed = (P(DP, "mp"), P("mp", None), P(DP, "mp"), P(DP, "mp"), P(DP, "mp"), P(DP))
    return jax.shard_map(
        body,
        mesh=finer,
        in_specs=placed,
        out_specs=(P(DP, "mp"), P(DP, "mp"), P()),
        check_vma=False,
    )
```

time: 124 us -> 124 us (level)
  waiting for transfers between devices: 34.8 us -> 26.4 us
  starting transfers between devices: 33.3 us -> 38.9 us
  Pallas kernels: 3.27 us -> 7.8 us
  local copies, waits for them, and re-layouts: 7.27 us -> 5.18 us
  matrix products: 3.03 us -> 4.32 us
    all_to_all x3, waiting for transfers between devices: 34.8 us -> 26.4 us  [exchange(): return lax.all_to_all(x, axes, 0, 0, tiled=True)]
    all_to_all x3, starting transfers between devices: 29.3 us -> 35.1 us  [exchange(): return lax.all_to_all(x, axes, 0, 0, tiled=True)]
    pallas_call x0 -> x3, Pallas kernels: none -> 2.72 us  [the longest x1 1.28 us: count_sweep(): pl.pallas_call(count_kernel, out_shape=jax.ShapeDtypeStruct((group(plane)...]
    pallas_call x1, Pallas kernels: 3.27 us -> 5.09 us  [forward(): pl.pallas_call(forward_kernel, out_shape=(jax.ShapeDtypeStruct((tokens, h...]
    dot_general x1, matrix products: 1.39 us -> 2.66 us  [body(): partial = jnp.dot(features, d_proj, preferred_element_type=jnp.float32)]
    unnamed x15 -> x17, local copies, waits for them, and re-layouts: 5.1 us -> 4.18 us
  transfers between devices with their start and end apart: 5 -> 5, of which waited for: 3 -> 3; matrix products, arithmetic and copies ran while one was open for 4% -> 3% of each run, Pallas kernels for 0% -> 6%
where the time goes in v4:
time: 124 us; the launch traced here: 123 us
  starting transfers between devices  38.9 us (31%)
  blocking collectives  34.6 us (28%)
  waiting for transfers between devices  26.4 us (21%)
  Pallas kernels  7.8 us (6%)
  other arithmetic  5.28 us (4%)
  local copies, waits for them, and re-layouts  5.18 us (4%)
  matrix products  4.32 us (3%)
    all_to_all x3, starting transfers between devices, exchange(): return lax.all_to_all(x, axes, 0, 0, tiled=True)  35.1 us
    all_to_all x1, blocking collectives, exchange(): return lax.all_to_all(x, axes, 0, 0, tiled=True)  34.6 us
    all_to_all x3, waiting for transfers between devices, exchange(): return lax.all_to_all(x, axes, 0, 0, tiled=True)  26.4 us
    pallas_call x1, Pallas kernels, forward(): pl.pallas_call(forward_kernel, out_shape=(jax.ShapeDtypeStruct((tokens, h...  5.09 us
    unnamed x17, local copies, waits for them, and re-layouts  4.18 us
    ppermute x2, starting transfers between devices, partner(): return lax.ppermute(x, 'mp', [(0, 1), (1, 0)])  3.83 us
    dot_general x1, matrix products, body(): partial = jnp.dot(features, d_proj, preferred_element_type=jnp.float32)  2.66 us
  transfers between devices with their start and end apart: 5, of which 3 were waited for; matrix products, arithmetic and copies ran while one was open for 3% of the time, Pallas kernels for 6%

profile of v4, /device:TPU:8, one launch (start us, length us, event | category | flops | bytes accessed | tf_op | source)
XLA Modules:
  0.0 123.3 jit_solution(17456423588346483896)
XLA Ops:
  0.7 1.6 %copy-done = bf16[768,1536]{1,0:T(8,128)(2,1)S(1)} copy-done((bf16[768,1536]{1,0:T(8,128)(2,1)S(1)}, bf16[768,1536]{1,0:T(8,128)(2,1)}, u32[]{:S(2)}) %copy-start) | copy-done | bytes 2359320
  2.3 0.1 constant_dynamic-slice_fusion
  2.4 0.0 copy-done.6
  2.4 1.3 %pad_maximum_fusion.1 = bf16[1152,768]{1,0:T(8,128)(2,1)} fusion(bf16[384,768]{1,0:T(8,128)(2,1)S(1)} %copy-done.6, bf16[768,768]{1,0:T(8,128)(2,1)S(1)} %constant_dynamic-slice_fusion), kind=kLoop, calls=%fused_computation.3 | loop fusion | flops 3538944 | bytes 3538944 | tf_op jit(solution)/shard_map/concatenate | solution.py:273
  3.7 1.9 %collective-permute-start = (bf16[1152,768]{1,0:T(8,128)(2,1)}, bf16[1152,768]{1,0:T(8,128)(2,1)}, u32[]{:S(2)}, u32[]{:S(2)}) collective-permute-start(bf16[1152,768]{1,0:T(8,128)(2,1)} %pad_maximum_fusion.1), channel_id=1, source_target_pairs={{0,1},{1,0},{2,3},{3,2},{4,5},{5,4},{6,7},{7,6},{8,9},{9,8},{10,11... | collective-permute-start | bytes 5308424 | tf_op jit(solution)/shard_map/ppermute | solution.py:34
  5.7 1.3 %count.1 = f32[32,1,128]{2,1,0:T(1,128)} custom-call(s32[3]{0:T(128)} %bins.5), custom_call_target="tpu_custom_call" | custom-call | tf_op jit(solution)/shard_map/count/pallas_call | solution.py:77
  6.9 12.8 %all-to-all-start = ((f32[32,1,128]{2,1,0:T(1,128)}), f32[32,1,128]{2,1,0:T(1,128)S(1)}, u32[]{:S(2)}, u32[]{:S(2)}) async-start(f32[32,1,128]{2,1,0:T(1,128)} %count.1), calls=%async_computation | async-start | bytes 32768 | tf_op jit(solution)/shard_map/all_to_all | solution.py:38
  19.8 1.7 %convolution_bitcast_fusion.part_hbm = f32[384,768]{1,0:T(8,128)} fusion(bf16[384,768]{1,0:T(8,128)(2,1)S(1)} %copy-done.6, bf16[768,1536]{1,0:T(8,128)(2,1)S(1)} %copy-done, s32[]{:T(128)S(6)} %select_n.7), kind=kOutput, calls=%fused_computation.4 | convolution fusion | flops 452984832 | bytes 2949124 | tf_op jit(solution)/shard_map/dot_general | solution.py:274
  21.4 7.1 %all-to-all-done.got = f32[32,1,128]{2,1,0:T(1,128)S(1)} async-done(((f32[32,1,128]{2,1,0:T(1,128)}), f32[32,1,128]{2,1,0:T(1,128)S(1)}, u32[]{:S(2)}, u32[]{:S(2)}) %all-to-all-start) | async-done | bytes 16416 | tf_op jit(solution)/shard_map/all_to_all | solution.py:38
  28.5 0.6 fold.1
  29.2 12.4 %all-to-all-start.1 = ((f32[12,1,128]{2,1,0:T(1,128)}), f32[12,1,128]{2,1,0:T(1,128)S(1)}, u32[]{:S(2)}, u32[]{:S(2)}) async-start(f32[12,1,128]{2,1,0:T(1,128)} %fold.1), calls=%async_computation.1 | async-start | bytes 12288 | tf_op jit(solution)/shard_map/all_to_all | solution.py:38
  41.6 5.1 %forward.1 = (f32[384,768]{1,0:T(8,128)}, bf16[1536,384]{1,0:T(8,128)(2,1)}, f32[3,768]{1,0:T(4,128)}, f32[1,128]{1,0:T(1,128)}, f32[1,128]{1,0:T(1,128)}, /*index=5*/f32[1,768]{1,0:T(1,128)}) custom-call(s32[1]{0:T(128)} %bitcast.me, s32[3]{0:T(128)} %bins.5, bf16[384,768]{1,0:T(8,128)(2,1)} %attn_hbm.1, bf16[1152,768]{1,0:T(8,128)(2,1)} %collective-permute-done.other_hbm, ...), custom_call_target="tpu_custom_call" | custom-call | flops 1000000000 | bytes 6000000 | tf_op jit(solution)/shard_map/forward/pallas_call | solution.py:204
  46.7 1.9 %collective-permute-start.1 = (f32[1,128]{1,0:T(1,128)}, f32[1,128]{1,0:T(1,128)S(1)}, u32[]{:S(2)}, u32[]{:S(2)}) collective-permute-start(f32[1,128]{1,0:T(1,128)} %get-tuple-element.14.losses), channel_id=1, source_target_pairs={{0,1},{1,0},{2,3},{3,2},{4,5},{5,4},{6,7},{7,6},{8,9},{9,8},{10,11... | collective-permute-start | bytes 1544 | tf_op jit(solution)/shard_map/ppermute | solution.py:34
  48.6 0.7 reduce.3
  49.3 2.3 %all-to-all-done.1.got = f32[12,1,128]{2,1,0:T(1,128)S(1)} async-done(((f32[12,1,128]{2,1,0:T(1,128)}), f32[12,1,128]{2,1,0:T(1,128)S(1)}, u32[]{:S(2)}, u32[]{:S(2)}) %all-to-all-start.1) | async-done | bytes 6176 | tf_op jit(solution)/shard_map/all_to_all | solution.py:38
  51.6 1.3 %copy-done.1 = f32[384,768]{1,0:T(8,128)S(1)} copy-done((f32[384,768]{1,0:T(8,128)S(1)}, f32[384,768]{1,0:T(8,128)}, u32[]{:S(2)}) %copy-start.1) | copy-done | bytes 1179672
  52.9 0.6 copy-done.4
  53.5 0.6 copy-done.5
  54.1 0.8 scaled.1
  54.9 2.7 %multiply_convert_fusion = f16[1536,768]{1,0:T(8,128)(2,1)S(1)} fusion(bf16[1536,384]{1,0:T(8,128)(2,1)} %get-tuple-element.13, bf16[384,768]{1,0:T(8,128)(2,1)S(1)} %get-tuple-element.17, f32[768]{0:T(1024)S(1)} %reduce.3), kind=kOutput, calls=%fused_computation.1 | convolution fusion | flops 908328960 | bytes 4131840 | tf_op jit(solution)/shard_map/dot_general | solution.py:282
  57.6 0.6 pad_maximum_fusion
  58.3 34.6 %all_to_all.20 = f16[16,104,768]{2,1,0:T(8,128)(2,1)S(1)} all-to-all(f16[16,104,768]{2,1,0:T(8,128)(2,1)S(1)} %pad_maximum_fusion), channel_id=1, replica_groups=mesh['dp_x'=4,'dp_yh'=4,'dp_yl'=2,'dp_zh'=6,'dp_zl'=2,'mp'=2] {'dp_x','d..., dimensions={0} | all-to-all | bytes 5111808 | tf_op jit(solution)/shard_map/all_to_all | solution.py:38
  92.9 0.5 multiply_reduce_fusion
  93.4 0.2 convert_element_type.30
  93.7 0.7 pad_maximum_fusion.2
  94.4 9.9 %all-to-all-start.3 = ((f16[24,32,128]{2,1,0:T(8,128)(2,1)}), f16[24,32,128]{2,1,0:T(8,128)(2,1)S(1)}, u32[]{:S(2)}, u32[]{:S(2)}) async-start(f16[24,32,128]{2,1,0:T(8,128)(2,1)} %pad_maximum_fusion.2), calls=%async_computation.3 | async-start | bytes 393216 | tf_op jit(solution)/shard_map/all_to_all | solution.py:38
  104.3 0.1 slice_reduce_fusion.2
  104.4 0.7 broadcast_multiply_fusion
  105.0 17.0 %all-to-all-done.3 = f16[24,32,128]{2,1,0:T(8,128)(2,1)S(1)} async-done(((f16[24,32,128]{2,1,0:T(8,128)(2,1)}), f16[24,32,128]{2,1,0:T(8,128)(2,1)S(1)}, u32[]{:S(2)}, u32[]{:S(2)}) %all-to-all-start.3) | async-done | bytes 196640 | tf_op jit(solution)/shard_map/all_to_all | solution.py:38
  122.1 0.1 copy_convert_fusion
  122.2 0.6 reshape.97
  122.8 0.5 bitcast_multiply_fusion
  (28 shorter events, 0.3 us)
Async XLA Ops:
  0.6 1.7 %copy-start = (bf16[768,1536]{1,0:T(8,128)(2,1)S(1)}, bf16[768,1536]{1,0:T(8,128)(2,1)}, u32[]{:S(2)}) copy-start(bf16[768,1536]{1,0:T(8,128)(2,1)} %param.7) | copy-start | bytes 7077892
  0.6 1.8 %copy-start.6 = (bf16[384,768]{1,0:T(8,128)(2,1)S(1)}, bf16[384,768]{1,0:T(8,128)(2,1)}, u32[]{:S(2)}) copy-start(bf16[384,768]{1,0:T(8,128)(2,1)} %attn_hbm.1) | copy-start | bytes 1769476
  3.7 37.8 %collective-permute-start = (bf16[1152,768]{1,0:T(8,128)(2,1)}, bf16[1152,768]{1,0:T(8,128)(2,1)}, u32[]{:S(2)}, u32[]{:S(2)}) collective-permute-start(bf16[1152,768]{1,0:T(8,128)(2,1)} %pad_maximum_fusion.1), channel_id=1, source_target_pairs={{0,1},{1,0},{2,3},{3,2},{4,5},{5,4},{6,7},{7,6},{8,9},{9,8},{10,11... | collective-permute-start | bytes 5308424 | tf_op jit(solution)/shard_map/ppermute | solution.py:34
  6.9 21.6 %all-to-all-start = ((f32[32,1,128]{2,1,0:T(1,128)}), f32[32,1,128]{2,1,0:T(1,128)S(1)}, u32[]{:S(2)}, u32[]{:S(2)}) async-start(f32[32,1,128]{2,1,0:T(1,128)} %count.1), calls=%async_computation | async-start | bytes 32768 | tf_op jit(solution)/shard_map/all_to_all | solution.py:38
  29.2 22.4 %all-to-all-start.1 = ((f32[12,1,128]{2,1,0:T(1,128)}), f32[12,1,128]{2,1,0:T(1,128)S(1)}, u32[]{:S(2)}, u32[]{:S(2)}) async-start(f32[12,1,128]{2,1,0:T(1,128)} %fold.1), calls=%async_computation.1 | async-start | bytes 12288 | tf_op jit(solution)/shard_map/all_to_all | solution.py:38
  41.6 10.0 %copy-start.2 = (f32[3,768]{1,0:T(4,128)S(1)}, f32[3,768]{1,0:T(4,128)}, u32[]{:S(2)}) copy-start(f32[3,768]{1,0:T(4,128)} %gate.3) | copy-start | bytes 27652
  41.6 10.0 %copy-start.3 = (s32[3]{0:T(128)S(1)}, s32[3]{0:T(128)}, u32[]{:S(2)}) copy-start(s32[3]{0:T(128)} %bins.5) | copy-start | bytes 40
  46.7 4.9 %collective-permute-start.1 = (f32[1,128]{1,0:T(1,128)}, f32[1,128]{1,0:T(1,128)S(1)}, u32[]{:S(2)}, u32[]{:S(2)}) collective-permute-start(f32[1,128]{1,0:T(1,128)} %get-tuple-element.14.losses), channel_id=1, source_target_pairs={{0,1},{1,0},{2,3},{3,2},{4,5},{5,4},{6,7},{7,6},{8,9},{9,8},{10,11... | collective-permute-start | bytes 1544 | tf_op jit(solution)/shard_map/ppermute | solution.py:34
  51.6 1.3 %copy-start.1 = (f32[384,768]{1,0:T(8,128)S(1)}, f32[384,768]{1,0:T(8,128)}, u32[]{:S(2)}) copy-start(f32[384,768]{1,0:T(8,128)} %get-tuple-element.16.error) | copy-start | bytes 3538948
  52.9 0.6 copy-start.4
  53.5 0.6 copy-start.5
  92.8 11.6 %copy-start.7 = (f32[3,768]{1,0:T(4,128)S(1)}, f32[3,768]{1,0:T(4,128)}, u32[]{:S(2)}) copy-start(f32[3,768]{1,0:T(4,128)} %get-tuple-element.21) | copy-start | bytes 27652
  94.4 27.7 %all-to-all-start.3 = ((f16[24,32,128]{2,1,0:T(8,128)(2,1)}), f16[24,32,128]{2,1,0:T(8,128)(2,1)S(1)}, u32[]{:S(2)}, u32[]{:S(2)}) async-start(f16[24,32,128]{2,1,0:T(8,128)(2,1)} %pad_maximum_fusion.2), calls=%async_computation.3 | async-start | bytes 393216 | tf_op jit(solution)/shard_map/all_to_all | solution.py:38

commit v5 on v4

--- a/solution.py
+++ b/solution.py
@@ -127,9 +127,7 @@
     error,
     features_hbm,
     error_proj,
-    losses,
-    grad_exp,
-    grad_scale,
+    marks,
     attn,
     other,
     part,
@@ -190,10 +188,9 @@
         reach = reach + largest * jnp.sum(jnp.abs(diff * scale), axis=0, keepdims=True)
         squares = jnp.sum(jnp.sum(diff * diff, axis=0, keepdims=True), axis=1, keepdims=True)
         found = found + jnp.where(hit, squares * (1.0 / (per_sample * 2 * half)), 0.0)
-    losses[...] = found
     bound = exponent_of(jnp.max(reach, axis=1, keepdims=True) * (1.01 * ATTN_BOUND))
-    grad_exp[...] = jnp.broadcast_to(bound, grad_exp.shape)
-    grad_scale[...] = jnp.broadcast_to(jnp.exp2(TOP - bound), grad_scale.shape)
+    marks[...] = jnp.broadcast_to(bound, marks.shape)
+    marks[:1, :] = found
     for store in stores:
         store.wait()
 
@@ -207,12 +204,10 @@
             jax.ShapeDtypeStruct((tokens, half), jnp.float32),
             jax.ShapeDtypeStruct((2 * half, tokens), jnp.bfloat16),
             jax.ShapeDtypeStruct(gate.shape, jnp.float32),
-            jax.ShapeDtypeStruct((1, NBINS), jnp.float32),
-            jax.ShapeDtypeStruct((1, NBINS), jnp.float32),
-            jax.ShapeDtypeStruct((1, half), jnp.float32),
+            jax.ShapeDtypeStruct((SIDE, NBINS), jnp.float32),
         ),
         in_specs=[SMEM] * 2 + [HBM] * 5 + [VMEM],
-        out_specs=(VMEM, HBM, VMEM, VMEM, VMEM, VMEM),
+        out_specs=(VMEM, HBM, VMEM, VMEM),
         scratch_shapes=[
             *(pltpu.VMEM(x.shape, x.dtype) for x in operands),
             pltpu.VMEM((2 * half, tokens), jnp.bfloat16),
@@ -224,44 +219,82 @@
 
 
 def scale_kernel(
-    bins, got, losses, other_losses, grad_exp, error, gate, d_proj, steepness, per_count, side
+    bins,
+    got_hbm,
+    marks_hbm,
+    other_hbm,
+    gate_hbm,
+    error_proj_hbm,
+    error_hbm,
+    d_proj,
+    grad_gate,
+    per_count,
+    side,
+    got,
+    marks,
+    other,
+    gate,
+    error_proj,
+    error,
+    sems,
 ):
     tokens, half = error.shape
     samples = gate.shape[0]
     per_sample = tokens // samples
+    sample_rows = [slice(s * per_sample, (s + 1) * per_sample) for s in range(samples)]
+    pairs = [(got_hbm, got), (marks_hbm, marks), (other_hbm, other), (gate_hbm, gate)]
+    pairs += [(error_hbm.at[rows, :], error.at[rows, :]) for rows in sample_rows]
+    pairs += [(error_proj_hbm, error_proj)]
+    loads = [pltpu.make_async_copy(src, dst, sems.at[n]) for n, (src, dst) in enumerate(pairs)]
+    for load in loads:
+        load.start()
     lane = bin_lanes()
-    floored = jnp.maximum(jnp.sum(got[...], axis=0), 1.0)
-    slope = weights_at(lane.astype(jnp.float32)) / floored
+    weights = weights_at(lane.astype(jnp.float32))
+    side[...] = jnp.zeros(side.shape, jnp.float32)
+    for load in loads[:4]:
+        load.wait()
+    slope = weights / jnp.maximum(jnp.sum(got[...], axis=0), 1.0)
     per_count[...] = slope
-    for s in range(samples):
-        rows = slice(s * per_sample, (s + 1) * per_sample)
-        coefficient = jnp.sum(jnp.where(lane == bins[s], slope * LOSS_SCALE, 0.0), axis=1, keepdims=True)
-        coefficient = coefficient * (1.0 / (per_sample * half))
-        d_proj[rows, :] = (coefficient * error[rows, :] * gate[s : s + 1, :]).astype(jnp.bfloat16)
-        steepness[s : s + 1, :] = jnp.broadcast_to(coefficient, (1, NBINS))
-    total = losses[...] + other_losses[...]
+    grad_exp = marks[1:2, :]
+    lift = jnp.exp2(TOP - grad_exp[:, :1])
+    coefficients = [
+        jnp.sum(jnp.where(lane == bins[s], slope * LOSS_SCALE, 0.0), axis=1, keepdims=True)
+        * (1.0 / (per_sample * half))
+        for s in range(samples)
+    ]
+    total = marks[:1, :] + other[:1, :]
     loss_exp = exponent_of(total)
     high, low = halves(total * jnp.exp2(TOP - loss_exp))
-    side[...] = jnp.zeros(side.shape, jnp.float32)
-    for n, row in enumerate((high, low, grad_exp[...], loss_exp)):
+    for n, row in enumerate((high, low, grad_exp, loss_exp)):
         side[n : n + 1, :NBINS] = row
-
-
-def scaled(bins, got, losses, other_losses, grad_exp, error, gate):
+    for s, rows in enumerate(sample_rows):
+        loads[4 + s].wait()
+        rounded = (coefficients[s] * error[rows, :] * gate[s : s + 1, :]).astype(jnp.bfloat16)
+        d_proj[rows, :] = (rounded.astype(jnp.float32) * lift).astype(jnp.bfloat16)
+    loads[-1].wait()
+    for s in range(samples):
+        grad_gate[s : s + 1, :] = coefficients[s] * error_proj[s : s + 1, :]
+
+
+def scaled(bins, got, marks, other_marks, gate, error_proj, error):
+    operands = (got, marks, other_marks, gate, error_proj, error)
     return pl.pallas_call(
         scale_kernel,
         out_shape=(
             jax.ShapeDtypeStruct(error.shape, jnp.bfloat16),
-            jax.ShapeDtypeStruct((gate.shape[0], NBINS), jnp.float32),
+            jax.ShapeDtypeStruct(gate.shape, jnp.float32),
             jax.ShapeDtypeStruct((1, NBINS), jnp.float32),
             jax.ShapeDtypeStruct((SIDE, gate.shape[1]), jnp.float32),
         ),
-        in_specs=[SMEM] + [VMEM] * 6,
+        in_specs=[SMEM] + [HBM] * 6,
         out_specs=(VMEM,) * 4,
+        scratch_shapes=[
+            *(pltpu.VMEM(x.shape, x.dtype) for x in operands),
+            pltpu.SemaphoreType.DMA((len(operands) - 1 + gate.shape[0],)),
+        ],
         cost_estimate=pl.CostEstimate(flops=10**7, bytes_accessed=2 * 10**6, transcendentals=0),
-        compiler_params=grant(20),
         name="scaled",
-    )(bins, got, losses, other_losses, grad_exp, error, gate)
+    )(bins, *operands)
 
 
 def body(attn, w_out, resid, target, gate, bins):
@@ -272,15 +305,13 @@
     w_theirs = lax.dynamic_slice_in_dim(w_out, (1 - me) * own_cols, own_cols, axis=1)
     other = partner(jnp.concatenate([w_theirs, attn], axis=0))
     part = jnp.dot(attn, w_mine, preferred_element_type=jnp.float32)
-    error, features, error_proj, losses, grad_exp, grad_scale = forward(
-        me.reshape(1), bins, attn, other, part, resid, target, gate
-    )
-    other_losses = partner(losses)
+    error, features, error_proj, marks = forward(me.reshape(1), bins, attn, other, part, resid, target, gate)
+    other_marks = partner(marks)
     near, far = group(NEAR), group(FAR)
-    d_proj, steepness, per_count, side = scaled(bins, got, losses, other_losses, grad_exp, error, gate)
+    d_proj, grad_gate, per_count, side = scaled(bins, got, marks, other_marks, gate, error_proj, error)
     side = side.astype(jnp.float16)
     partial = jnp.dot(features, d_proj, preferred_element_type=jnp.float32)
-    partial = (partial * grad_scale).astype(jnp.float16).reshape(near, -1, own_cols)
+    partial = partial.astype(jnp.float16).reshape(near, -1, own_cols)
     keep = partial.shape[1]
     partial = jnp.concatenate([partial, jnp.broadcast_to(side[None], (near, *side.shape))], axis=1)
     got = exchange(partial, NEAR)
@@ -303,7 +334,7 @@
     sides = got[:, keep : keep + 4]
     total = jnp.sum(got[:, :keep] * jnp.exp2(sides[:, 2:3] - TOP), axis=0)
     losses = jnp.sum((sides[:, 0] + sides[:, 1] * (1.0 / LOW)) * jnp.exp2(sides[:, 3] - TOP), axis=0)
-    return (total.reshape(-1, own_cols), steepness[:, :1] * error_proj, per_count[0] * losses)
+    return (total.reshape(-1, own_cols), grad_gate, per_count[0] * losses)
 
 
 def solution(mesh):

time: 124 us -> 124 us (level)
  blocking collectives: 34.6 us -> 62 us
  waiting for transfers between devices: 26.4 us -> 10.2 us
  starting transfers between devices: 38.9 us -> 29 us
  local copies, waits for them, and re-layouts: 5.18 us -> 3.17 us
  Pallas kernels: 7.8 us -> 9.8 us
  other arithmetic: 5.28 us -> 3.97 us
    all_to_all x1 -> x2, blocking collectives: 34.6 us -> 62 us  [exchange(): return lax.all_to_all(x, axes, 0, 0, tiled=True)]
    all_to_all x3 -> x2, waiting for transfers between devices: 26.4 us -> 10.2 us  [exchange(): return lax.all_to_all(x, axes, 0, 0, tiled=True)]
    all_to_all x3 -> x2, starting transfers between devices: 35.1 us -> 25.2 us  [exchange(): return lax.all_to_all(x, axes, 0, 0, tiled=True)]
    pallas_call x1, Pallas kernels: 0.81 us -> 2.89 us  [scaled(): pl.pallas_call(scale_kernel, out_shape=(jax.ShapeDtypeStruct(error.shape,...]
    unnamed x17 -> x11, local copies, waits for them, and re-layouts: 4.18 us -> 2.29 us
  transfers between devices with their start and end apart: 5 -> 4, of which waited for: 3 -> 2; matrix products, arithmetic and copies ran while one was open for 3% -> 1% of each run, Pallas kernels for 6% -> 6%
where the time goes in v5:
time: 124 us; the launch traced here: 123 us
  blocking collectives  62 us (50%)
  starting transfers between devices  29 us (23%)
  waiting for transfers between devices  10.2 us (8%)
  Pallas kernels  9.8 us (8%)
  matrix products  4.45 us (4%)
  other arithmetic  3.97 us (3%)
  local copies, waits for them, and re-layouts  3.17 us (3%)
    all_to_all x2, blocking collectives, exchange(): return lax.all_to_all(x, axes, 0, 0, tiled=True)  62 us
    all_to_all x2, starting transfers between devices, exchange(): return lax.all_to_all(x, axes, 0, 0, tiled=True)  25.2 us
    all_to_all x2, waiting for transfers between devices, exchange(): return lax.all_to_all(x, axes, 0, 0, tiled=True)  10.2 us
    pallas_call x1, Pallas kernels, forward(): pl.pallas_call(forward_kernel, out_shape=(jax.ShapeDtypeStruct((tokens, h...  5 us
    ppermute x2, starting transfers between devices, partner(): return lax.ppermute(x, 'mp', [(0, 1), (1, 0)])  3.83 us
    pallas_call x1, Pallas kernels, scaled(): pl.pallas_call(scale_kernel, out_shape=(jax.ShapeDtypeStruct(error.shape,...  2.89 us
    dot_general x1, matrix products, body(): partial = jnp.dot(features, d_proj, preferred_element_type=jnp.float32)  2.8 us
  transfers between devices with their start and end apart: 4, of which 2 were waited for; matrix products, arithmetic and copies ran while one was open for 1% of the time, Pallas kernels for 6%

profile of v5, /device:TPU:8, one launch (start us, length us, event | category | flops | bytes accessed | tf_op | source)
XLA Modules:
  0.0 123.4 jit_solution(9963929234073435283)
XLA Ops:
  0.6 0.0 copy-start
  0.6 0.0 copy-start.1
  0.7 1.6 %copy-done = bf16[768,1536]{1,0:T(8,128)(2,1)S(1)} copy-done((bf16[768,1536]{1,0:T(8,128)(2,1)S(1)}, bf16[768,1536]{1,0:T(8,128)(2,1)}, u32[]{:S(2)}) %copy-start) | copy-done | bytes 2359320
  2.3 0.1 constant_dynamic-slice_fusion
  2.4 0.0 copy-done.1
  2.4 1.3 %pad_maximum_fusion.1 = bf16[1152,768]{1,0:T(8,128)(2,1)} fusion(bf16[384,768]{1,0:T(8,128)(2,1)S(1)} %copy-done.1, bf16[768,768]{1,0:T(8,128)(2,1)S(1)} %constant_dynamic-slice_fusion), kind=kLoop, calls=%fused_computation.3 | loop fusion | flops 3538944 | bytes 3538944 | tf_op jit(solution)/shard_map/concatenate | solution.py:306
  3.7 1.9 %collective-permute-start = (bf16[1152,768]{1,0:T(8,128)(2,1)}, bf16[1152,768]{1,0:T(8,128)(2,1)}, u32[]{:S(2)}, u32[]{:S(2)}) collective-permute-start(bf16[1152,768]{1,0:T(8,128)(2,1)} %pad_maximum_fusion.1), channel_id=1, source_target_pairs={{0,1},{1,0},{2,3},{3,2},{4,5},{5,4},{6,7},{7,6},{8,9},{9,8},{10,11... | collective-permute-start | bytes 5308424 | tf_op jit(solution)/shard_map/ppermute | solution.py:34
  5.7 1.3 %count.1 = f32[32,1,128]{2,1,0:T(1,128)} custom-call(s32[3]{0:T(128)} %bins.5), custom_call_target="tpu_custom_call" | custom-call | tf_op jit(solution)/shard_map/count/pallas_call | solution.py:77
  6.9 12.8 %all-to-all-start = ((f32[32,1,128]{2,1,0:T(1,128)}), f32[32,1,128]{2,1,0:T(1,128)S(1)}, u32[]{:S(2)}, u32[]{:S(2)}) async-start(f32[32,1,128]{2,1,0:T(1,128)} %count.1), calls=%async_computation | async-start | bytes 32768 | tf_op jit(solution)/shard_map/all_to_all | solution.py:38
  19.8 1.7 %convolution_bitcast_fusion.part_hbm = f32[384,768]{1,0:T(8,128)} fusion(bf16[384,768]{1,0:T(8,128)(2,1)S(1)} %copy-done.1, bf16[768,1536]{1,0:T(8,128)(2,1)S(1)} %copy-done, s32[]{:T(128)S(6)} %select_n.7), kind=kOutput, calls=%fused_computation.4 | convolution fusion | flops 452984832 | bytes 2949124 | tf_op jit(solution)/shard_map/dot_general | solution.py:307
  21.4 7.1 %all-to-all-done.got = f32[32,1,128]{2,1,0:T(1,128)S(1)} async-done(((f32[32,1,128]{2,1,0:T(1,128)}), f32[32,1,128]{2,1,0:T(1,128)S(1)}, u32[]{:S(2)}, u32[]{:S(2)}) %all-to-all-start) | async-done | bytes 16416 | tf_op jit(solution)/shard_map/all_to_all | solution.py:38
  28.5 0.6 fold.1
  29.2 12.4 %all-to-all-start.1 = ((f32[12,1,128]{2,1,0:T(1,128)}), f32[12,1,128]{2,1,0:T(1,128)S(1)}, u32[]{:S(2)}, u32[]{:S(2)}) async-start(f32[12,1,128]{2,1,0:T(1,128)} %fold.1), calls=%async_computation.1 | async-start | bytes 12288 | tf_op jit(solution)/shard_map/all_to_all | solution.py:38
  41.5 0.0 collective-permute-done.other_hbm
  41.5 5.0 %forward.1 = (f32[384,768]{1,0:T(8,128)}, bf16[1536,384]{1,0:T(8,128)(2,1)}, f32[3,768]{1,0:T(4,128)}, f32[8,128]{1,0:T(8,128)}) custom-call(s32[1]{0:T(128)} %bitcast.me, s32[3]{0:T(128)} %bins.5, bf16[384,768]{1,0:T(8,128)(2,1)} %attn_hbm.1, bf16[1152,768]{1,0:T(8,128)(2,1)} %collective-permute-done.other_hbm, ...), custom_call_target="tpu_custom_call" | custom-call | flops 1000000000 | bytes 6000000 | tf_op jit(solution)/shard_map/forward/pallas_call | solution.py:201
  46.5 1.9 %collective-permute-start.1 = (f32[8,128]{1,0:T(8,128)}, f32[8,128]{1,0:T(8,128)S(1)}, u32[]{:S(2)}, u32[]{:S(2)}) collective-permute-start(f32[8,128]{1,0:T(8,128)} %get-tuple-element.12.marks_hbm), channel_id=1, source_target_pairs={{0,1},{1,0},{2,3},{3,2},{4,5},{5,4},{6,7},{7,6},{8,9},{9,8},{10,11... | collective-permute-start | bytes 12296 | tf_op jit(solution)/shard_map/ppermute | solution.py:34
  48.5 3.1 %all-to-all-done.1.got_hbm = f32[12,1,128]{2,1,0:T(1,128)S(1)} async-done(((f32[12,1,128]{2,1,0:T(1,128)}), f32[12,1,128]{2,1,0:T(1,128)S(1)}, u32[]{:S(2)}, u32[]{:S(2)}) %all-to-all-start.1) | async-done | bytes 6176 | tf_op jit(solution)/shard_map/all_to_all | solution.py:38
  51.5 0.0 collective-permute-done.1.other_hbm
  51.6 0.6 copy-done.2
  52.1 2.9 %scaled.1 = (bf16[384,768]{1,0:T(8,128)(2,1)}, f32[3,768]{1,0:T(4,128)}, f32[1,128]{1,0:T(1,128)}, f32[8,768]{1,0:T(8,128)}) custom-call(s32[3]{0:T(128)} %bins.5, f32[12,1,128]{2,1,0:T(1,128)} %copy-done.2, f32[8,128]{1,0:T(8,128)} %get-tuple-element.12.marks_hbm, f32[8,128]{1,0:T(8,128)} %copy-done.3, f32[3,768]{1,0:T(4,128)} %gate_hbm.1, ...), custom_call_target="tpu_custom_call" | custom-call | flops 10000000 | bytes 2000000 | tf_op jit(solution)/shard_map/scaled/pallas_call | solution.py:281
  55.0 0.7 convert_element_type.26
  55.8 2.8 %convolution_convert_fusion = f16[1536,768]{1,0:T(8,128)(2,1)S(1)} fusion(bf16[1536,384]{1,0:T(8,128)(2,1)} %get-tuple-element.11, bf16[384,768]{1,0:T(8,128)(2,1)} %get-tuple-element.15), kind=kOutput, calls=%fused_computation.1 | convolution fusion | flops 907149312 | bytes 4128768 | tf_op jit(solution)/shard_map/dot_general | solution.py:313
  58.6 0.6 pad_maximum_fusion
  59.2 34.5 %all_to_all.20 = f16[16,104,768]{2,1,0:T(8,128)(2,1)S(1)} all-to-all(f16[16,104,768]{2,1,0:T(8,128)(2,1)S(1)} %pad_maximum_fusion), channel_id=1, replica_groups=mesh['dp_x'=4,'dp_yh'=4,'dp_yl'=2,'dp_zh'=6,'dp_zl'=2,'mp'=2] {'dp_x','d..., dimensions={0} | all-to-all | bytes 5111808 | tf_op jit(solution)/shard_map/all_to_all | solution.py:38
  93.8 0.0 copy-start.4
  93.9 0.5 multiply_reduce_fusion
  94.4 0.2 convert_element_type.30
  94.6 0.1 pad_maximum_fusion.2
  94.6 27.5 %all_to_all.21 = f16[24,32,128]{2,1,0:T(8,128)(2,1)S(1)} all-to-all(f16[24,32,128]{2,1,0:T(8,128)(2,1)S(1)} %pad_maximum_fusion.2), channel_id=1, replica_groups=mesh['dp_x'=4,'dp_yh'=4,'dp_yl'=2,'dp_zh'=6,'dp_zl'=2,'mp'=2] {'dp_yh','..., dimensions={0} | all-to-all | bytes 393216 | tf_op jit(solution)/shard_map/all_to_all | solution.py:38
  122.1 0.1 copy_convert_fusion
  122.3 0.6 reshape.97
  122.9 0.5 bitcast_multiply_fusion
  (18 shorter events, 0.2 us)
Async XLA Ops:
  0.6 1.7 %copy-start = (bf16[768,1536]{1,0:T(8,128)(2,1)S(1)}, bf16[768,1536]{1,0:T(8,128)(2,1)}, u32[]{:S(2)}) copy-start(bf16[768,1536]{1,0:T(8,128)(2,1)} %param.7) | copy-start | bytes 7077892
  0.6 1.8 %copy-start.1 = (bf16[384,768]{1,0:T(8,128)(2,1)S(1)}, bf16[384,768]{1,0:T(8,128)(2,1)}, u32[]{:S(2)}) copy-start(bf16[384,768]{1,0:T(8,128)(2,1)} %attn_hbm.1) | copy-start | bytes 1769476
  3.7 37.8 %collective-permute-start = (bf16[1152,768]{1,0:T(8,128)(2,1)}, bf16[1152,768]{1,0:T(8,128)(2,1)}, u32[]{:S(2)}, u32[]{:S(2)}) collective-permute-start(bf16[1152,768]{1,0:T(8,128)(2,1)} %pad_maximum_fusion.1), channel_id=1, source_target_pairs={{0,1},{1,0},{2,3},{3,2},{4,5},{5,4},{6,7},{7,6},{8,9},{9,8},{10,11... | collective-permute-start | bytes 5308424 | tf_op jit(solution)/shard_map/ppermute | solution.py:34
  6.9 21.6 %all-to-all-start = ((f32[32,1,128]{2,1,0:T(1,128)}), f32[32,1,128]{2,1,0:T(1,128)S(1)}, u32[]{:S(2)}, u32[]{:S(2)}) async-start(f32[32,1,128]{2,1,0:T(1,128)} %count.1), calls=%async_computation | async-start | bytes 32768 | tf_op jit(solution)/shard_map/all_to_all | solution.py:38
  29.2 22.4 %all-to-all-start.1 = ((f32[12,1,128]{2,1,0:T(1,128)}), f32[12,1,128]{2,1,0:T(1,128)S(1)}, u32[]{:S(2)}, u32[]{:S(2)}) async-start(f32[12,1,128]{2,1,0:T(1,128)} %fold.1), calls=%async_computation.1 | async-start | bytes 12288 | tf_op jit(solution)/shard_map/all_to_all | solution.py:38
  46.5 5.0 %collective-permute-start.1 = (f32[8,128]{1,0:T(8,128)}, f32[8,128]{1,0:T(8,128)S(1)}, u32[]{:S(2)}, u32[]{:S(2)}) collective-permute-start(f32[8,128]{1,0:T(8,128)} %get-tuple-element.12.marks_hbm), channel_id=1, source_target_pairs={{0,1},{1,0},{2,3},{3,2},{4,5},{5,4},{6,7},{7,6},{8,9},{9,8},{10,11... | collective-permute-start | bytes 12296 | tf_op jit(solution)/shard_map/ppermute | solution.py:34
  51.5 0.6 copy-start.2
  51.6 0.6 copy-start.3
  93.8 29.1 %copy-start.4 = (f32[1,128]{1,0:T(1,128)S(1)}, f32[1,128]{1,0:T(1,128)}, u32[]{:S(2)}) copy-start(f32[1,128]{1,0:T(1,128)} %get-tuple-element.18) | copy-start | bytes 1540

commit v6 on v4

--- a/solution.py
+++ b/solution.py
@@ -120,53 +120,54 @@
     bins,
     attn_hbm,
     other_hbm,
-    part_hbm,
+    w_hbm,
     resid_hbm,
     target_hbm,
     gate,
-    error,
+    error_hbm,
     features_hbm,
     error_proj,
-    losses,
-    grad_exp,
-    grad_scale,
+    marks,
     attn,
-    other,
-    part,
+    attn_far,
+    w_near,
+    w_far,
     resid,
     target,
+    error,
     features,
-    sems,
+    load_sems,
+    store_sems,
 ):
-    tokens, half = part.shape
+    tokens, half = attn.shape
     samples = gate.shape[0]
     per_sample = tokens // samples
     run = half // 2
-    loads = [
-        pltpu.make_async_copy(src, dst, sems.at[n])
-        for n, (src, dst) in enumerate(
-            (
-                (attn_hbm, attn),
-                (other_hbm, other),
-                (part_hbm, part),
-                (resid_hbm, resid),
-                (target_hbm, target),
-            )
-        )
-    ]
+    mine = pl.multiple_of(me[0] * half, half)
+    theirs = pl.multiple_of((1 - me[0]) * half, half)
+    pairs = (
+        (attn_hbm, attn),
+        (other_hbm.at[half:, :], attn_far),
+        (w_hbm.at[:, pl.ds(mine, half)], w_near),
+        (other_hbm.at[:half, :], w_far),
+        (resid_hbm, resid),
+        (target_hbm, target),
+    )
+    loads = [pltpu.make_async_copy(src, dst, load_sems.at[n]) for n, (src, dst) in enumerate(pairs)]
     for load in loads:
         load.start()
+    stores = []
+
+    def store(src, dst, rows):
+        stores.append(pltpu.make_async_copy(src.at[rows, :], dst.at[rows, :], store_sems.at[len(stores)]))
+        stores[-1].start()
+
     picks = row_picks(run)
-    mine = pl.multiple_of(me[0] * half, half)
-    theirs = pl.multiple_of((1 - me[0]) * half, half)
-    stores = []
-    for first, block, load in ((mine, attn, loads[0]), (theirs, other.at[half:, :], loads[1])):
+    for first, block, load in ((mine, attn, loads[0]), (theirs, attn_far, loads[1])):
         load.wait()
         for n, moved in enumerate(feature_rows(block, picks)):
             features[pl.ds(pl.multiple_of(first + n * run, run), run), :] = moved
-        rows = pl.ds(first, half)
-        stores.append(pltpu.make_async_copy(features.at[rows, :], features_hbm.at[rows, :], sems.at[len(loads) + len(stores)]))
-        stores[-1].start()
+        store(features, features_hbm, pl.ds(first, half))
     for load in loads[2:]:
         load.wait()
 
@@ -176,55 +177,60 @@
     reach = jnp.zeros((1, half), jnp.float32)
     for s in range(samples):
         rows = slice(s * per_sample, (s + 1) * per_sample)
-        projected = part[rows, :] + jnp.dot(
-            other[half + s * per_sample : half + (s + 1) * per_sample, :],
-            other[:half, :],
-            preferred_element_type=jnp.float32,
+        projected = jnp.dot(attn[rows, :], w_near[...], preferred_element_type=jnp.float32) + jnp.dot(
+            attn_far[rows, :], w_far[...], preferred_element_type=jnp.float32
         )
         scale = gate[s : s + 1, :]
         diff = resid[rows, :].astype(jnp.float32) + scale * projected - target[rows, :].astype(jnp.float32)
         error[rows, :] = diff
+        store(error, error_hbm, pl.ds(s * per_sample, per_sample))
         error_proj[s : s + 1, :] = jnp.sum(diff * projected, axis=0, keepdims=True)
         hit = lane == bins[s]
         largest = jnp.sum(jnp.where(hit, steepest, 0.0), axis=1, keepdims=True)
         reach = reach + largest * jnp.sum(jnp.abs(diff * scale), axis=0, keepdims=True)
         squares = jnp.sum(jnp.sum(diff * diff, axis=0, keepdims=True), axis=1, keepdims=True)
         found = found + jnp.where(hit, squares * (1.0 / (per_sample * 2 * half)), 0.0)
-    losses[...] = found
     bound = exponent_of(jnp.max(reach, axis=1, keepdims=True) * (1.01 * ATTN_BOUND))
-    grad_exp[...] = jnp.broadcast_to(bound, grad_exp.shape)
-    grad_scale[...] = jnp.broadcast_to(jnp.exp2(TOP - bound), grad_scale.shape)
-    for store in stores:
-        store.wait()
-
-
-def forward(me, bins, attn, other, part, resid, target, gate):
-    tokens, half = part.shape
-    operands = (attn, other, part, resid, target)
+    marks[...] = jnp.broadcast_to(bound, marks.shape)
+    marks[:1, :] = found
+    for copy in stores:
+        copy.wait()
+
+
+def forward(me, bins, attn, other, w_out, resid, target, gate):
+    tokens, half = attn.shape
+    block = pltpu.VMEM(attn.shape, attn.dtype)
+    square = pltpu.VMEM((half, half), attn.dtype)
     return pl.pallas_call(
         forward_kernel,
         out_shape=(
             jax.ShapeDtypeStruct((tokens, half), jnp.float32),
             jax.ShapeDtypeStruct((2 * half, tokens), jnp.bfloat16),
             jax.ShapeDtypeStruct(gate.shape, jnp.float32),
-            jax.ShapeDtypeStruct((1, NBINS), jnp.float32),
-            jax.ShapeDtypeStruct((1, NBINS), jnp.float32),
-            jax.ShapeDtypeStruct((1, half), jnp.float32),
+            jax.ShapeDtypeStruct((SIDE, NBINS), jnp.float32),
         ),
         in_specs=[SMEM] * 2 + [HBM] * 5 + [VMEM],
-        out_specs=(VMEM, HBM, VMEM, VMEM, VMEM, VMEM),
+        out_specs=(HBM, HBM, VMEM, VMEM),
         scratch_shapes=[
-            *(pltpu.VMEM(x.shape, x.dtype) for x in operands),
+            block,
+            block,
+            square,
+            square,
+            block,
+            block,
+            pltpu.VMEM((tokens, half), jnp.float32),
             pltpu.VMEM((2 * half, tokens), jnp.bfloat16),
-            pltpu.SemaphoreType.DMA((len(operands) + 2,)),
+            pltpu.SemaphoreType.DMA((6,)),
+            pltpu.SemaphoreType.DMA((2 + gate.shape[0],)),
         ],
         cost_estimate=pl.CostEstimate(flops=10**9, bytes_accessed=6 * 10**6, transcendentals=0),
+        compiler_params=grant(50),
         name="forward",
-    )(me, bins, *operands, gate)
+    )(me, bins, attn, other, w_out, resid, target, gate)
 
 
 def scale_kernel(
-    bins, got, losses, other_losses, grad_exp, error, gate, d_proj, steepness, per_count, side
+    bins, got, marks, other_marks, error, gate, d_proj, steepness, per_count, side
 ):
     tokens, half = error.shape
     samples = gate.shape[0]
@@ -233,21 +239,24 @@
     floored = jnp.maximum(jnp.sum(got[...], axis=0), 1.0)
     slope = weights_at(lane.astype(jnp.float32)) / floored
     per_count[...] = slope
+    grad_exp = marks[1:2, :]
+    lift = jnp.exp2(TOP - grad_exp[:, :1])
     for s in range(samples):
         rows = slice(s * per_sample, (s + 1) * per_sample)
         coefficient = jnp.sum(jnp.where(lane == bins[s], slope * LOSS_SCALE, 0.0), axis=1, keepdims=True)
         coefficient = coefficient * (1.0 / (per_sample * half))
-        d_proj[rows, :] = (coefficient * error[rows, :] * gate[s : s + 1, :]).astype(jnp.bfloat16)
+        rounded = (coefficient * error[rows, :] * gate[s : s + 1, :]).astype(jnp.bfloat16)
+        d_proj[rows, :] = (rounded.astype(jnp.float32) * lift).astype(jnp.bfloat16)
         steepness[s : s + 1, :] = jnp.broadcast_to(coefficient, (1, NBINS))
-    total = losses[...] + other_losses[...]
+    total = marks[:1, :] + other_marks[:1, :]
     loss_exp = exponent_of(total)
     high, low = halves(total * jnp.exp2(TOP - loss_exp))
     side[...] = jnp.zeros(side.shape, jnp.float32)
-    for n, row in enumerate((high, low, grad_exp[...], loss_exp)):
+    for n, row in enumerate((high, low, grad_exp, loss_exp)):
         side[n : n + 1, :NBINS] = row
 
 
-def scaled(bins, got, losses, other_losses, grad_exp, error, gate):
+def scaled(bins, got, marks, other_marks, error, gate):
     return pl.pallas_call(
         scale_kernel,
         out_shape=(
@@ -256,31 +265,29 @@
             jax.ShapeDtypeStruct((1, NBINS), jnp.float32),
             jax.ShapeDtypeStruct((SIDE, gate.shape[1]), jnp.float32),
         ),
-        in_specs=[SMEM] + [VMEM] * 6,
+        in_specs=[SMEM] + [VMEM] * 5,
         out_specs=(VMEM,) * 4,
         cost_estimate=pl.CostEstimate(flops=10**7, bytes_accessed=2 * 10**6, transcendentals=0),
         compiler_params=grant(20),
         name="scaled",
-    )(bins, got, losses, other_losses, grad_exp, error, gate)
+    )(bins, got, marks, other_marks, error, gate)
 
 
 def body(attn, w_out, resid, target, gate, bins):
     own_cols = resid.shape[1]
     me = lax.axis_index("mp")
     got = count_sweep(bins)
-    w_mine = lax.dynamic_slice_in_dim(w_out, me * own_cols, own_cols, axis=1)
     w_theirs = lax.dynamic_slice_in_dim(w_out, (1 - me) * own_cols, own_cols, axis=1)
     other = partner(jnp.concatenate([w_theirs, attn], axis=0))
-    part = jnp.dot(attn, w_mine, preferred_element_type=jnp.float32)
-    error, features, error_proj, losses, grad_exp, grad_scale = forward(
-        me.reshape(1), bins, attn, other, part, resid, target, gate
+    error, features, error_proj, marks = forward(
+        me.reshape(1), bins, attn, other, w_out, resid, target, gate
     )
-    other_losses = partner(losses)
+    other_marks = partner(marks)
     near, far = group(NEAR), group(FAR)
-    d_proj, steepness, per_count, side = scaled(bins, got, losses, other_losses, grad_exp, error, gate)
+    d_proj, steepness, per_count, side = scaled(bins, got, marks, other_marks, error, gate)
     side = side.astype(jnp.float16)
     partial = jnp.dot(features, d_proj, preferred_element_type=jnp.float32)
-    partial = (partial * grad_scale).astype(jnp.float16).reshape(near, -1, own_cols)
+    partial = partial.astype(jnp.float16).reshape(near, -1, own_cols)
     keep = partial.shape[1]
     partial = jnp.concatenate([partial, jnp.broadcast_to(side[None], (near, *side.shape))], axis=1)
     got = exchange(partial, NEAR)

time: 124 us -> 121 us (0.976)
  blocking collectives: 34.6 us -> 56 us
  starting transfers between devices: 38.9 us -> 26.1 us
  waiting for transfers between devices: 26.4 us -> 20 us
  local copies, waits for them, and re-layouts: 5.18 us -> 2.37 us
  matrix products: 4.32 us -> 2.65 us
    all_to_all x1 -> x2, blocking collectives: 34.6 us -> 56 us  [exchange(): return lax.all_to_all(x, axes, 0, 0, tiled=True)]
    all_to_all x3 -> x2, starting transfers between devices: 35.1 us -> 22.3 us  [exchange(): return lax.all_to_all(x, axes, 0, 0, tiled=True)]
    all_to_all x3 -> x2, waiting for transfers between devices: 26.4 us -> 20 us  [exchange(): return lax.all_to_all(x, axes, 0, 0, tiled=True)]
    unnamed x17 -> x11, local copies, waits for them, and re-layouts: 4.18 us -> 0.04 us
    dot_general x1 -> x0, matrix products: 1.66 us -> none  [body(): part = jnp.dot(attn, w_mine, preferred_element_type=jnp.float32)]
    dynamic_slice x1, local copies, waits for them, and re-layouts: 0.08 us -> 1.41 us  [body(): lax.dynamic_slice_in_dim(w_out, (1 - me) * own_cols, own_cols, axis=1)]
  transfers between devices with their start and end apart: 5 -> 4, of which waited for: 3 -> 2; matrix products, arithmetic and copies ran while one was open for 3% -> 1% of each run, Pallas kernels for 6% -> 6%
where the time goes in v6:
time: 121 us; the launch traced here: 120 us
  blocking collectives  56 us (46%)
  starting transfers between devices  26.1 us (22%)
  waiting for transfers between devices  20 us (17%)
  Pallas kernels  7.94 us (7%)
  other arithmetic  4.58 us (4%)
  matrix products  2.65 us (2%)
  local copies, waits for them, and re-layouts  2.37 us (2%)
    all_to_all x2, blocking collectives, exchange(): return lax.all_to_all(x, axes, 0, 0, tiled=True)  56 us
    all_to_all x2, starting transfers between devices, exchange(): return lax.all_to_all(x, axes, 0, 0, tiled=True)  22.3 us
    all_to_all x2, waiting for transfers between devices, exchange(): return lax.all_to_all(x, axes, 0, 0, tiled=True)  20 us
    pallas_call x1, Pallas kernels, forward(): pl.pallas_call(forward_kernel, out_shape=(jax.ShapeDtypeStruct((tokens, h...  5.1 us
    ppermute x2, starting transfers between devices, partner(): return lax.ppermute(x, 'mp', [(0, 1), (1, 0)])  3.83 us
    dot_general x1, matrix products, body(): partial = jnp.dot(features, d_proj, preferred_element_type=jnp.float32)  2.65 us
  transfers between devices with their start and end apart: 4, of which 2 were waited for; matrix products, arithmetic and copies ran while one was open for 1% of the time, Pallas kernels for 6%

profile of v6, /device:TPU:8, one launch (start us, length us, event | category | flops | bytes accessed | tf_op | source)
XLA Modules:
  0.0 120.5 jit_solution(4491206532241501021)
XLA Ops:
  0.6 0.0 copy-start
  0.6 1.4 %constant_dynamic-slice_fusion = bf16[768,768]{1,0:T(8,128)(2,1)S(1)} fusion(bf16[768,1536]{1,0:T(8,128)(2,1)} %w_hbm.1, s32[]{:T(128)S(6)} %select_n.3), kind=kLoop, calls=%fused_computation.53 | loop fusion | bytes 2359300 | tf_op jit(solution)/shard_map/dynamic_slice | solution.py:280
  2.1 0.0 copy-done
  2.1 0.0 copy-start.1
  2.1 0.0 copy-start.2
  2.1 0.0 copy-start.3
  2.1 0.0 copy-start.4
  2.1 1.3 %pad_maximum_fusion.1 = bf16[1152,768]{1,0:T(8,128)(2,1)} fusion(bf16[384,768]{1,0:T(8,128)(2,1)S(1)} %copy-done, bf16[768,768]{1,0:T(8,128)(2,1)S(1)} %constant_dynamic-slice_fusion), kind=kLoop, calls=%fused_computation.3 | loop fusion | flops 3538944 | bytes 3538944 | tf_op jit(solution)/shard_map/concatenate | solution.py:281
  3.4 1.9 %collective-permute-start = (bf16[1152,768]{1,0:T(8,128)(2,1)}, bf16[1152,768]{1,0:T(8,128)(2,1)}, u32[]{:S(2)}, u32[]{:S(2)}) collective-permute-start(bf16[1152,768]{1,0:T(8,128)(2,1)} %pad_maximum_fusion.1), channel_id=1, source_target_pairs={{0,1},{1,0},{2,3},{3,2},{4,5},{5,4},{6,7},{7,6},{8,9},{9,8},{10,11... | collective-permute-start | bytes 5308424 | tf_op jit(solution)/shard_map/ppermute | solution.py:34
  5.4 1.3 %count.1 = f32[32,1,128]{2,1,0:T(1,128)} custom-call(s32[3]{0:T(128)} %bins.5), custom_call_target="tpu_custom_call" | custom-call | tf_op jit(solution)/shard_map/count/pallas_call | solution.py:77
  6.6 21.6 %all_to_all.20.got = f32[32,1,128]{2,1,0:T(1,128)S(1)} all-to-all(f32[32,1,128]{2,1,0:T(1,128)} %count.1), channel_id=1, replica_groups=mesh['dp_x'=4,'dp_yh'=4,'dp_yl'=2,'dp_zh'=6,'dp_zl'=2,'mp'=2] {'dp_x','d..., dimensions={0} | all-to-all | bytes 32768 | tf_op jit(solution)/shard_map/all_to_all | solution.py:38
  28.2 0.6 fold.1
  28.9 12.4 %all-to-all-start.1 = ((f32[12,1,128]{2,1,0:T(1,128)}), f32[12,1,128]{2,1,0:T(1,128)S(1)}, u32[]{:S(2)}, u32[]{:S(2)}) async-start(f32[12,1,128]{2,1,0:T(1,128)} %fold.1), calls=%async_computation.1 | async-start | bytes 12288 | tf_op jit(solution)/shard_map/all_to_all | solution.py:38
  41.2 0.0 collective-permute-done.other_hbm
  41.3 5.1 %forward.1 = (f32[384,768]{1,0:T(8,128)S(1)}, bf16[1536,384]{1,0:T(8,128)(2,1)}, f32[3,768]{1,0:T(4,128)S(1)}, f32[8,128]{1,0:T(8,128)S(1)}) custom-call(s32[1]{0:T(128)} %bitcast.me, s32[3]{0:T(128)S(1)} %copy-done.4, bf16[384,768]{1,0:T(8,128)(2,1)S(1)} %copy-done, bf16[1152,768]{1,0:T(8,128)(2,1)} %collective-permute-done.other_hbm, ...), custom_call_target="tpu_custom_call" | custom-call | flops 1000000000 | bytes 6000000 | tf_op jit(solution)/shard_map/forward/pallas_call | solution.py:204
  46.4 1.9 %collective-permute-start.1 = (f32[8,128]{1,0:T(8,128)S(1)}, f32[8,128]{1,0:T(8,128)S(1)}, u32[]{:S(2)}, u32[]{:S(2)}) collective-permute-start(f32[8,128]{1,0:T(8,128)S(1)} %get-tuple-element.12.marks), channel_id=1, source_target_pairs={{0,1},{1,0},{2,3},{3,2},{4,5},{5,4},{6,7},{7,6},{8,9},{9,8},{10,11... | collective-permute-start | bytes 12296 | tf_op jit(solution)/shard_map/ppermute | solution.py:34
  48.3 2.9 %all-to-all-done.1.got = f32[12,1,128]{2,1,0:T(1,128)S(1)} async-done(((f32[12,1,128]{2,1,0:T(1,128)}), f32[12,1,128]{2,1,0:T(1,128)S(1)}, u32[]{:S(2)}, u32[]{:S(2)}) %all-to-all-start.1) | async-done | bytes 6176 | tf_op jit(solution)/shard_map/all_to_all | solution.py:38
  51.3 0.0 collective-permute-done.1.other_marks
  51.3 0.9 scaled.1
  52.2 2.7 %convolution_convert_fusion = f16[1536,768]{1,0:T(8,128)(2,1)S(1)} fusion(bf16[1536,384]{1,0:T(8,128)(2,1)} %get-tuple-element.11, bf16[384,768]{1,0:T(8,128)(2,1)S(1)} %get-tuple-element.14), kind=kOutput, calls=%fused_computation.1 | convolution fusion | flops 907149312 | bytes 4128768 | tf_op jit(solution)/shard_map/dot_general | solution.py:289
  54.9 0.6 pad_maximum_fusion
  55.5 34.4 %all_to_all.21 = f16[16,104,768]{2,1,0:T(8,128)(2,1)S(1)} all-to-all(f16[16,104,768]{2,1,0:T(8,128)(2,1)S(1)} %pad_maximum_fusion), channel_id=1, replica_groups=mesh['dp_x'=4,'dp_yh'=4,'dp_yl'=2,'dp_zh'=6,'dp_zl'=2,'mp'=2] {'dp_x','d..., dimensions={0} | all-to-all | bytes 5111808 | tf_op jit(solution)/shard_map/all_to_all | solution.py:38
  90.0 0.5 multiply_reduce_fusion
  90.5 0.2 convert_element_type.30
  90.7 0.7 pad_maximum_fusion.2
  91.5 9.9 %all-to-all-start.3 = ((f16[24,32,128]{2,1,0:T(8,128)(2,1)}), f16[24,32,128]{2,1,0:T(8,128)(2,1)S(1)}, u32[]{:S(2)}, u32[]{:S(2)}) async-start(f16[24,32,128]{2,1,0:T(8,128)(2,1)} %pad_maximum_fusion.2), calls=%async_computation.3 | async-start | bytes 393216 | tf_op jit(solution)/shard_map/all_to_all | solution.py:38
  101.4 0.1 slice_reduce_fusion.2
  101.5 0.7 broadcast_multiply_fusion
  102.2 17.0 %all-to-all-done.3 = f16[24,32,128]{2,1,0:T(8,128)(2,1)S(1)} async-done(((f16[24,32,128]{2,1,0:T(8,128)(2,1)}), f16[24,32,128]{2,1,0:T(8,128)(2,1)S(1)}, u32[]{:S(2)}, u32[]{:S(2)}) %all-to-all-start.3) | async-done | bytes 196640 | tf_op jit(solution)/shard_map/all_to_all | solution.py:38
  119.2 0.1 copy_convert_fusion
  119.4 0.6 reshape.97
  120.0 0.5 bitcast_multiply_fusion
  (19 shorter events, 0.3 us)
Async XLA Ops:
  0.6 1.4 %copy-start = (bf16[384,768]{1,0:T(8,128)(2,1)S(1)}, bf16[384,768]{1,0:T(8,128)(2,1)}, u32[]{:S(2)}) copy-start(bf16[384,768]{1,0:T(8,128)(2,1)} %attn_hbm.1) | copy-start | bytes 1769476
  2.1 39.2 %copy-start.1 = (bf16[384,768]{1,0:T(8,128)(2,1)S(1)}, bf16[384,768]{1,0:T(8,128)(2,1)}, u32[]{:S(2)}) copy-start(bf16[384,768]{1,0:T(8,128)(2,1)} %resid_hbm.1) | copy-start | bytes 1769476
  2.1 39.2 %copy-start.2 = (bf16[384,768]{1,0:T(8,128)(2,1)S(1)}, bf16[384,768]{1,0:T(8,128)(2,1)}, u32[]{:S(2)}) copy-start(bf16[384,768]{1,0:T(8,128)(2,1)} %target_hbm.1) | copy-start | bytes 1769476
  2.1 39.2 %copy-start.3 = (f32[3,768]{1,0:T(4,128)S(1)}, f32[3,768]{1,0:T(4,128)}, u32[]{:S(2)}) copy-start(f32[3,768]{1,0:T(4,128)} %gate.3) | copy-start | bytes 27652
  2.1 39.2 %copy-start.4 = (s32[3]{0:T(128)S(1)}, s32[3]{0:T(128)}, u32[]{:S(2)}) copy-start(s32[3]{0:T(128)} %bins.5) | copy-start | bytes 40
  3.4 37.8 %collective-permute-start = (bf16[1152,768]{1,0:T(8,128)(2,1)}, bf16[1152,768]{1,0:T(8,128)(2,1)}, u32[]{:S(2)}, u32[]{:S(2)}) collective-permute-start(bf16[1152,768]{1,0:T(8,128)(2,1)} %pad_maximum_fusion.1), channel_id=1, source_target_pairs={{0,1},{1,0},{2,3},{3,2},{4,5},{5,4},{6,7},{7,6},{8,9},{9,8},{10,11... | collective-permute-start | bytes 5308424 | tf_op jit(solution)/shard_map/ppermute | solution.py:34
  28.9 22.4 %all-to-all-start.1 = ((f32[12,1,128]{2,1,0:T(1,128)}), f32[12,1,128]{2,1,0:T(1,128)S(1)}, u32[]{:S(2)}, u32[]{:S(2)}) async-start(f32[12,1,128]{2,1,0:T(1,128)} %fold.1), calls=%async_computation.1 | async-start | bytes 12288 | tf_op jit(solution)/shard_map/all_to_all | solution.py:38
  46.4 4.9 %collective-permute-start.1 = (f32[8,128]{1,0:T(8,128)S(1)}, f32[8,128]{1,0:T(8,128)S(1)}, u32[]{:S(2)}, u32[]{:S(2)}) collective-permute-start(f32[8,128]{1,0:T(8,128)S(1)} %get-tuple-element.12.marks), channel_id=1, source_target_pairs={{0,1},{1,0},{2,3},{3,2},{4,5},{5,4},{6,7},{7,6},{8,9},{9,8},{10,11... | collective-permute-start | bytes 12296 | tf_op jit(solution)/shard_map/ppermute | solution.py:34
  91.5 27.8 %all-to-all-start.3 = ((f16[24,32,128]{2,1,0:T(8,128)(2,1)}), f16[24,32,128]{2,1,0:T(8,128)(2,1)S(1)}, u32[]{:S(2)}, u32[]{:S(2)}) async-start(f16[24,32,128]{2,1,0:T(8,128)(2,1)} %pad_maximum_fusion.2), calls=%async_computation.3 | async-start | bytes 393216 | tf_op jit(solution)/shard_map/all_to_all | solution.py:38

commit v7 on v6

--- a/solution.py
+++ b/solution.py
@@ -124,7 +124,7 @@
     resid_hbm,
     target_hbm,
     gate,
-    error_hbm,
+    error,
     features_hbm,
     error_proj,
     marks,
@@ -134,7 +134,6 @@
     w_far,
     resid,
     target,
-    error,
     features,
     load_sems,
     store_sems,
@@ -183,7 +182,6 @@
         scale = gate[s : s + 1, :]
         diff = resid[rows, :].astype(jnp.float32) + scale * projected - target[rows, :].astype(jnp.float32)
         error[rows, :] = diff
-        store(error, error_hbm, pl.ds(s * per_sample, per_sample))
         error_proj[s : s + 1, :] = jnp.sum(diff * projected, axis=0, keepdims=True)
         hit = lane == bins[s]
         largest = jnp.sum(jnp.where(hit, steepest, 0.0), axis=1, keepdims=True)
@@ -210,7 +208,7 @@
             jax.ShapeDtypeStruct((SIDE, NBINS), jnp.float32),
         ),
         in_specs=[SMEM] * 2 + [HBM] * 5 + [VMEM],
-        out_specs=(HBM, HBM, VMEM, VMEM),
+        out_specs=(VMEM, HBM, VMEM, VMEM),
         scratch_shapes=[
             block,
             block,
@@ -218,10 +216,9 @@
             square,
             block,
             block,
-            pltpu.VMEM((tokens, half), jnp.float32),
             pltpu.VMEM((2 * half, tokens), jnp.bfloat16),
             pltpu.SemaphoreType.DMA((6,)),
-            pltpu.SemaphoreType.DMA((2 + gate.shape[0],)),
+            pltpu.SemaphoreType.DMA((2,)),
         ],
         cost_estimate=pl.CostEstimate(flops=10**9, bytes_accessed=6 * 10**6, transcendentals=0),
         compiler_params=grant(50),
@@ -253,7 +250,7 @@
     high, low = halves(total * jnp.exp2(TOP - loss_exp))
     side[...] = jnp.zeros(side.shape, jnp.float32)
     for n, row in enumerate((high, low, grad_exp, loss_exp)):
-        side[n : n + 1, :NBINS] = row
+        side[n : n + 1, :] = row
 
 
 def scaled(bins, got, marks, other_marks, error, gate):
@@ -263,7 +260,7 @@
             jax.ShapeDtypeStruct(error.shape, jnp.bfloat16),
             jax.ShapeDtypeStruct((gate.shape[0], NBINS), jnp.float32),
             jax.ShapeDtypeStruct((1, NBINS), jnp.float32),
-            jax.ShapeDtypeStruct((SIDE, gate.shape[1]), jnp.float32),
+            jax.ShapeDtypeStruct((SIDE, NBINS), jnp.float32),
         ),
         in_specs=[SMEM] + [VMEM] * 5,
         out_specs=(VMEM,) * 4,
@@ -287,22 +284,25 @@
     d_proj, steepness, per_count, side = scaled(bins, got, marks, other_marks, error, gate)
     side = side.astype(jnp.float16)
     partial = jnp.dot(features, d_proj, preferred_element_type=jnp.float32)
-    partial = partial.astype(jnp.float16).reshape(near, -1, own_cols)
-    keep = partial.shape[1]
-    partial = jnp.concatenate([partial, jnp.broadcast_to(side[None], (near, *side.shape))], axis=1)
+    partial = partial.astype(jnp.float16).reshape(near, -1, SIDE, own_cols)
+    stripes = partial.shape[1]
+    partial = partial.transpose(0, 2, 1, 3).reshape(near, SIDE, stripes * own_cols)
+    partial = jnp.concatenate([partial, jnp.broadcast_to(side[None], (near, *side.shape))], axis=2)
     got = exchange(partial, NEAR)
 
-    sides = got[:, keep : keep + 4, :NBINS].astype(jnp.float32)
+    sides = got[:, :4, stripes * own_cols :].astype(jnp.float32)
     grad_exp = jnp.max(sides[:, 2], axis=0) + math.log2(near)
-    scale = jnp.tile(jnp.exp2(sides[:, 2] - grad_exp), (1, own_cols // NBINS))
-    total = jnp.sum(got[:, :keep].astype(jnp.float32) * scale[:, None, :], axis=0)
+    scale = jnp.exp2(sides[:, 2, :1] - grad_exp[:1])
+    got = got[:, :, : stripes * own_cols].astype(jnp.float32)
+    total = jnp.sum(got * scale[:, :, None], axis=0)
     loss_exp = jnp.max(sides[:, 3], axis=0) + math.log2(near)
     high, low = halves(
         jnp.sum((sides[:, 0] + sides[:, 1] * (1.0 / LOW)) * jnp.exp2(sides[:, 3] - loss_exp), axis=0)
     )
     side = jnp.stack([high, low, grad_exp, loss_exp])
     side = jnp.pad(side, ((0, SIDE - 4), (0, 0))).astype(jnp.float16)
-    rows = total.astype(jnp.float16).reshape(far, -1, NBINS)
+    rows = total.astype(jnp.float16).reshape(SIDE, stripes, own_cols).transpose(1, 0, 2)
+    rows = rows.reshape(far, -1, NBINS)
     keep = rows.shape[1]
     rows = jnp.concatenate([rows, jnp.broadcast_to(side[None], (far, *side.shape))], axis=1)
     got = exchange(rows, FAR).astype(jnp.float32)

time: 121 us -> 118 us (0.975)
  blocking collectives: 56 us -> 53.4 us
    all_to_all x2, blocking collectives: 56 us -> 53.4 us  [exchange(): return lax.all_to_all(x, axes, 0, 0, tiled=True)]
  transfers between devices with their start and end apart: 4 -> 4, of which waited for: 2 -> 2; matrix products, arithmetic and copies ran while one was open for 1% -> 1% of each run, Pallas kernels for 6% -> 5%
where the time goes in v7:
time: 118 us
  blocking collectives  53.4 us (45%)
  starting transfers between devices  26.1 us (22%)
  waiting for transfers between devices  20.8 us (18%)
  Pallas kernels  6.74 us (6%)
  other arithmetic  4.87 us (4%)
  matrix products  2.65 us (2%)
  local copies, waits for them, and re-layouts  2.34 us (2%)
    all_to_all x2, blocking collectives, exchange(): return lax.all_to_all(x, axes, 0, 0, tiled=True)  53.4 us
    all_to_all x2, starting transfers between devices, exchange(): return lax.all_to_all(x, axes, 0, 0, tiled=True)  22.3 us
    all_to_all x2, waiting for transfers between devices, exchange(): return lax.all_to_all(x, axes, 0, 0, tiled=True)  20.8 us
    pallas_call x1, Pallas kernels, forward(): pl.pallas_call(forward_kernel, out_shape=(jax.ShapeDtypeStruct((tokens, h...  3.9 us
    ppermute x2, starting transfers between devices, partner(): return lax.ppermute(x, 'mp', [(0, 1), (1, 0)])  3.83 us
    dot_general x1, matrix products, body(): partial = jnp.dot(features, d_proj, preferred_element_type=jnp.float32)  2.65 us
  transfers between devices with their start and end apart: 4, of which 2 were waited for; matrix products, arithmetic and copies ran while one was open for 1% of the time, Pallas kernels for 5%

profile of v7, /device:TPU:8, one launch (start us, length us, event | category | flops | bytes accessed | tf_op | source)
XLA Modules:
  0.0 117.7 jit_solution(4501251561934146635)
XLA Ops:
  0.6 0.0 copy-start
  0.6 1.4 %constant_dynamic-slice_fusion = bf16[768,768]{1,0:T(8,128)(2,1)S(1)} fusion(bf16[768,1536]{1,0:T(8,128)(2,1)} %w_hbm.1, s32[]{:T(128)S(6)} %select_n.3), kind=kLoop, calls=%fused_computation.46 | loop fusion | bytes 2359300 | tf_op jit(solution)/shard_map/dynamic_slice | solution.py:277
  2.1 0.0 copy-start.1
  2.1 0.0 copy-start.2
  2.1 0.0 copy-start.3
  2.1 0.0 copy-start.4
  2.1 1.3 %pad_maximum_fusion.1 = bf16[1152,768]{1,0:T(8,128)(2,1)} fusion(bf16[384,768]{1,0:T(8,128)(2,1)S(1)} %copy-done, bf16[768,768]{1,0:T(8,128)(2,1)S(1)} %constant_dynamic-slice_fusion), kind=kLoop, calls=%fused_computation.3 | loop fusion | flops 3538944 | bytes 3538944 | tf_op jit(solution)/shard_map/concatenate | solution.py:278
  3.4 1.9 %collective-permute-start = (bf16[1152,768]{1,0:T(8,128)(2,1)}, bf16[1152,768]{1,0:T(8,128)(2,1)}, u32[]{:S(2)}, u32[]{:S(2)}) collective-permute-start(bf16[1152,768]{1,0:T(8,128)(2,1)} %pad_maximum_fusion.1), channel_id=1, source_target_pairs={{0,1},{1,0},{2,3},{3,2},{4,5},{5,4},{6,7},{7,6},{8,9},{9,8},{10,11... | collective-permute-start | bytes 5308424 | tf_op jit(solution)/shard_map/ppermute | solution.py:34
  5.4 1.3 %count.1 = f32[32,1,128]{2,1,0:T(1,128)} custom-call(s32[3]{0:T(128)} %bins.5), custom_call_target="tpu_custom_call" | custom-call | tf_op jit(solution)/shard_map/count/pallas_call | solution.py:77
  6.6 21.6 %all_to_all.20.got = f32[32,1,128]{2,1,0:T(1,128)S(1)} all-to-all(f32[32,1,128]{2,1,0:T(1,128)} %count.1), channel_id=1, replica_groups=mesh['dp_x'=4,'dp_yh'=4,'dp_yl'=2,'dp_zh'=6,'dp_zl'=2,'mp'=2] {'dp_x','d..., dimensions={0} | all-to-all | bytes 32768 | tf_op jit(solution)/shard_map/all_to_all | solution.py:38
  28.2 0.6 fold.1
  28.9 12.4 %all-to-all-start.1 = ((f32[12,1,128]{2,1,0:T(1,128)}), f32[12,1,128]{2,1,0:T(1,128)S(1)}, u32[]{:S(2)}, u32[]{:S(2)}) async-start(f32[12,1,128]{2,1,0:T(1,128)} %fold.1), calls=%async_computation.1 | async-start | bytes 12288 | tf_op jit(solution)/shard_map/all_to_all | solution.py:38
  41.2 0.0 collective-permute-done.other_hbm
  41.3 3.9 %forward.1 = (f32[384,768]{1,0:T(8,128)S(1)}, bf16[1536,384]{1,0:T(8,128)(2,1)}, f32[3,768]{1,0:T(4,128)S(1)}, f32[8,128]{1,0:T(8,128)S(1)}) custom-call(s32[1]{0:T(128)} %bitcast.me, s32[3]{0:T(128)S(1)} %copy-done.4, bf16[384,768]{1,0:T(8,128)(2,1)S(1)} %copy-done, bf16[1152,768]{1,0:T(8,128)(2,1)} %collective-permute-done.other_hbm, ...), custom_call_target="tpu_custom_call" | custom-call | flops 1000000000 | bytes 6000000 | tf_op jit(solution)/shard_map/forward/pallas_call | solution.py:202
  45.2 1.9 %collective-permute-start.1 = (f32[8,128]{1,0:T(8,128)S(1)}, f32[8,128]{1,0:T(8,128)S(1)}, u32[]{:S(2)}, u32[]{:S(2)}) collective-permute-start(f32[8,128]{1,0:T(8,128)S(1)} %get-tuple-element.12.marks), channel_id=1, source_target_pairs={{0,1},{1,0},{2,3},{3,2},{4,5},{5,4},{6,7},{7,6},{8,9},{9,8},{10,11... | collective-permute-start | bytes 12296 | tf_op jit(solution)/shard_map/ppermute | solution.py:34
  47.1 4.1 %all-to-all-done.1.got = f32[12,1,128]{2,1,0:T(1,128)S(1)} async-done(((f32[12,1,128]{2,1,0:T(1,128)}), f32[12,1,128]{2,1,0:T(1,128)S(1)}, u32[]{:S(2)}, u32[]{:S(2)}) %all-to-all-start.1) | async-done | bytes 6176 | tf_op jit(solution)/shard_map/all_to_all | solution.py:38
  51.3 0.0 collective-permute-done.1.other_marks
  51.3 0.9 scaled.1
  52.2 2.7 %convolution_convert_fusion = f16[1536,768]{1,0:T(8,128)(2,1)S(1)} fusion(bf16[1536,384]{1,0:T(8,128)(2,1)} %get-tuple-element.11, bf16[384,768]{1,0:T(8,128)(2,1)S(1)} %get-tuple-element.14), kind=kOutput, calls=%fused_computation.1 | convolution fusion | flops 907149312 | bytes 4128768 | tf_op jit(solution)/shard_map/dot_general | solution.py:286
  54.9 0.5 pad_maximum_fusion
  55.4 31.7 %all_to_all.21 = f16[16,8,9344]{2,1,0:T(8,128)(2,1)S(1)} all-to-all(f16[16,8,9344]{2,1,0:T(8,128)(2,1)S(1)} %pad_maximum_fusion), channel_id=1, replica_groups=mesh['dp_x'=4,'dp_yh'=4,'dp_yl'=2,'dp_zh'=6,'dp_zl'=2,'mp'=2] {'dp_x','d..., dimensions={0} | all-to-all | bytes 4784128 | tf_op jit(solution)/shard_map/all_to_all | solution.py:38
  87.3 0.2 fusion.12
  87.5 0.6 multiply_reduce_fusion
  88.1 0.2 reshape.86
  88.3 0.7 pad_maximum_fusion.2
  89.1 9.9 %all-to-all-start.3 = ((f16[24,32,128]{2,1,0:T(8,128)(2,1)}), f16[24,32,128]{2,1,0:T(8,128)(2,1)S(1)}, u32[]{:S(2)}, u32[]{:S(2)}) async-start(f16[24,32,128]{2,1,0:T(8,128)(2,1)} %pad_maximum_fusion.2), calls=%async_computation.3 | async-start | bytes 393216 | tf_op jit(solution)/shard_map/all_to_all | solution.py:38
  99.0 0.1 slice_reduce_fusion.1
  99.1 0.7 broadcast_multiply_fusion
  99.8 16.6 %all-to-all-done.3 = f16[24,32,128]{2,1,0:T(8,128)(2,1)S(1)} async-done(((f16[24,32,128]{2,1,0:T(8,128)(2,1)}), f16[24,32,128]{2,1,0:T(8,128)(2,1)S(1)}, u32[]{:S(2)}, u32[]{:S(2)}) %all-to-all-start.3) | async-done | bytes 196640 | tf_op jit(solution)/shard_map/all_to_all | solution.py:38
  116.4 0.1 copy_convert_fusion
  116.6 0.6 reshape.87
  117.2 0.5 bitcast_multiply_fusion.1
  (17 shorter events, 0.2 us)
Async XLA Ops:
  0.6 1.4 %copy-start = (bf16[384,768]{1,0:T(8,128)(2,1)S(1)}, bf16[384,768]{1,0:T(8,128)(2,1)}, u32[]{:S(2)}) copy-start(bf16[384,768]{1,0:T(8,128)(2,1)} %attn_hbm.1) | copy-start | bytes 1769476
  2.1 39.2 %copy-start.1 = (bf16[384,768]{1,0:T(8,128)(2,1)S(1)}, bf16[384,768]{1,0:T(8,128)(2,1)}, u32[]{:S(2)}) copy-start(bf16[384,768]{1,0:T(8,128)(2,1)} %resid_hbm.1) | copy-start | bytes 1769476
  2.1 39.2 %copy-start.2 = (bf16[384,768]{1,0:T(8,128)(2,1)S(1)}, bf16[384,768]{1,0:T(8,128)(2,1)}, u32[]{:S(2)}) copy-start(bf16[384,768]{1,0:T(8,128)(2,1)} %target_hbm.1) | copy-start | bytes 1769476
  2.1 39.2 %copy-start.3 = (f32[3,768]{1,0:T(4,128)S(1)}, f32[3,768]{1,0:T(4,128)}, u32[]{:S(2)}) copy-start(f32[3,768]{1,0:T(4,128)} %gate.3) | copy-start | bytes 27652
  2.1 39.2 %copy-start.4 = (s32[3]{0:T(128)S(1)}, s32[3]{0:T(128)}, u32[]{:S(2)}) copy-start(s32[3]{0:T(128)} %bins.5) | copy-start | bytes 40
  3.4 37.8 %collective-permute-start = (bf16[1152,768]{1,0:T(8,128)(2,1)}, bf16[1152,768]{1,0:T(8,128)(2,1)}, u32[]{:S(2)}, u32[]{:S(2)}) collective-permute-start(bf16[1152,768]{1,0:T(8,128)(2,1)} %pad_maximum_fusion.1), channel_id=1, source_target_pairs={{0,1},{1,0},{2,3},{3,2},{4,5},{5,4},{6,7},{7,6},{8,9},{9,8},{10,11... | collective-permute-start | bytes 5308424 | tf_op jit(solution)/shard_map/ppermute | solution.py:34
  28.9 22.4 %all-to-all-start.1 = ((f32[12,1,128]{2,1,0:T(1,128)}), f32[12,1,128]{2,1,0:T(1,128)S(1)}, u32[]{:S(2)}, u32[]{:S(2)}) async-start(f32[12,1,128]{2,1,0:T(1,128)} %fold.1), calls=%async_computation.1 | async-start | bytes 12288 | tf_op jit(solution)/shard_map/all_to_all | solution.py:38
  45.2 6.1 %collective-permute-start.1 = (f32[8,128]{1,0:T(8,128)S(1)}, f32[8,128]{1,0:T(8,128)S(1)}, u32[]{:S(2)}, u32[]{:S(2)}) collective-permute-start(f32[8,128]{1,0:T(8,128)S(1)} %get-tuple-element.12.marks), channel_id=1, source_target_pairs={{0,1},{1,0},{2,3},{3,2},{4,5},{5,4},{6,7},{7,6},{8,9},{9,8},{10,11... | collective-permute-start | bytes 12296 | tf_op jit(solution)/shard_map/ppermute | solution.py:34
  89.1 27.4 %all-to-all-start.3 = ((f16[24,32,128]{2,1,0:T(8,128)(2,1)}), f16[24,32,128]{2,1,0:T(8,128)(2,1)S(1)}, u32[]{:S(2)}, u32[]{:S(2)}) async-start(f16[24,32,128]{2,1,0:T(8,128)(2,1)} %pad_maximum_fusion.2), calls=%async_computation.3 | async-start | bytes 393216 | tf_op jit(solution)/shard_map/all_to_all | solution.py:38

commit v8 on v7

--- a/solution.py
+++ b/solution.py
@@ -113,6 +113,41 @@
     z_high = quad - 6 * y_high
     source = y_high * 96 + (piece >> 1) * 48 + z_high * 8 + (piece & 1) * 4 + (inner & 3)
     return (source == lax.broadcasted_iota(jnp.int32, (run, run), 1)).astype(jnp.bfloat16)
+
+
+def pack_kernel(me, w_hbm, attn_hbm, send):
+    half = attn_hbm.shape[1]
+    theirs = pl.multiple_of((1 - me[0]) * half, half)
+    parts = 4
+
+    def body(sems):
+        copies = []
+        for src, top in ((w_hbm.at[:, pl.ds(theirs, half)], 0), (attn_hbm, half)):
+            step = src.shape[0] // parts
+            for n in range(parts):
+                rows = pl.ds(n * step, step)
+                copies.append(
+                    pltpu.make_async_copy(
+                        src.at[rows, :], send.at[pl.ds(top + n * step, step), :], sems.at[len(copies)]
+                    )
+                )
+                copies[-1].start()
+        for copy in copies:
+            copy.wait()
+
+    pl.run_scoped(body, pltpu.SemaphoreType.DMA((2 * parts,)))
+
+
+def packed(me, w_out, attn):
+    tokens, half = attn.shape
+    return pl.pallas_call(
+        pack_kernel,
+        out_shape=jax.ShapeDtypeStruct((half + tokens, half), attn.dtype),
+        in_specs=[SMEM, HBM, HBM],
+        out_specs=HBM,
+        cost_estimate=pl.CostEstimate(flops=10**7, bytes_accessed=4 * 10**6, transcendentals=0),
+        name="packed",
+    )(me, w_out, attn)
 
 
 def forward_kernel(
@@ -274,8 +309,7 @@
     own_cols = resid.shape[1]
     me = lax.axis_index("mp")
     got = count_sweep(bins)
-    w_theirs = lax.dynamic_slice_in_dim(w_out, (1 - me) * own_cols, own_cols, axis=1)
-    other = partner(jnp.concatenate([w_theirs, attn], axis=0))
+    other = partner(packed(me.reshape(1), w_out, attn))
     error, features, error_proj, marks = forward(
         me.reshape(1), bins, attn, other, w_out, resid, target, gate
     )
@@ -299,18 +333,16 @@
     high, low = halves(
         jnp.sum((sides[:, 0] + sides[:, 1] * (1.0 / LOW)) * jnp.exp2(sides[:, 3] - loss_exp), axis=0)
     )
-    side = jnp.stack([high, low, grad_exp, loss_exp])
-    side = jnp.pad(side, ((0, SIDE - 4), (0, 0))).astype(jnp.float16)
+    side = jnp.stack([high, low, grad_exp, loss_exp]).astype(jnp.float16)
     rows = total.astype(jnp.float16).reshape(SIDE, stripes, own_cols).transpose(1, 0, 2)
-    rows = rows.reshape(far, -1, NBINS)
-    keep = rows.shape[1]
-    rows = jnp.concatenate([rows, jnp.broadcast_to(side[None], (far, *side.shape))], axis=1)
+    rows = rows.reshape(far, -1, own_cols)
+    rows = jnp.concatenate([rows, jnp.broadcast_to(side[None], (far, *side.shape))], axis=2)
     got = exchange(rows, FAR).astype(jnp.float32)
 
-    sides = got[:, keep : keep + 4]
-    total = jnp.sum(got[:, :keep] * jnp.exp2(sides[:, 2:3] - TOP), axis=0)
+    sides = got[:, :, own_cols:]
+    total = jnp.sum(got[:, :, :own_cols] * jnp.exp2(sides[:, 2:3, :1] - TOP), axis=0)
     losses = jnp.sum((sides[:, 0] + sides[:, 1] * (1.0 / LOW)) * jnp.exp2(sides[:, 3] - TOP), axis=0)
-    return (total.reshape(-1, own_cols), steepness[:, :1] * error_proj, per_count[0] * losses)
+    return (total, steepness[:, :1] * error_proj, per_count[0] * losses)
 
 
 def solution(mesh):

time: 118 us -> 169 us (1.43)
  Pallas kernels: 6.74 us -> 61.5 us
  local copies, waits for them, and re-layouts: 2.34 us -> 0.21 us
    pallas_call x0 -> x1, Pallas kernels: none -> 54.7 us  [packed(): pl.pallas_call(pack_kernel, out_shape=jax.ShapeDtypeStruct((half + tokens...]
  transfers between devices with their start and end apart: 4 -> 4, of which waited for: 2 -> 2; matrix products, arithmetic and copies ran while one was open for 1% -> 0% of each run, Pallas kernels for 5% -> 3%
where the time goes in v8:
time: 169 us
  Pallas kernels  61.5 us (36%)
  blocking collectives  53.4 us (32%)
  starting transfers between devices  26.1 us (15%)
  waiting for transfers between devices  20 us (12%)
  other arithmetic  4.37 us (3%)
  matrix products  2.66 us (2%)
    pallas_call x1, Pallas kernels, packed(): pl.pallas_call(pack_kernel, out_shape=jax.ShapeDtypeStruct((half + tokens...  54.7 us
    all_to_all x2, blocking collectives, exchange(): return lax.all_to_all(x, axes, 0, 0, tiled=True)  53.4 us
    all_to_all x2, starting transfers between devices, exchange(): return lax.all_to_all(x, axes, 0, 0, tiled=True)  22.3 us
    all_to_all x2, waiting for transfers between devices, exchange(): return lax.all_to_all(x, axes, 0, 0, tiled=True)  20 us
    pallas_call x1, Pallas kernels, forward(): pl.pallas_call(forward_kernel, out_shape=(jax.ShapeDtypeStruct((tokens, h...  3.9 us
    ppermute x2, starting transfers between devices, partner(): return lax.ppermute(x, 'mp', [(0, 1), (1, 0)])  3.83 us
  transfers between devices with their start and end apart: 4, of which 2 were waited for; matrix products, arithmetic and copies ran while one was open for 0% of the time, Pallas kernels for 3%

profile of v8, /device:TPU:8, one launch (start us, length us, event | category | flops | bytes accessed | tf_op | source)
XLA Modules:
  0.0 169.0 jit_solution(3422487136215940295)
XLA Ops:
  0.6 0.0 copy-start
  0.6 0.0 copy-start.1
  0.7 0.0 copy-start.2
  0.7 0.0 copy-start.3
  0.7 0.0 copy-start.4
  0.7 54.7 %packed.1 = bf16[1152,768]{1,0:T(8,128)(2,1)} custom-call(s32[1]{0:T(128)} %bitcast.me, bf16[768,1536]{1,0:T(8,128)(2,1)} %w_hbm.3, bf16[384,768]{1,0:T(8,128)(2,1)} %attn_hbm.3), custom_call_target="tpu_custom_call" | custom-call | flops 10000000 | bytes 4000000 | tf_op jit(solution)/shard_map/packed/pallas_call | solution.py:143
  55.4 1.9 %collective-permute-start = (bf16[1152,768]{1,0:T(8,128)(2,1)}, bf16[1152,768]{1,0:T(8,128)(2,1)}, u32[]{:S(2)}, u32[]{:S(2)}) collective-permute-start(bf16[1152,768]{1,0:T(8,128)(2,1)} %packed.1), channel_id=1, source_target_pairs={{0,1},{1,0},{2,3},{3,2},{4,5},{5,4},{6,7},{7,6},{8,9},{9,8},{10,11... | collective-permute-start | bytes 5308424 | tf_op jit(solution)/shard_map/ppermute | solution.py:34
  57.3 1.3 count.1
  58.6 21.6 %all_to_all.20.got = f32[32,1,128]{2,1,0:T(1,128)S(1)} all-to-all(f32[32,1,128]{2,1,0:T(1,128)} %count.1), channel_id=1, replica_groups=mesh['dp_x'=4,'dp_yh'=4,'dp_yl'=2,'dp_zh'=6,'dp_zl'=2,'mp'=2] {'dp_x','d..., dimensions={0} | all-to-all | bytes 32768 | tf_op jit(solution)/shard_map/all_to_all | solution.py:38
  80.2 0.6 fold.1
  80.8 12.4 %all-to-all-start.1 = ((f32[12,1,128]{2,1,0:T(1,128)}), f32[12,1,128]{2,1,0:T(1,128)S(1)}, u32[]{:S(2)}, u32[]{:S(2)}) async-start(f32[12,1,128]{2,1,0:T(1,128)} %fold.1), calls=%async_computation.1 | async-start | bytes 12288 | tf_op jit(solution)/shard_map/all_to_all | solution.py:38
  93.2 0.0 collective-permute-done.other_hbm
  93.2 0.0 copy-done
  93.3 3.9 %forward.1 = (f32[384,768]{1,0:T(8,128)S(1)}, bf16[1536,384]{1,0:T(8,128)(2,1)}, f32[3,768]{1,0:T(4,128)S(1)}, f32[8,128]{1,0:T(8,128)S(1)}) custom-call(s32[1]{0:T(128)} %bitcast.me, s32[3]{0:T(128)S(1)} %copy-done.4, bf16[384,768]{1,0:T(8,128)(2,1)S(1)} %copy-done, bf16[1152,768]{1,0:T(8,128)(2,1)} %collective-permute-done.other_hbm, ...), custom_call_target="tpu_custom_call" | custom-call | flops 1000000000 | bytes 6000000 | tf_op jit(solution)/shard_map/forward/pallas_call | solution.py:237
  97.2 1.9 %collective-permute-start.1 = (f32[8,128]{1,0:T(8,128)S(1)}, f32[8,128]{1,0:T(8,128)S(1)}, u32[]{:S(2)}, u32[]{:S(2)}) collective-permute-start(f32[8,128]{1,0:T(8,128)S(1)} %get-tuple-element.12.marks), channel_id=1, source_target_pairs={{0,1},{1,0},{2,3},{3,2},{4,5},{5,4},{6,7},{7,6},{8,9},{9,8},{10,11... | collective-permute-start | bytes 12296 | tf_op jit(solution)/shard_map/ppermute | solution.py:34
  99.1 4.1 %all-to-all-done.1.got = f32[12,1,128]{2,1,0:T(1,128)S(1)} async-done(((f32[12,1,128]{2,1,0:T(1,128)}), f32[12,1,128]{2,1,0:T(1,128)S(1)}, u32[]{:S(2)}, u32[]{:S(2)}) %all-to-all-start.1) | async-done | bytes 6176 | tf_op jit(solution)/shard_map/all_to_all | solution.py:38
  103.2 0.0 collective-permute-done.1.other_marks
  103.2 0.9 scaled.1
  104.2 2.7 %convolution_convert_fusion = f16[1536,768]{1,0:T(8,128)(2,1)S(1)} fusion(bf16[1536,384]{1,0:T(8,128)(2,1)} %get-tuple-element.11, bf16[384,768]{1,0:T(8,128)(2,1)S(1)} %get-tuple-element.14), kind=kOutput, calls=%fused_computation.1 | convolution fusion | flops 907149312 | bytes 4128768 | tf_op jit(solution)/shard_map/dot_general | solution.py:320
  106.9 0.5 pad_maximum_fusion
  107.4 31.8 %all_to_all.21 = f16[16,8,9344]{2,1,0:T(8,128)(2,1)S(1)} all-to-all(f16[16,8,9344]{2,1,0:T(8,128)(2,1)S(1)} %pad_maximum_fusion), channel_id=1, replica_groups=mesh['dp_x'=4,'dp_yh'=4,'dp_yl'=2,'dp_zh'=6,'dp_zl'=2,'mp'=2] {'dp_x','d..., dimensions={0} | all-to-all | bytes 4784128 | tf_op jit(solution)/shard_map/all_to_all | solution.py:38
  139.2 0.2 fusion.12
  139.5 0.6 multiply_reduce_fusion
  140.1 0.1 reshape.112
  140.2 0.8 pad_maximum_fusion.1
  141.0 9.9 %all-to-all-start.3 = ((f16[24,4,896]{2,1,0:T(4,128)(2,1)}), f16[24,4,896]{2,1,0:T(4,128)(2,1)S(1)}, u32[]{:S(2)}, u32[]{:S(2)}) async-start(f16[24,4,896]{2,1,0:T(4,128)(2,1)} %pad_maximum_fusion.1), calls=%async_computation.3 | async-start | bytes 344064 | tf_op jit(solution)/shard_map/all_to_all | solution.py:38
  150.9 0.1 slice_reduce_fusion.1
  151.1 0.7 broadcast_multiply_fusion
  151.7 15.9 %all-to-all-done.3 = f16[24,4,896]{2,1,0:T(4,128)(2,1)S(1)} async-done(((f16[24,4,896]{2,1,0:T(4,128)(2,1)}), f16[24,4,896]{2,1,0:T(4,128)(2,1)S(1)}, u32[]{:S(2)}, u32[]{:S(2)}) %all-to-all-start.3) | async-done | bytes 172064 | tf_op jit(solution)/shard_map/all_to_all | solution.py:38
  167.7 0.1 fusion.8
  167.8 0.7 fusion
  168.5 0.5 bitcast_multiply_fusion.1
  (16 shorter events, 0.2 us)
Async XLA Ops:
  0.6 92.6 %copy-start = (bf16[384,768]{1,0:T(8,128)(2,1)S(1)}, bf16[384,768]{1,0:T(8,128)(2,1)}, u32[]{:S(2)}) copy-start(bf16[384,768]{1,0:T(8,128)(2,1)} %attn_hbm.3) | copy-start | bytes 1769476
  0.6 92.6 %copy-start.1 = (bf16[384,768]{1,0:T(8,128)(2,1)S(1)}, bf16[384,768]{1,0:T(8,128)(2,1)}, u32[]{:S(2)}) copy-start(bf16[384,768]{1,0:T(8,128)(2,1)} %resid_hbm.1) | copy-start | bytes 1769476
  0.7 92.6 %copy-start.2 = (bf16[384,768]{1,0:T(8,128)(2,1)S(1)}, bf16[384,768]{1,0:T(8,128)(2,1)}, u32[]{:S(2)}) copy-start(bf16[384,768]{1,0:T(8,128)(2,1)} %target_hbm.1) | copy-start | bytes 1769476
  0.7 92.6 %copy-start.3 = (f32[3,768]{1,0:T(4,128)S(1)}, f32[3,768]{1,0:T(4,128)}, u32[]{:S(2)}) copy-start(f32[3,768]{1,0:T(4,128)} %gate.3) | copy-start | bytes 27652
  0.7 92.6 %copy-start.4 = (s32[3]{0:T(128)S(1)}, s32[3]{0:T(128)}, u32[]{:S(2)}) copy-start(s32[3]{0:T(128)} %bins.5) | copy-start | bytes 40
  55.4 37.8 %collective-permute-start = (bf16[1152,768]{1,0:T(8,128)(2,1)}, bf16[1152,768]{1,0:T(8,128)(2,1)}, u32[]{:S(2)}, u32[]{:S(2)}) collective-permute-start(bf16[1152,768]{1,0:T(8,128)(2,1)} %packed.1), channel_id=1, source_target_pairs={{0,1},{1,0},{2,3},{3,2},{4,5},{5,4},{6,7},{7,6},{8,9},{9,8},{10,11... | collective-permute-start | bytes 5308424 | tf_op jit(solution)/shard_map/ppermute | solution.py:34
  80.8 22.4 %all-to-all-start.1 = ((f32[12,1,128]{2,1,0:T(1,128)}), f32[12,1,128]{2,1,0:T(1,128)S(1)}, u32[]{:S(2)}, u32[]{:S(2)}) async-start(f32[12,1,128]{2,1,0:T(1,128)} %fold.1), calls=%async_computation.1 | async-start | bytes 12288 | tf_op jit(solution)/shard_map/all_to_all | solution.py:38
  97.2 6.1 %collective-permute-start.1 = (f32[8,128]{1,0:T(8,128)S(1)}, f32[8,128]{1,0:T(8,128)S(1)}, u32[]{:S(2)}, u32[]{:S(2)}) collective-permute-start(f32[8,128]{1,0:T(8,128)S(1)} %get-tuple-element.12.marks), channel_id=1, source_target_pairs={{0,1},{1,0},{2,3},{3,2},{4,5},{5,4},{6,7},{7,6},{8,9},{9,8},{10,11... | collective-permute-start | bytes 12296 | tf_op jit(solution)/shard_map/ppermute | solution.py:34
  141.0 26.6 %all-to-all-start.3 = ((f16[24,4,896]{2,1,0:T(4,128)(2,1)}), f16[24,4,896]{2,1,0:T(4,128)(2,1)S(1)}, u32[]{:S(2)}, u32[]{:S(2)}) async-start(f16[24,4,896]{2,1,0:T(4,128)(2,1)} %pad_maximum_fusion.1), calls=%async_computation.3 | async-start | bytes 344064 | tf_op jit(solution)/shard_map/all_to_all | solution.py:38

commit v9 on v7

--- a/solution.py
+++ b/solution.py
@@ -73,7 +73,7 @@
 
 
 def count_sweep(bins):
-    plane, column = (X, YH, YL), (ZH, ZL)
+    plane, column = (ZH, ZL), (X, YH, YL)
     spread = pl.pallas_call(
         count_kernel,
         out_shape=jax.ShapeDtypeStruct((group(plane), 1, NBINS), jnp.float32),
@@ -299,18 +299,16 @@
     high, low = halves(
         jnp.sum((sides[:, 0] + sides[:, 1] * (1.0 / LOW)) * jnp.exp2(sides[:, 3] - loss_exp), axis=0)
     )
-    side = jnp.stack([high, low, grad_exp, loss_exp])
-    side = jnp.pad(side, ((0, SIDE - 4), (0, 0))).astype(jnp.float16)
+    side = jnp.stack([high, low, grad_exp, loss_exp]).astype(jnp.float16)
     rows = total.astype(jnp.float16).reshape(SIDE, stripes, own_cols).transpose(1, 0, 2)
-    rows = rows.reshape(far, -1, NBINS)
-    keep = rows.shape[1]
-    rows = jnp.concatenate([rows, jnp.broadcast_to(side[None], (far, *side.shape))], axis=1)
+    rows = rows.reshape(far, -1, own_cols)
+    rows = jnp.concatenate([rows, jnp.broadcast_to(side[None], (far, *side.shape))], axis=2)
     got = exchange(rows, FAR).astype(jnp.float32)
 
-    sides = got[:, keep : keep + 4]
-    total = jnp.sum(got[:, :keep] * jnp.exp2(sides[:, 2:3] - TOP), axis=0)
+    sides = got[:, :, own_cols:]
+    total = jnp.sum(got[:, :, :own_cols] * jnp.exp2(sides[:, 2:3, :1] - TOP), axis=0)
     losses = jnp.sum((sides[:, 0] + sides[:, 1] * (1.0 / LOW)) * jnp.exp2(sides[:, 3] - TOP), axis=0)
-    return (total.reshape(-1, own_cols), steepness[:, :1] * error_proj, per_count[0] * losses)
+    return (total, steepness[:, :1] * error_proj, per_count[0] * losses)
 
 
 def solution(mesh):

time: 118 us -> 117 us (level)
  blocking collectives: 53.4 us -> 58.6 us
  starting transfers between devices: 26.1 us -> 21.5 us
  waiting for transfers between devices: 20.8 us -> 18.9 us
    all_to_all x2, blocking collectives: 53.4 us -> 58.6 us  [exchange(): return lax.all_to_all(x, axes, 0, 0, tiled=True)]
    all_to_all x2, starting transfers between devices: 22.3 us -> 17.7 us  [exchange(): return lax.all_to_all(x, axes, 0, 0, tiled=True)]
    all_to_all x2, waiting for transfers between devices: 20.8 us -> 18.9 us  [exchange(): return lax.all_to_all(x, axes, 0, 0, tiled=True)]
where the time goes in v9:
time: 117 us
  blocking collectives  58.6 us (50%)
  starting transfers between devices  21.5 us (18%)
  waiting for transfers between devices  18.9 us (16%)
  Pallas kernels  6.74 us (6%)
  other arithmetic  5.68 us (5%)
  matrix products  2.65 us (2%)
  local copies, waits for them, and re-layouts  1.63 us (1%)
    all_to_all x2, blocking collectives, exchange(): return lax.all_to_all(x, axes, 0, 0, tiled=True)  58.6 us
    all_to_all x2, waiting for transfers between devices, exchange(): return lax.all_to_all(x, axes, 0, 0, tiled=True)  18.9 us
    all_to_all x2, starting transfers between devices, exchange(): return lax.all_to_all(x, axes, 0, 0, tiled=True)  17.7 us
    pallas_call x1, Pallas kernels, forward(): pl.pallas_call(forward_kernel, out_shape=(jax.ShapeDtypeStruct((tokens, h...  3.9 us
    ppermute x2, starting transfers between devices, partner(): return lax.ppermute(x, 'mp', [(0, 1), (1, 0)])  3.83 us
    dot_general x1, matrix products, body(): partial = jnp.dot(features, d_proj, preferred_element_type=jnp.float32)  2.65 us
  transfers between devices with their start and end apart: 4, of which 2 were waited for; matrix products, arithmetic and copies ran while one was open for 1% of the time, Pallas kernels for 5%

profile of v9, /device:TPU:8, one launch (start us, length us, event | category | flops | bytes accessed | tf_op | source)
XLA Modules:
  0.0 116.5 jit_solution(8668959164407507055)
XLA Ops:
  0.6 0.0 copy-start
  0.6 1.4 %constant_dynamic-slice_fusion = bf16[768,768]{1,0:T(8,128)(2,1)S(1)} fusion(bf16[768,1536]{1,0:T(8,128)(2,1)} %w_hbm.1, s32[]{:T(128)S(6)} %select_n.3), kind=kLoop, calls=%fused_computation.39 | loop fusion | bytes 2359300 | tf_op jit(solution)/shard_map/dynamic_slice | solution.py:277
  2.1 0.0 copy-start.1
  2.1 0.0 copy-start.2
  2.1 0.0 copy-start.3
  2.1 0.0 copy-start.4
  2.1 1.3 %pad_maximum_fusion.1 = bf16[1152,768]{1,0:T(8,128)(2,1)} fusion(bf16[384,768]{1,0:T(8,128)(2,1)S(1)} %copy-done, bf16[768,768]{1,0:T(8,128)(2,1)S(1)} %constant_dynamic-slice_fusion), kind=kLoop, calls=%fused_computation.3 | loop fusion | flops 3538944 | bytes 3538944 | tf_op jit(solution)/shard_map/concatenate | solution.py:278
  3.4 1.9 %collective-permute-start = (bf16[1152,768]{1,0:T(8,128)(2,1)}, bf16[1152,768]{1,0:T(8,128)(2,1)}, u32[]{:S(2)}, u32[]{:S(2)}) collective-permute-start(bf16[1152,768]{1,0:T(8,128)(2,1)} %pad_maximum_fusion.1), channel_id=1, source_target_pairs={{0,1},{1,0},{2,3},{3,2},{4,5},{5,4},{6,7},{7,6},{8,9},{9,8},{10,11... | collective-permute-start | bytes 5308424 | tf_op jit(solution)/shard_map/ppermute | solution.py:34
  5.4 1.3 %count.1 = f32[12,1,128]{2,1,0:T(1,128)} custom-call(s32[3]{0:T(128)} %bins.5), custom_call_target="tpu_custom_call" | custom-call | tf_op jit(solution)/shard_map/count/pallas_call | solution.py:77
  6.6 25.2 %all_to_all.20.got = f32[12,1,128]{2,1,0:T(1,128)S(1)} all-to-all(f32[12,1,128]{2,1,0:T(1,128)} %count.1), channel_id=1, replica_groups=mesh['dp_x'=4,'dp_yh'=4,'dp_yl'=2,'dp_zh'=6,'dp_zl'=2,'mp'=2] {'dp_zh','..., dimensions={0} | all-to-all | bytes 12288 | tf_op jit(solution)/shard_map/all_to_all | solution.py:38
  31.8 0.6 fold.1
  32.4 10.2 %all-to-all-start.1 = ((f32[32,1,128]{2,1,0:T(1,128)}), f32[32,1,128]{2,1,0:T(1,128)S(1)}, u32[]{:S(2)}, u32[]{:S(2)}) async-start(f32[32,1,128]{2,1,0:T(1,128)} %fold.1), calls=%async_computation.1 | async-start | bytes 32768 | tf_op jit(solution)/shard_map/all_to_all | solution.py:38
  42.6 0.0 collective-permute-done.other_hbm
  42.6 3.9 %forward.1 = (f32[384,768]{1,0:T(8,128)S(1)}, bf16[1536,384]{1,0:T(8,128)(2,1)}, f32[3,768]{1,0:T(4,128)S(1)}, f32[8,128]{1,0:T(8,128)S(1)}) custom-call(s32[1]{0:T(128)} %bitcast.me, s32[3]{0:T(128)S(1)} %copy-done.4, bf16[384,768]{1,0:T(8,128)(2,1)S(1)} %copy-done, bf16[1152,768]{1,0:T(8,128)(2,1)} %collective-permute-done.other_hbm, ...), custom_call_target="tpu_custom_call" | custom-call | flops 1000000000 | bytes 6000000 | tf_op jit(solution)/shard_map/forward/pallas_call | solution.py:202
  46.5 1.9 %collective-permute-start.1 = (f32[8,128]{1,0:T(8,128)S(1)}, f32[8,128]{1,0:T(8,128)S(1)}, u32[]{:S(2)}, u32[]{:S(2)}) collective-permute-start(f32[8,128]{1,0:T(8,128)S(1)} %get-tuple-element.12.marks), channel_id=1, source_target_pairs={{0,1},{1,0},{2,3},{3,2},{4,5},{5,4},{6,7},{7,6},{8,9},{9,8},{10,11... | collective-permute-start | bytes 12296 | tf_op jit(solution)/shard_map/ppermute | solution.py:34
  48.5 2.8 %all-to-all-done.1.got = f32[32,1,128]{2,1,0:T(1,128)S(1)} async-done(((f32[32,1,128]{2,1,0:T(1,128)}), f32[32,1,128]{2,1,0:T(1,128)S(1)}, u32[]{:S(2)}, u32[]{:S(2)}) %all-to-all-start.1) | async-done | bytes 16416 | tf_op jit(solution)/shard_map/all_to_all | solution.py:38
  51.2 0.0 collective-permute-done.1.other_marks
  51.2 1.0 scaled.1
  52.2 2.7 %convolution_convert_fusion = f16[1536,768]{1,0:T(8,128)(2,1)S(1)} fusion(bf16[1536,384]{1,0:T(8,128)(2,1)} %get-tuple-element.11, bf16[384,768]{1,0:T(8,128)(2,1)S(1)} %get-tuple-element.14), kind=kOutput, calls=%fused_computation.1 | convolution fusion | flops 907149312 | bytes 4128768 | tf_op jit(solution)/shard_map/dot_general | solution.py:286
  54.9 0.5 pad_maximum_fusion
  55.4 33.5 %all_to_all.21 = f16[16,8,9344]{2,1,0:T(8,128)(2,1)S(1)} all-to-all(f16[16,8,9344]{2,1,0:T(8,128)(2,1)S(1)} %pad_maximum_fusion), channel_id=1, replica_groups=mesh['dp_x'=4,'dp_yh'=4,'dp_yl'=2,'dp_zh'=6,'dp_zl'=2,'mp'=2] {'dp_x','d..., dimensions={0} | all-to-all | bytes 4784128 | tf_op jit(solution)/shard_map/all_to_all | solution.py:38
  89.0 0.2 fusion.12
  89.2 0.6 multiply_reduce_fusion
  89.8 0.1 reshape.111
  89.9 0.8 pad_maximum_fusion.2
  90.7 7.5 %all-to-all-start.3 = ((f16[24,4,896]{2,1,0:T(4,128)(2,1)}), f16[24,4,896]{2,1,0:T(4,128)(2,1)S(1)}, u32[]{:S(2)}, u32[]{:S(2)}) async-start(f16[24,4,896]{2,1,0:T(4,128)(2,1)} %pad_maximum_fusion.2), calls=%async_computation.3 | async-start | bytes 344064 | tf_op jit(solution)/shard_map/all_to_all | solution.py:38
  98.2 0.1 slice_reduce_fusion.1
  98.3 0.7 broadcast_multiply_fusion
  99.0 16.1 %all-to-all-done.3 = f16[24,4,896]{2,1,0:T(4,128)(2,1)S(1)} async-done(((f16[24,4,896]{2,1,0:T(4,128)(2,1)}), f16[24,4,896]{2,1,0:T(4,128)(2,1)S(1)}, u32[]{:S(2)}, u32[]{:S(2)}) %all-to-all-start.3) | async-done | bytes 172064 | tf_op jit(solution)/shard_map/all_to_all | solution.py:38
  115.2 0.1 fusion.8
  115.3 0.7 fusion
  116.0 0.5 bitcast_multiply_fusion.1
  (17 shorter events, 0.2 us)
Async XLA Ops:
  0.6 1.4 %copy-start = (bf16[384,768]{1,0:T(8,128)(2,1)S(1)}, bf16[384,768]{1,0:T(8,128)(2,1)}, u32[]{:S(2)}) copy-start(bf16[384,768]{1,0:T(8,128)(2,1)} %attn_hbm.1) | copy-start | bytes 1769476
  2.1 40.5 %copy-start.1 = (bf16[384,768]{1,0:T(8,128)(2,1)S(1)}, bf16[384,768]{1,0:T(8,128)(2,1)}, u32[]{:S(2)}) copy-start(bf16[384,768]{1,0:T(8,128)(2,1)} %resid_hbm.1) | copy-start | bytes 1769476
  2.1 40.5 %copy-start.2 = (bf16[384,768]{1,0:T(8,128)(2,1)S(1)}, bf16[384,768]{1,0:T(8,128)(2,1)}, u32[]{:S(2)}) copy-start(bf16[384,768]{1,0:T(8,128)(2,1)} %target_hbm.1) | copy-start | bytes 1769476
  2.1 40.5 %copy-start.3 = (f32[3,768]{1,0:T(4,128)S(1)}, f32[3,768]{1,0:T(4,128)}, u32[]{:S(2)}) copy-start(f32[3,768]{1,0:T(4,128)} %gate.3) | copy-start | bytes 27652
  2.1 40.5 %copy-start.4 = (s32[3]{0:T(128)S(1)}, s32[3]{0:T(128)}, u32[]{:S(2)}) copy-start(s32[3]{0:T(128)} %bins.5) | copy-start | bytes 40
  3.4 39.2 %collective-permute-start = (bf16[1152,768]{1,0:T(8,128)(2,1)}, bf16[1152,768]{1,0:T(8,128)(2,1)}, u32[]{:S(2)}, u32[]{:S(2)}) collective-permute-start(bf16[1152,768]{1,0:T(8,128)(2,1)} %pad_maximum_fusion.1), channel_id=1, source_target_pairs={{0,1},{1,0},{2,3},{3,2},{4,5},{5,4},{6,7},{7,6},{8,9},{9,8},{10,11... | collective-permute-start | bytes 5308424 | tf_op jit(solution)/shard_map/ppermute | solution.py:34
  32.4 18.8 %all-to-all-start.1 = ((f32[32,1,128]{2,1,0:T(1,128)}), f32[32,1,128]{2,1,0:T(1,128)S(1)}, u32[]{:S(2)}, u32[]{:S(2)}) async-start(f32[32,1,128]{2,1,0:T(1,128)} %fold.1), calls=%async_computation.1 | async-start | bytes 32768 | tf_op jit(solution)/shard_map/all_to_all | solution.py:38
  46.5 4.7 %collective-permute-start.1 = (f32[8,128]{1,0:T(8,128)S(1)}, f32[8,128]{1,0:T(8,128)S(1)}, u32[]{:S(2)}, u32[]{:S(2)}) collective-permute-start(f32[8,128]{1,0:T(8,128)S(1)} %get-tuple-element.12.marks), channel_id=1, source_target_pairs={{0,1},{1,0},{2,3},{3,2},{4,5},{5,4},{6,7},{7,6},{8,9},{9,8},{10,11... | collective-permute-start | bytes 12296 | tf_op jit(solution)/shard_map/ppermute | solution.py:34
  90.7 24.4 %all-to-all-start.3 = ((f16[24,4,896]{2,1,0:T(4,128)(2,1)}), f16[24,4,896]{2,1,0:T(4,128)(2,1)S(1)}, u32[]{:S(2)}, u32[]{:S(2)}) async-start(f16[24,4,896]{2,1,0:T(4,128)(2,1)} %pad_maximum_fusion.2), calls=%async_computation.3 | async-start | bytes 344064 | tf_op jit(solution)/shard_map/all_to_all | solution.py:38
